TPU v7x, 32 devices: a whole 2x2x4 slice. The times are simulated.
32 devices in a mesh: shard: 2 (over y), context: 4 (over x, core), tensor: 4 (over z).
Axes of the slice: x: 2, y: 2, z: 4, core: 2. Of those that a mesh axis runs over, the one named last changes fastest.
Arguments:
- inputs: bfloat16 [8, 1024, 2048], P('shard', 'context', 'tensor')
- cotangent: bfloat16 [8, 1024, 2048], P('shard', 'context', 'tensor'), may hold values from -8 to 8
- doc_lengths: int32 [8, 8], P('shard'), may hold values from 1 to 512, 1024 in all within a row
- attn_weights: float32 [4, 2048, 2048], P(None, ('shard', 'context'), 'tensor')
- mlp_weights: float32 [2, 2048, 8192], P(None, ('shard', 'context'), 'tensor'), may hold values from -0.09375 to 0.09375
- vectors: float32 [7, 2048], P(None, 'tensor')
- hidden_bias: float32 [8192], P('tensor'), may hold values from -1.5 to 1.5
- attn_moment: float32 [4, 2048, 2048], P(None, ('shard', 'context'), 'tensor'), may hold values from -5 to 5
- mlp_moment: float32 [2, 2048, 8192], P(None, ('shard', 'context'), 'tensor'), may hold values from -10 to 10
- vector_moment: float32 [7, 2048], P(None, 'tensor'), may hold values from -56 to 56
- hidden_moment: float32 [8192], P('tensor'), may hold values from -16 to 16
- attn_second: float32 [4, 2048, 2048], P(None, ('shard', 'context'), 'tensor'), may hold values from 0.8192 to 8.192
- mlp_second: float32 [2, 2048, 8192], P(None, ('shard', 'context'), 'tensor'), may hold values from 3.2768 to 32.768
- vector_second: float32 [7, 2048], P(None, 'tensor'), may hold values from 81.92 to 819.2
- hidden_second: float32 [8192], P('tensor'), may hold values from 7.3728 to 73.728
Outputs:
- output: bfloat16 [8, 1024, 2048], P('shard', 'context', 'tensor')
- input_grad: bfloat16 [8, 1024, 2048], P('shard', 'context', 'tensor')
- attn_grad: float32 [4, 2048, 2048], P(None, ('shard', 'context'), 'tensor')
- mlp_grad: float32 [2, 2048, 8192], P(None, ('shard', 'context'), 'tensor')
- vector_grad: float32 [7, 2048], P(None, 'tensor')
- hidden_grad: float32 [8192], P('tensor')
- attn_new: float32 [4, 2048, 2048], P(None, ('shard', 'context'), 'tensor')
- mlp_new: float32 [2, 2048, 8192], P(None, ('shard', 'context'), 'tensor')
- vector_new: float32 [7, 2048], P(None, 'tensor')
- hidden_new: float32 [8192], P('tensor')
- attn_moment_new: float32 [4, 2048, 2048], P(None, ('shard', 'context'), 'tensor')
- mlp_moment_new: float32 [2, 2048, 8192], P(None, ('shard', 'context'), 'tensor')
- vector_moment_new: float32 [7, 2048], P(None, 'tensor')
- hidden_moment_new: float32 [8192], P('tensor')
- attn_second_new: float32 [4, 2048, 2048], P(None, ('shard', 'context'), 'tensor')
- mlp_second_new: float32 [2, 2048, 8192], P(None, ('shard', 'context'), 'tensor')
- vector_second_new: float32 [7, 2048], P(None, 'tensor')
- hidden_second_new: float32 [8192], P('tensor')
Inputs may be any that keep to these rules, and one draw needn't show every extreme that they name: `doc_lengths`: each row lists its 8 documents in order; they fill the row, and the longest in each row has 512 tokens.
All inputs are finite; a program needn't handle non-finite values.
Results may differ from a plain program's by a relative error of at most 0.006.
The roundings to bfloat16 on the way count: a program that leaves them out, or rounds other values in their place, can miss the bound.
Values may be sent and summed in bfloat16 or wider, within the bound.
A program may use at most 256 MiB of HBM per device.

v0:
```python
import jax
import jax.numpy as jnp
from jax import lax
from jax.sharding import PartitionSpec as P

D = 2048
HEADS = 32
HD = 64
ROT = 32
STEP = 7


norm_epsilon = 1e-05
first_beta = 0.9
second_beta = 0.95
adam_epsilon = 1e-08
learn_rate = 0.1
weight_decay = 0.1
rotary_base = 10000.0
masked_score = -1e30


def rotate(field, cosine, sine, half_rot):
    first = field[:, :, :half_rot]
    second = field[:, :, half_rot : 2 * half_rot]
    return jnp.concatenate(
        [
            first * cosine - second * sine,
            second * cosine + first * sine,
            field[:, :, 2 * half_rot :],
        ],
        axis=2,
    )


def block_scores(query_blk, key_blk, scale):
    return jnp.einsum("eq,ek->qk", query_blk, key_blk, preferred_element_type=jnp.float32) * scale


def block_mask(doc_row, q_start, k_start, block):
    q_docs = lax.dynamic_slice_in_dim(doc_row, q_start, block)
    k_docs = lax.dynamic_slice_in_dim(doc_row, k_start, block)
    offsets = jnp.arange(block, dtype=jnp.int32)
    causal = (k_start + offsets)[None, :] <= (q_start + offsets)[:, None]
    return (q_docs[:, None] == k_docs[None, :]) & causal


def block_empty(doc_row, q_start, k_start, block):
    return doc_row[k_start + block - 1] < doc_row[q_start]


def attend_item(query, key_rows, values, doc_row, block, scale):
    head_dim, length = query.shape

    def query_step(q_block, carry):
        out_acc, lse_acc = carry
        q_start = q_block * block
        query_blk = lax.dynamic_slice_in_dim(query, q_start, block, 1)

        def stats_step(k_block, state):
            k_start = k_block * block

            def stats_live(state_in):
                run_max, run_sum = state_in
                key_blk = lax.dynamic_slice_in_dim(key_rows, k_start, block, 1)
                allowed = block_mask(doc_row, q_start, k_start, block)
                scores = jnp.where(allowed, block_scores(query_blk, key_blk, scale), masked_score)
                new_max = jnp.maximum(run_max, jnp.max(scores, axis=1))
                weights = jnp.where(allowed, jnp.exp(scores - new_max[:, None]), 0.0)
                return (new_max, run_sum * jnp.exp(run_max - new_max) + jnp.sum(weights, axis=1))

            return lax.cond(
                block_empty(doc_row, q_start, k_start, block),
                lambda state_in: state_in,
                stats_live,
                state,
            )

        first_state = (
            jnp.full((block,), masked_score, jnp.float32),
            jnp.zeros((block,), jnp.float32),
        )
        run_max, run_sum = lax.fori_loop(0, q_block + 1, stats_step, first_state)
        lse_blk = run_max + jnp.log(run_sum)

        def value_step(k_block, acc):
            k_start = k_block * block

            def value_live(acc_in):
                key_blk = lax.dynamic_slice_in_dim(key_rows, k_start, block, 1)
                value_blk = lax.dynamic_slice_in_dim(values, k_start, block, 1)
                allowed = block_mask(doc_row, q_start, k_start, block)
                scores = block_scores(query_blk, key_blk, scale)
                probs = jnp.where(allowed, jnp.exp(scores - lse_blk[:, None]), 0.0).astype(
                    jnp.bfloat16
                )
                return acc_in + jnp.einsum(
                    "qk,ek->eq", probs, value_blk, preferred_element_type=jnp.float32
                )

            return lax.cond(
                block_empty(doc_row, q_start, k_start, block),
                lambda acc_in: acc_in,
                value_live,
                acc,
            )

        acc = lax.fori_loop(0, q_block + 1, value_step, jnp.zeros((head_dim, block), jnp.float32))
        out_acc = lax.dynamic_update_slice_in_dim(out_acc, acc.astype(jnp.bfloat16), q_start, 1)
        lse_acc = lax.dynamic_update_slice_in_dim(lse_acc, lse_blk, q_start, 0)
        return (out_acc, lse_acc)

    first_carry = (jnp.zeros((head_dim, length), jnp.bfloat16), jnp.zeros((length,), jnp.float32))
    return lax.fori_loop(0, length // block, query_step, first_carry)


def attend_back(query, key_rows, values, grad_out, lse, doc_row, block, scale):
    head_dim, length = query.shape

    def query_step(q_block, carry):
        grad_query, grad_key, grad_value = carry
        q_start = q_block * block
        query_blk = lax.dynamic_slice_in_dim(query, q_start, block, 1)
        gout_blk = lax.dynamic_slice_in_dim(grad_out, q_start, block, 1)
        lse_blk = lax.dynamic_slice_in_dim(lse, q_start, block, 0)

        def pieces(k_start):
            key_blk = lax.dynamic_slice_in_dim(key_rows, k_start, block, 1)
            value_blk = lax.dynamic_slice_in_dim(values, k_start, block, 1)
            allowed = block_mask(doc_row, q_start, k_start, block)
            scores = block_scores(query_blk, key_blk, scale)
            probs = jnp.where(allowed, jnp.exp(scores - lse_blk[:, None]), 0.0)
            dprobs = jnp.einsum(
                "eq,ek->qk", gout_blk, value_blk, preferred_element_type=jnp.float32
            )
            return (key_blk, probs, dprobs)

        def delta_step(k_block, delta):
            k_start = k_block * block

            def delta_live(delta_in):
                key_blk, probs, dprobs = pieces(k_start)
                return delta_in + jnp.sum(probs * dprobs, axis=1)

            return lax.cond(
                block_empty(doc_row, q_start, k_start, block),
                lambda delta_in: delta_in,
                delta_live,
                delta,
            )

        delta = lax.fori_loop(0, q_block + 1, delta_step, jnp.zeros((block,), jnp.float32))

        def grad_step(k_block, state):
            k_start = k_block * block

            def grad_live(state_in):
                query_part, key_all, value_all = state_in
                key_blk, probs, dprobs = pieces(k_start)
                dscores = (probs * (dprobs - delta[:, None])).astype(jnp.bfloat16)
                query_part = query_part + jnp.einsum(
                    "qk,ek->eq", dscores, key_blk, preferred_element_type=jnp.float32
                )
                key_add = (
                    jnp.einsum("qk,eq->ek", dscores, query_blk, preferred_element_type=jnp.float32)
                    * scale
                )
                value_add = jnp.einsum(
                    "qk,eq->ek",
                    probs.astype(jnp.bfloat16),
                    gout_blk,
                    preferred_element_type=jnp.float32,
                )
                key_all = lax.dynamic_update_slice_in_dim(
                    key_all,
                    lax.dynamic_slice_in_dim(key_all, k_start, block, 1) + key_add,
                    k_start,
                    1,
                )
                value_all = lax.dynamic_update_slice_in_dim(
                    value_all,
                    lax.dynamic_slice_in_dim(value_all, k_start, block, 1) + value_add,
                    k_start,
                    1,
                )
                return (query_part, key_all, value_all)

            return lax.cond(
                block_empty(doc_row, q_start, k_start, block),
                lambda state_in: state_in,
                grad_live,
                state,
            )

        first_state = (jnp.zeros((head_dim, block), jnp.float32), grad_key, grad_value)
        query_part, grad_key, grad_value = lax.fori_loop(0, q_block + 1, grad_step, first_state)
        grad_query = lax.dynamic_update_slice_in_dim(grad_query, query_part * scale, q_start, 1)
        return (grad_query, grad_key, grad_value)

    zero_grid = jnp.zeros((head_dim, length), jnp.float32)
    grad_query, grad_key, grad_value = lax.fori_loop(
        0, length // block, query_step, (zero_grid, zero_grid, zero_grid)
    )
    return (
        grad_query.astype(jnp.bfloat16),
        grad_key.astype(jnp.bfloat16),
        grad_value.astype(jnp.bfloat16),
    )


def adam_update(weight, moment, second, grad):
    count = float(STEP)
    new_moment = first_beta * moment + (1.0 - first_beta) * grad
    new_second = second_beta * second + (1.0 - second_beta) * grad * grad
    moment_hat = new_moment / (1.0 - first_beta**count)
    second_hat = new_second / (1.0 - second_beta**count)
    new_weight = weight - learn_rate * (
        moment_hat / (jnp.sqrt(second_hat) + adam_epsilon) + weight_decay * weight
    )
    return (new_weight, new_moment, new_second)


def body(
    inputs,
    cotangent,
    doc_lengths,
    attn_weights,
    mlp_weights,
    vectors,
    hidden_bias,
    attn_moment,
    mlp_moment,
    vector_moment,
    hidden_moment,
    attn_second,
    mlp_second,
    vector_second,
    hidden_second,
):
    sequences, local_len, width_part = inputs.shape
    n_context = lax.axis_size("context")
    n_tensor = lax.axis_size("tensor")
    heads_here = HEADS // n_tensor
    tokens_here = sequences * local_len
    length = local_len * n_context
    block = min(512, length)
    per_device = sequences * heads_here // n_context
    scale = HD ** (-0.5)
    half_rot = ROT // 2
    ends = jnp.cumsum(doc_lengths, axis=1)
    starts = ends - doc_lengths
    all_index = jnp.arange(length, dtype=jnp.int32)
    doc_ids = jnp.sum((all_index[None, :, None] >= ends[:, None, :]).astype(jnp.int32), axis=2)
    local_index = lax.axis_index("context") * local_len + jnp.arange(local_len, dtype=jnp.int32)
    inside = (local_index[None, :, None] >= starts[:, None, :]) & (
        local_index[None, :, None] < ends[:, None, :]
    )
    doc_start = jnp.sum(jnp.where(inside, starts[:, None, :], 0), axis=2)
    position = (local_index[None, :] - doc_start).astype(jnp.float32)
    freq = rotary_base ** (-(2.0 * jnp.arange(half_rot, dtype=jnp.float32)) / ROT)
    angle = freq[None, :, None] * position[:, None, :]
    cosine = jnp.cos(angle)[:, None]
    sine = jnp.sin(angle)[:, None]
    norm_low = vectors[0:2].astype(jnp.bfloat16)
    tokens_full, norm_full = (
        lax.all_gather(inputs, "tensor", axis=2, tiled=True),
        lax.all_gather(norm_low, "tensor", axis=1, tiled=True),
    )
    rows_in = tokens_full.astype(jnp.float32).reshape(tokens_here, D)
    mean_val = jnp.mean(rows_in, axis=1, keepdims=True)
    centered = rows_in - mean_val
    variance = jnp.mean(centered * centered, axis=1, keepdims=True)
    inv_std = lax.rsqrt(variance + norm_epsilon)
    normal = centered * inv_std
    gain_full = norm_full[0].astype(jnp.float32)
    normed = (normal * gain_full + norm_full[1].astype(jnp.float32)).astype(jnp.bfloat16)
    attn_full, mlp_full = (
        lax.all_gather(attn_weights.astype(jnp.bfloat16), ("shard", "context"), axis=1, tiled=True),
        lax.all_gather(mlp_weights.astype(jnp.bfloat16), ("shard", "context"), axis=1, tiled=True),
    )
    token_grid = normed.reshape(sequences, local_len, D)
    qkv_weights = attn_full[0:3].reshape(3, D, heads_here, HD)
    projected = jnp.einsum(
        "std,cdhe->cshet", token_grid, qkv_weights, preferred_element_type=jnp.float32
    )
    query_pre = projected[0] + vectors[2].reshape(heads_here, HD)[None, :, :, None]
    key_pre = projected[1] + vectors[3].reshape(heads_here, HD)[None, :, :, None]
    value_pre = projected[2] + vectors[4].reshape(heads_here, HD)[None, :, :, None]
    outgoing = jnp.stack(
        [
            rotate(query_pre, cosine, sine, half_rot),
            rotate(key_pre, cosine, sine, half_rot),
            value_pre,
        ]
    ).astype(jnp.bfloat16)
    outgoing = outgoing.reshape(3, sequences * heads_here, HD, local_len)
    attn_in = lax.all_to_all(outgoing, "context", split_axis=1, concat_axis=3, tiled=True)
    item_index = lax.axis_index("context") * per_device + jnp.arange(per_device, dtype=jnp.int32)
    item_docs = jnp.take(doc_ids, item_index // heads_here, axis=0)

    def attend_one(parts):
        query, key_part, value_part, doc_row = parts
        return attend_item(query, key_part, value_part, doc_row, block, scale)

    attn_out, lse = lax.map(attend_one, (attn_in[0], attn_in[1], attn_in[2], item_docs))
    heads_out = lax.all_to_all(attn_out, "context", split_axis=2, concat_axis=0, tiled=True)
    heads_grid = heads_out.reshape(sequences, heads_here, HD, local_len)
    out_weights = attn_full[3].reshape(D, heads_here, HD)
    branch = jnp.einsum(
        "shet,ohe->sto", heads_grid, out_weights, preferred_element_type=jnp.float32
    ).reshape(tokens_here, D)
    pre_act = jnp.dot(normed, mlp_full[0], preferred_element_type=jnp.float32) + hidden_bias
    gelu_value, gelu_back = jax.vjp(lambda field: jax.nn.gelu(field, approximate=True), pre_act)
    hidden = gelu_value.astype(jnp.bfloat16)
    branch = branch + jnp.einsum(
        "tf,of->to", hidden, mlp_full[1], preferred_element_type=jnp.float32
    )
    summed = lax.psum_scatter(branch, "tensor", scatter_dimension=1, tiled=True)
    input_rows = inputs.astype(jnp.float32).reshape(tokens_here, width_part)
    output = (
        (input_rows + summed + vectors[5] + vectors[6])
        .astype(jnp.bfloat16)
        .reshape(sequences, local_len, width_part)
    )
    grad_full = lax.all_gather(cotangent, "tensor", axis=2, tiled=True)
    grad_rows = grad_full.reshape(tokens_here, D)
    attn_back, mlp_back = (
        lax.all_gather(attn_weights.astype(jnp.bfloat16), ("shard", "context"), axis=1, tiled=True),
        lax.all_gather(mlp_weights.astype(jnp.bfloat16), ("shard", "context"), axis=1, tiled=True),
    )
    out_back = attn_back[3].reshape(D, heads_here, HD)
    grad_heads = jnp.einsum(
        "sto,ohe->shet", grad_full, out_back, preferred_element_type=jnp.float32
    ).astype(jnp.bfloat16)
    grad_heads = grad_heads.reshape(sequences * heads_here, HD, local_len)
    grad_items = lax.all_to_all(grad_heads, "context", split_axis=0, concat_axis=2, tiled=True)

    def attend_grad(parts):
        query, key_part, value_part, gout, lse_row, doc_row = parts
        return attend_back(query, key_part, value_part, gout, lse_row, doc_row, block, scale)

    grad_query_item, grad_key_item, grad_value_item = lax.map(
        attend_grad, (attn_in[0], attn_in[1], attn_in[2], grad_items, lse, item_docs)
    )
    grads_back = lax.all_to_all(
        jnp.stack([grad_query_item, grad_key_item, grad_value_item]),
        "context",
        split_axis=3,
        concat_axis=1,
        tiled=True,
    )
    grad_grid = grads_back.reshape(3, sequences, heads_here, HD, local_len)
    grad_query = rotate(grad_grid[0].astype(jnp.float32), cosine, -sine, half_rot).astype(
        jnp.bfloat16
    )
    grad_key = rotate(grad_grid[1].astype(jnp.float32), cosine, -sine, half_rot).astype(
        jnp.bfloat16
    )
    grad_proj = jnp.stack([grad_query, grad_key, grad_grid[2]])
    qkv_back = attn_back[0:3].reshape(3, D, heads_here, HD)
    qkv_grad = jnp.einsum(
        "std,cshet->cdhe", token_grid, grad_proj, preferred_element_type=jnp.float32
    ).reshape(3, D, width_part)
    normed_grad = jnp.einsum(
        "cshet,cdhe->std", grad_proj, qkv_back, preferred_element_type=jnp.float32
    ).reshape(tokens_here, D)
    out_grad = jnp.einsum(
        "sto,shet->ohe", grad_full, heads_grid, preferred_element_type=jnp.float32
    ).reshape(D, width_part)
    hidden_act_grad = jnp.dot(grad_rows, mlp_back[1], preferred_element_type=jnp.float32)
    pre_grad = gelu_back(hidden_act_grad)[0].astype(jnp.bfloat16)
    second_grad = jnp.einsum("to,tf->of", grad_rows, hidden, preferred_element_type=jnp.float32)
    first_grad = jnp.einsum("td,tf->df", normed, pre_grad, preferred_element_type=jnp.float32)
    normed_grad = normed_grad + jnp.einsum(
        "tf,df->td", pre_grad, mlp_back[0], preferred_element_type=jnp.float32
    )
    norm_stats = jnp.stack([jnp.sum(normed_grad * normal, axis=0), jnp.sum(normed_grad, axis=0)])
    scaled = normed_grad * gain_full
    input_part = inv_std * (
        scaled
        - jnp.mean(scaled, axis=1, keepdims=True)
        - normal * jnp.mean(scaled * normal, axis=1, keepdims=True)
    )
    input_slice, norm_slice = (
        lax.psum_scatter(input_part, "tensor", scatter_dimension=1, tiled=True),
        lax.psum_scatter(norm_stats, "tensor", scatter_dimension=1, tiled=True),
    )
    cot_rows = cotangent.astype(jnp.float32).reshape(tokens_here, width_part)
    input_grad = (
        (cot_rows + input_slice).astype(jnp.bfloat16).reshape(sequences, local_len, width_part)
    )
    cot_total = jnp.sum(cot_rows, axis=0)
    query_bias_grad = jnp.sum(grad_query.astype(jnp.float32), axis=(0, 3)).reshape(width_part)
    key_bias_grad = jnp.sum(grad_key.astype(jnp.float32), axis=(0, 3)).reshape(width_part)
    value_bias_grad = jnp.sum(grad_grid[2].astype(jnp.float32), axis=(0, 3)).reshape(width_part)
    local_vectors = jnp.stack(
        [
            norm_slice[0],
            norm_slice[1],
            query_bias_grad,
            key_bias_grad,
            value_bias_grad,
            cot_total,
            cot_total,
        ]
    )
    local_hidden = jnp.sum(pre_grad.astype(jnp.float32), axis=0)
    vector_grad, hidden_grad = lax.psum((local_vectors, local_hidden), ("shard", "context"))
    attn_local = jnp.concatenate([qkv_grad, out_grad[None]], axis=0)
    mlp_local = jnp.stack([first_grad, second_grad])
    attn_grad, mlp_grad = (
        lax.psum_scatter(attn_local, ("shard", "context"), scatter_dimension=1, tiled=True),
        lax.psum_scatter(mlp_local, ("shard", "context"), scatter_dimension=1, tiled=True),
    )
    attn_new, attn_moment_new, attn_second_new = adam_update(
        attn_weights, attn_moment, attn_second, attn_grad
    )
    mlp_new, mlp_moment_new, mlp_second_new = adam_update(
        mlp_weights, mlp_moment, mlp_second, mlp_grad
    )
    vector_new, vector_moment_new, vector_second_new = adam_update(
        vectors, vector_moment, vector_second, vector_grad
    )
    hidden_new, hidden_moment_new, hidden_second_new = adam_update(
        hidden_bias, hidden_moment, hidden_second, hidden_grad
    )
    return (
        output,
        input_grad,
        attn_grad,
        mlp_grad,
        vector_grad,
        hidden_grad,
        attn_new,
        mlp_new,
        vector_new,
        hidden_new,
        attn_moment_new,
        mlp_moment_new,
        vector_moment_new,
        hidden_moment_new,
        attn_second_new,
        mlp_second_new,
        vector_second_new,
        hidden_second_new,
    )


def solution(mesh):
    return jax.shard_map(
        body,
        mesh=mesh,
        in_specs=(
            P("shard", "context", "tensor"),
            P("shard", "context", "tensor"),
            P("shard", None),
            P(None, ("shard", "context"), "tensor"),
            P(None, ("shard", "context"), "tensor"),
            P(None, "tensor"),
            P("tensor"),
            P(None, ("shard", "context"), "tensor"),
            P(None, ("shard", "context"), "tensor"),
            P(None, "tensor"),
            P("tensor"),
            P(None, ("shard", "context"), "tensor"),
            P(None, ("shard", "context"), "tensor"),
            P(None, "tensor"),
            P("tensor"),
        ),
        out_specs=(
            P("shard", "context", "tensor"),
            P("shard", "context", "tensor"),
            P(None, ("shard", "context"), "tensor"),
            P(None, ("shard", "context"), "tensor"),
            P(None, "tensor"),
            P("tensor"),
            P(None, ("shard", "context"), "tensor"),
            P(None, ("shard", "context"), "tensor"),
            P(None, "tensor"),
            P("tensor"),
            P(None, ("shard", "context"), "tensor"),
            P(None, ("shard", "context"), "tensor"),
            P(None, "tensor"),
            P("tensor"),
            P(None, ("shard", "context"), "tensor"),
            P(None, ("shard", "context"), "tensor"),
            P(None, "tensor"),
            P("tensor"),
        ),
        check_vma=False,
    )
```

profile of v0, /device:TPU:0, one launch (start us, length us, event | category | flops | bytes accessed | tf_op | source)
XLA Modules:
  0.0 1545.1 jit_solution(11216418029102425786)
XLA Ops:
  27.4 65.7 %all-gather.5.cloned.1.call-done = bf16[4,256,2048]{2,1,0:T(8,128)(2,1)} async-done(((bf16[4,256,512]{2,1,0:T(8,128)(2,1)}), bf16[4,256,2048]{2,1,0:T(8,128)(2,1)}) %all-gather.5.cloned.1.call-update) | async-done | bytes 4194320 | tf_op jit(solution)/shard_map/all_gather | solution.py:266
  101.5 46.8 %all-gather.7.cloned.1.call-done = bf16[4,2048,512]{2,1,0:T(8,128)(2,1)} async-done(((bf16[4,256,512]{2,1,0:T(8,128)(2,1)}), bf16[4,2048,512]{2,1,0:T(8,128)(2,1)}) %all-gather.7.cloned.1.call-update) | async-done | bytes 8388624 | tf_op jit(solution)/shard_map/all_gather | solution.py:278
  167.1 63.6 %all-gather.11.cloned.1.call-done = bf16[4,256,2048]{2,1,0:T(8,128)(2,1)} async-done(((bf16[4,256,512]{2,1,0:T(8,128)(2,1)}), bf16[4,256,2048]{2,1,0:T(8,128)(2,1)}) %all-gather.11.cloned.1.call-update) | async-done | bytes 4194320 | tf_op jit(solution)/shard_map/all_gather | solution.py:325
  267.1 51.6 %all-to-all-done = bf16[3,32,64,256]{3,2,0,1:T(8,128)(2,1)S(1)} async-done(((bf16[3,32,64,256]{3,2,0,1:T(8,128)(2,1)}), bf16[3,32,64,256]{3,2,0,1:T(8,128)(2,1)S(1)}, u32[]{:S(2)}, u32[]{:S(2)}) %all-to-all-start) | async-done | bytes 3145760 | tf_op jit(solution)/shard_map/all_to_all | solution.py:297
  330.4 159.5 %while.289 = (s32[]{:T(128)}, bf16[8,64,1024]{2,1,0:T(8,128)(2,1)}, f32[8,1024]{1,0:T(8,128)S(1)}, bf16[8,64,1024]{2,1,0:T(8,128)(2,1)S(1)}, s32[8,1024]{1,0:T(8...) while((s32[]{:T(128)}, bf16[8,64,1024]{2,1,0:T(8,128)(2,1)}, ...), condition=%wide.region_18.19_spmd, body=%wide.region_5.18_spmd.sunk | while | flops 105713184 | bytes 4438764 | solution.py:305
  331.4 18.2 %while.292 = (s32[]{:T(128)}, bf16[64,1024]{1,0:T(8,128)(2,1)S(1)}, f32[1024]{0:T(1024)S(1)}, bf16[64,1024]{1,0:T(8,128)(2,1)S(1)}, s32[1024]{0:T(1024)S(1)}, /*...) while((s32[]{:T(128)}, bf16[64,1024]{1,0:T(8,128)(2,1)S(1)}, ...), condition=%wide.region_17.17_spmd, body=%wide.region_6.16_spmd.sunk | while | flops 105713184 | bytes 3238173 | solution.py:114
  351.4 18.1 %while.292 = (s32[]{:T(128)}, bf16[64,1024]{1,0:T(8,128)(2,1)S(1)}, f32[1024]{0:T(1024)S(1)}, bf16[64,1024]{1,0:T(8,128)(2,1)S(1)}, s32[1024]{0:T(1024)S(1)}, /*...) while((s32[]{:T(128)}, bf16[64,1024]{1,0:T(8,128)(2,1)S(1)}, ...), condition=%wide.region_17.17_spmd, body=%wide.region_6.16_spmd.sunk | while | flops 105713184 | bytes 3238173 | solution.py:114
  371.3 18.1 %while.292 = (s32[]{:T(128)}, bf16[64,1024]{1,0:T(8,128)(2,1)S(1)}, f32[1024]{0:T(1024)S(1)}, bf16[64,1024]{1,0:T(8,128)(2,1)S(1)}, s32[1024]{0:T(1024)S(1)}, /*...) while((s32[]{:T(128)}, bf16[64,1024]{1,0:T(8,128)(2,1)S(1)}, ...), condition=%wide.region_17.17_spmd, body=%wide.region_6.16_spmd.sunk | while | flops 105713184 | bytes 3238173 | solution.py:114
  391.2 18.1 %while.292 = (s32[]{:T(128)}, bf16[64,1024]{1,0:T(8,128)(2,1)S(1)}, f32[1024]{0:T(1024)S(1)}, bf16[64,1024]{1,0:T(8,128)(2,1)S(1)}, s32[1024]{0:T(1024)S(1)}, /*...) while((s32[]{:T(128)}, bf16[64,1024]{1,0:T(8,128)(2,1)S(1)}, ...), condition=%wide.region_17.17_spmd, body=%wide.region_6.16_spmd.sunk | while | flops 105713184 | bytes 3238173 | solution.py:114
  411.1 18.1 %while.292 = (s32[]{:T(128)}, bf16[64,1024]{1,0:T(8,128)(2,1)S(1)}, f32[1024]{0:T(1024)S(1)}, bf16[64,1024]{1,0:T(8,128)(2,1)S(1)}, s32[1024]{0:T(1024)S(1)}, /*...) while((s32[]{:T(128)}, bf16[64,1024]{1,0:T(8,128)(2,1)S(1)}, ...), condition=%wide.region_17.17_spmd, body=%wide.region_6.16_spmd.sunk | while | flops 105713184 | bytes 3238173 | solution.py:114
  431.1 18.1 %while.292 = (s32[]{:T(128)}, bf16[64,1024]{1,0:T(8,128)(2,1)S(1)}, f32[1024]{0:T(1024)S(1)}, bf16[64,1024]{1,0:T(8,128)(2,1)S(1)}, s32[1024]{0:T(1024)S(1)}, /*...) while((s32[]{:T(128)}, bf16[64,1024]{1,0:T(8,128)(2,1)S(1)}, ...), condition=%wide.region_17.17_spmd, body=%wide.region_6.16_spmd.sunk | while | flops 105713184 | bytes 3238173 | solution.py:114
  451.0 18.1 %while.292 = (s32[]{:T(128)}, bf16[64,1024]{1,0:T(8,128)(2,1)S(1)}, f32[1024]{0:T(1024)S(1)}, bf16[64,1024]{1,0:T(8,128)(2,1)S(1)}, s32[1024]{0:T(1024)S(1)}, /*...) while((s32[]{:T(128)}, bf16[64,1024]{1,0:T(8,128)(2,1)S(1)}, ...), condition=%wide.region_17.17_spmd, body=%wide.region_6.16_spmd.sunk | while | flops 105713184 | bytes 3238173 | solution.py:114
  470.9 18.1 %while.292 = (s32[]{:T(128)}, bf16[64,1024]{1,0:T(8,128)(2,1)S(1)}, f32[1024]{0:T(1024)S(1)}, bf16[64,1024]{1,0:T(8,128)(2,1)S(1)}, s32[1024]{0:T(1024)S(1)}, /*...) while((s32[]{:T(128)}, bf16[64,1024]{1,0:T(8,128)(2,1)S(1)}, ...), condition=%wide.region_17.17_spmd, body=%wide.region_6.16_spmd.sunk | while | flops 105713184 | bytes 3238173 | solution.py:114
  503.7 195.2 %while.291 = (s32[]{:T(128)}, bf16[8,64,1024]{2,1,0:T(8,128)(2,1)}, bf16[8,64,1024]{2,1,0:T(8,128)(2,1)}, bf16[8,64,1024]{2,1,0:T(8,128)(2,1)}, bf16[8,64,1024]{...) while((s32[]{:T(128)}, bf16[8,64,1024]{2,1,0:T(8,128)(2,1)}, ...), condition=%wide.region_32.33_spmd, body=%wide.region_20.0_spmd.sunk | while | flops 239962144 | bytes 11810782 | solution.py:342
  506.6 20.1 %while.293 = (s32[]{:T(128)}, bf16[64,1024]{1,0:T(8,128)(2,1)S(1)}, f32[64,1024]{1,0:T(8,128)S(1)}, f32[64,1024]{1,0:T(8,128)S(1)}, bf16[64,1024]{1,0:T(8,128)(2...) while((s32[]{:T(128)}, bf16[64,1024]{1,0:T(8,128)(2,1)S(1)}, ...), condition=%wide.region_31.31_spmd, body=%wide.region_21.30_spmd.sunk | while | flops 239765536 | bytes 9041385 | solution.py:201
  531.0 20.1 %while.293 = (s32[]{:T(128)}, bf16[64,1024]{1,0:T(8,128)(2,1)S(1)}, f32[64,1024]{1,0:T(8,128)S(1)}, f32[64,1024]{1,0:T(8,128)S(1)}, bf16[64,1024]{1,0:T(8,128)(2...) while((s32[]{:T(128)}, bf16[64,1024]{1,0:T(8,128)(2,1)S(1)}, ...), condition=%wide.region_31.31_spmd, body=%wide.region_21.30_spmd.sunk | while | flops 239765536 | bytes 9041385 | solution.py:201
  555.3 20.1 %while.293 = (s32[]{:T(128)}, bf16[64,1024]{1,0:T(8,128)(2,1)S(1)}, f32[64,1024]{1,0:T(8,128)S(1)}, f32[64,1024]{1,0:T(8,128)S(1)}, bf16[64,1024]{1,0:T(8,128)(2...) while((s32[]{:T(128)}, bf16[64,1024]{1,0:T(8,128)(2,1)S(1)}, ...), condition=%wide.region_31.31_spmd, body=%wide.region_21.30_spmd.sunk | while | flops 239765536 | bytes 9041385 | solution.py:201
  579.7 20.1 %while.293 = (s32[]{:T(128)}, bf16[64,1024]{1,0:T(8,128)(2,1)S(1)}, f32[64,1024]{1,0:T(8,128)S(1)}, f32[64,1024]{1,0:T(8,128)S(1)}, bf16[64,1024]{1,0:T(8,128)(2...) while((s32[]{:T(128)}, bf16[64,1024]{1,0:T(8,128)(2,1)S(1)}, ...), condition=%wide.region_31.31_spmd, body=%wide.region_21.30_spmd.sunk | while | flops 239765536 | bytes 9041385 | solution.py:201
  604.1 20.1 %while.293 = (s32[]{:T(128)}, bf16[64,1024]{1,0:T(8,128)(2,1)S(1)}, f32[64,1024]{1,0:T(8,128)S(1)}, f32[64,1024]{1,0:T(8,128)S(1)}, bf16[64,1024]{1,0:T(8,128)(2...) while((s32[]{:T(128)}, bf16[64,1024]{1,0:T(8,128)(2,1)S(1)}, ...), condition=%wide.region_31.31_spmd, body=%wide.region_21.30_spmd.sunk | while | flops 239765536 | bytes 9041385 | solution.py:201
  628.5 20.1 %while.293 = (s32[]{:T(128)}, bf16[64,1024]{1,0:T(8,128)(2,1)S(1)}, f32[64,1024]{1,0:T(8,128)S(1)}, f32[64,1024]{1,0:T(8,128)S(1)}, bf16[64,1024]{1,0:T(8,128)(2...) while((s32[]{:T(128)}, bf16[64,1024]{1,0:T(8,128)(2,1)S(1)}, ...), condition=%wide.region_31.31_spmd, body=%wide.region_21.30_spmd.sunk | while | flops 239765536 | bytes 9041385 | solution.py:201
  652.9 20.1 %while.293 = (s32[]{:T(128)}, bf16[64,1024]{1,0:T(8,128)(2,1)S(1)}, f32[64,1024]{1,0:T(8,128)S(1)}, f32[64,1024]{1,0:T(8,128)S(1)}, bf16[64,1024]{1,0:T(8,128)(2...) while((s32[]{:T(128)}, bf16[64,1024]{1,0:T(8,128)(2,1)S(1)}, ...), condition=%wide.region_31.31_spmd, body=%wide.region_21.30_spmd.sunk | while | flops 239765536 | bytes 9041385 | solution.py:201
  677.3 20.1 %while.293 = (s32[]{:T(128)}, bf16[64,1024]{1,0:T(8,128)(2,1)S(1)}, f32[64,1024]{1,0:T(8,128)S(1)}, f32[64,1024]{1,0:T(8,128)S(1)}, bf16[64,1024]{1,0:T(8,128)(2...) while((s32[]{:T(128)}, bf16[64,1024]{1,0:T(8,128)(2,1)S(1)}, ...), condition=%wide.region_31.31_spmd, body=%wide.region_21.30_spmd.sunk | while | flops 239765536 | bytes 9041385 | solution.py:201
  744.1 19.1 %all-to-all-done.3 = bf16[4,2,196608]{2,1,0:T(2,128)(2,1)} async-done(((bf16[4,2,196608]{2,1,0:T(2,128)(2,1)}), bf16[4,2,196608]{2,1,0:T(2,128)(2,1)}, u32[]{:S(2)}, u32[]{:S(2)}) %all-to-all-start.3) | async-done | bytes 3145760 | tf_op jit(solution)/shard_map/all_to_all | solution.py:345
  836.9 21.7 %convert_reduce_fusion = (f32[2048]{0:T(1024)}, bf16[1024,2048]{1,0:T(8,128)(2,1)}) fusion(f32[1024,2048]{1,0:T(8,128)S(1)} %fusion.66, f32[2048]{0:T(1024)S(1)} %copy-done.41, bf16[1024,2048]{1,0:T(8,128)(2,1)S(1)} %bitcast.370, bf16[2,2048,2048]{2,1,0:T(8,128)(2,1)} %all-gather.9.cloned.1.call-done), kind=kOutput, calls=%fused_computation.115 | convolution fusion | flops 8638167040 | bytes 25182208 | tf_op jit(solution)/shard_map/dot_general | solution.py:370
  858.7 18.6 %multiply_reduce_fusion = (f32[2048]{0:T(1024)S(1)}, f32[1024]{0:T(1024)S(1)}, f32[1024]{0:T(1024)S(1)}, f32[2048]{0:T(1024)S(1)}, bf16[1024,2048]{1,0:T(8,128)(2,1)}, /*index=5*/f32[1024,2048]{1,0:T(8,128)}) fusion(bf16[4,256,2048]{2,1,0:T(8,128)(2,1)S(1)} %copy-done.1, f32[1024]{0:T(1024)S(1)} %bitcast.361, f32[1024]{0:T(1024)S(1)} %bitcast.363, ...), kind=kOutput, calls=%fused_computation.116 | convolution fusion | flops 8619288576 | bytes 37797888 | tf_op jit(solution)/shard_map/tf,df->td/dot_general | solution.py:374
  910.2 20.8 %bitcast_add_fusion.1 = f32[1024,2048]{1,0:T(8,128)} fusion(f32[1024,2048,1]{1,0,2:T(8,128)} %fusion.119, bf16[2,2048,2048]{2,1,0:T(8,128)(2,1)} %all-gather.9.cloned.1.call-done, f32[1024,2048]{1,0:T(8,128)} %copy-done.48, f32[2048]{0:T(1024)S(1)} %copy-done.41), kind=kOutput, calls=%fused_computation.114 | convolution fusion | flops 8613003264 | bytes 33562624 | tf_op jit(solution)/shard_map/tf,of->to/dot_general | solution.py:315
  944.1 17.0 %convolution_bitcast_fusion.2 = f32[1,2048,2048]{2,1,0:T(8,128)} fusion(bf16[1024,2048]{1,0:T(8,128)(2,1)} %bitcast.369, f32[1024,2048]{1,0:T(8,128)} %copy-done.48, f32[2048]{0:T(1024)S(1)} %copy-done.41), kind=kOutput, calls=%fused_computation.100 | convolution fusion | flops 8610906112 | bytes 29368320 | tf_op jit(solution)/shard_map/to,tf->of/dot_general | solution.py:372
  961.1 18.9 %pad_maximum_fusion = f32[2,2048,2048]{2,1,0:T(8,128)} fusion(f32[1,2048,2048]{2,1,0:T(8,128)} %convolution_bitcast_fusion.2, f32[1,2048,2048]{2,1,0:T(8,128)S(1)} %convolution_bitcast_fusion.3), kind=kLoop, calls=%fused_computation.96 | loop fusion | flops 8388608 | bytes 67108864 | tf_op jit(solution)/shard_map/stack | solution.py:410
  991.5 24.8 %all-reduce = (f32[7,512]{1,0:T(8,128)S(1)}, f32[2048]{0:T(1024)S(1)}) all-reduce(f32[7,512]{1,0:T(8,128)S(1)} %stack.71, f32[2048]{0:T(1024)S(1)} %copy-done.44), channel_id=1, replica_groups=mesh['shard'=2,'context'=4,'tensor'=4] {'shard','context'}, use_global_device_ids=true, to_apply=%region_45.46 | all-reduce | flops 5632 | bytes 45056 | tf_op jit(solution)/shard_map/psum | solution.py:408
  1029.4 140.0 %reduce-scatter.10.cloned.1.call-done = f32[1024,512]{1,0:T(8,128)} async-done(((f32[1024,2048]{1,0:T(8,128)}), f32[1024,512]{1,0:T(8,128)}) %reduce-scatter.10.cloned.1.call-update) | async-done | bytes 2097168 | tf_op jit(solution)/shard_map/reduce_scatter | solution.py:385
  1172.3 144.7 %reduce-scatter.8.cloned.1.call-done = f32[1024,512]{1,0:T(8,128)} async-done(((f32[1024,2048]{1,0:T(8,128)}), f32[1024,512]{1,0:T(8,128)}) %reduce-scatter.8.cloned.1.call-update) | async-done | bytes 2097168 | tf_op jit(solution)/shard_map/reduce_scatter | solution.py:318
  1320.0 207.3 %reduce-scatter.14.cloned.1.call-done = f32[2,256,2048]{2,1,0:T(8,128)} async-done(((f32[2,2048,2048]{2,1,0:T(8,128)}), f32[2,256,2048]{2,1,0:T(8,128)}) %reduce-scatter.14.cloned.1.call-update) | async-done | bytes 4194320 | tf_op jit(solution)/shard_map/reduce_scatter | solution.py:413
  (1369 shorter events, 925.3 us)
Async XLA Ops:
  7.2 85.9 %all-gather.5.cloned.1.call-start = ((), (), s32[]{:S(2)}) async-start(), calls=%async_computation.9 | async-start | bytes 5242880 | tf_op jit(solution)/shard_map/all_gather | solution.py:266
  7.9 140.4 %all-gather.7.cloned.1.call-start = ((), (), s32[]{:S(2)}) async-start(), calls=%async_computation.10 | async-start | bytes 9437184 | tf_op jit(solution)/shard_map/all_gather | solution.py:278
  10.7 220.0 %all-gather.11.cloned.1.call-start = ((), (), s32[]{:S(2)}) async-start(), calls=%async_computation.13 | async-start | bytes 5242880 | tf_op jit(solution)/shard_map/all_gather | solution.py:325
  27.4 224.0 %copy-start.23 = (f32[4,16,256]{2,1,0:T(8,128)}, f32[4,16,256]{2,1,0:T(8,128)S(1)}, u32[]{:S(2)}) copy-start(f32[4,16,256]{2,1,0:T(8,128)S(1)} %get-tuple-element.2472) | copy-start | bytes 196612
  27.4 71.1 %copy-start.26 = (f32[1,2048]{1,0:T(1,128)}, f32[1,2048]{1,0:T(1,128)S(1)}, u32[]{:S(2)}) copy-start(f32[1,2048]{1,0:T(1,128)S(1)} %get-tuple-element.2468) | copy-start | bytes 24580
  27.4 71.1 %copy-start.30 = (f32[1,2048]{1,0:T(1,128)}, f32[1,2048]{1,0:T(1,128)S(1)}, u32[]{:S(2)}) copy-start(f32[1,2048]{1,0:T(1,128)S(1)} %get-tuple-element.2469) | copy-start | bytes 24580
  237.0 17.9 %all-to-all-start.2 = ((bf16[32,64,256]{2,1,0:T(8,128)(2,1)}), bf16[32,64,256]{2,1,0:T(8,128)(2,1)S(1)}, u32[]{:S(2)}, u32[]{:S(2)}) async-start(bf16[32,64,256]{2,1,0:T(8,128)(2,1)} %bitcast.62), calls=%async_computation.3 | async-start | bytes 2097152 | tf_op jit(solution)/shard_map/all_to_all | solution.py:336
  255.9 62.8 %all-to-all-start = ((bf16[3,32,64,256]{3,2,0,1:T(8,128)(2,1)}), bf16[3,32,64,256]{3,2,0,1:T(8,128)(2,1)S(1)}, u32[]{:S(2)}, u32[]{:S(2)}) async-start(bf16[3,32,64,256]{3,2,0,1:T(8,128)(2,1)} %pad_maximum_fusion.3), calls=%async_computation | async-start | bytes 6291456 | tf_op jit(solution)/shard_map/all_to_all | solution.py:297
  259.6 564.6 %all-gather.9.cloned.1.call-start = ((), (), s32[]{:S(2)}) async-start(), calls=%async_computation.11 | async-start | bytes 18874368 | tf_op jit(solution)/shard_map/all_gather | solution.py:279
  496.1 225.3 %all-to-all-start.1 = ((bf16[4,2,65536]{2,1,0:T(2,128)(2,1)}), bf16[4,2,65536]{2,1,0:T(2,128)(2,1)}, u32[]{:S(2)}, u32[]{:S(2)}) async-start(bf16[4,2,65536]{2,1,0:T(2,128)(2,1)} %reshape.490), calls=%async_computation.1 | async-start | bytes 2097152 | tf_op jit(solution)/shard_map/all_to_all | solution.py:306
  721.4 41.8 %all-to-all-start.3 = ((bf16[4,2,196608]{2,1,0:T(2,128)(2,1)}), bf16[4,2,196608]{2,1,0:T(2,128)(2,1)}, u32[]{:S(2)}, u32[]{:S(2)}) async-start(bf16[4,2,196608]{2,1,0:T(2,128)(2,1)} %reshape.492), calls=%async_computation.4 | async-start | bytes 6291456 | tf_op jit(solution)/shard_map/all_to_all | solution.py:345
  726.2 264.2 %reduce-scatter.16.cloned.1.call-start = ((), (), s32[]{:S(2)}) async-start(), calls=%async_computation.17 | async-start | bytes 1310720
  836.9 21.8 %copy-start.48 = (f32[1024,2048]{1,0:T(8,128)}, f32[1024,2048]{1,0:T(8,128)S(1)}, u32[]{:S(2)}) copy-start(f32[1024,2048]{1,0:T(8,128)S(1)} %fusion.66) | copy-start | bytes 25165828
  836.9 21.7 %copy-start.1 = (bf16[4,256,2048]{2,1,0:T(8,128)(2,1)S(1)}, bf16[4,256,2048]{2,1,0:T(8,128)(2,1)}, u32[]{:S(2)}) copy-start(bf16[4,256,2048]{2,1,0:T(8,128)(2,1)} %all-gather.5.cloned.1.call-done) | copy-start | bytes 12582916
  836.9 21.7 %copy-start.27 = (f32[1,2048]{1,0:T(1,128)S(1)}, f32[1,2048]{1,0:T(1,128)}, u32[]{:S(2)}) copy-start(f32[1,2048]{1,0:T(1,128)} %copy-done.26) | copy-start | bytes 24580
  836.9 21.7 %copy-start.31 = (f32[1,2048]{1,0:T(1,128)S(1)}, f32[1,2048]{1,0:T(1,128)}, u32[]{:S(2)}) copy-start(f32[1,2048]{1,0:T(1,128)} %copy-done.30) | copy-start | bytes 24580
  836.9 21.7 %copy-start.37 = (f32[1,2,4,128]{3,1,2,0:T(2,128)S(1)}, f32[1,2,4,128]{3,1,2,0:T(2,128)}, u32[]{:S(2)}) copy-start(f32[1,2,4,128]{3,1,2,0:T(2,128)} %copy.135) | copy-start | bytes 12292
  836.9 21.7 %copy-start.38 = (f32[1,2,4,128]{3,1,2,0:T(2,128)S(1)}, f32[1,2,4,128]{3,1,2,0:T(2,128)}, u32[]{:S(2)}) copy-start(f32[1,2,4,128]{3,1,2,0:T(2,128)} %copy.134) | copy-start | bytes 12292
  878.6 144.0 %reduce-scatter.12.cloned.1.call-start = ((), (), s32[]{:S(2)}) async-start(), calls=%async_computation.15 | async-start | bytes 18874368 | tf_op jit(solution)/shard_map/reduce_scatter | solution.py:412
  890.5 278.9 %reduce-scatter.10.cloned.1.call-start = ((), (), s32[]{:S(2)}) async-start(), calls=%async_computation.14 | async-start | bytes 10485760 | tf_op jit(solution)/shard_map/reduce_scatter | solution.py:385
  898.8 418.3 %reduce-scatter.8.cloned.1.call-start = ((), (), s32[]{:S(2)}) async-start(), calls=%async_computation.12 | async-start | bytes 10485760 | tf_op jit(solution)/shard_map/reduce_scatter | solution.py:318
  931.0 596.3 %reduce-scatter.14.cloned.1.call-start = ((), (), s32[]{:S(2)}) async-start(), calls=%async_computation.16 | async-start | bytes 37748736 | tf_op jit(solution)/shard_map/reduce_scatter | solution.py:413
  981.2 35.1 %copy-start.42 = (f32[2048]{0:T(1024)S(1)}, f32[2048]{0:T(1024)}, u32[]{:S(2)}) copy-start(f32[2048]{0:T(1024)} %param.49) | copy-start | bytes 24580
  981.2 35.1 %copy-start.43 = (f32[2048]{0:T(1024)S(1)}, f32[2048]{0:T(1024)}, u32[]{:S(2)}) copy-start(f32[2048]{0:T(1024)} %param.53) | copy-start | bytes 24580
  981.2 35.7 %copy-start.29 = (f32[7,512]{1,0:T(8,128)S(1)}, f32[7,512]{1,0:T(8,128)}, u32[]{:S(2)}) copy-start(f32[7,512]{1,0:T(8,128)} %param.44) | copy-start | bytes 43012
  981.3 35.7 %copy-start.32 = (f32[7,512]{1,0:T(8,128)S(1)}, f32[7,512]{1,0:T(8,128)}, u32[]{:S(2)}) copy-start(f32[7,512]{1,0:T(8,128)} %param.48) | copy-start | bytes 43012
  981.3 35.7 %copy-start.33 = (f32[7,512]{1,0:T(8,128)S(1)}, f32[7,512]{1,0:T(8,128)}, u32[]{:S(2)}) copy-start(f32[7,512]{1,0:T(8,128)} %param.52) | copy-start | bytes 43012
  981.3 41.3 %copy-start.6 = (f32[4,256,512]{2,1,0:T(8,128)S(1)}, f32[4,256,512]{2,1,0:T(8,128)}, u32[]{:S(2)}) copy-start(f32[4,256,512]{2,1,0:T(8,128)} %param.42) | copy-start | bytes 6291460
  1016.3 13.0 copy-start.45
  1029.3 287.7 %copy-start.10 = (bf16[4,256,512]{2,1,0:T(8,128)(2,1)S(1)}, bf16[4,256,512]{2,1,0:T(8,128)(2,1)}, u32[]{:S(2)}) copy-start(bf16[4,256,512]{2,1,0:T(8,128)(2,1)} %param.39) | copy-start | bytes 3145732
  1029.3 287.7 %copy-start.39 = (f32[1,512]{1,0:T(1,128)S(1)}, f32[1,512]{1,0:T(1,128)}, u32[]{:S(2)}) copy-start(f32[1,512]{1,0:T(1,128)} %get-tuple-element.2466) | copy-start | bytes 6148
  1029.3 287.7 %copy-start.40 = (f32[1,512]{1,0:T(1,128)S(1)}, f32[1,512]{1,0:T(1,128)}, u32[]{:S(2)}) copy-start(f32[1,512]{1,0:T(1,128)} %get-tuple-element.2467) | copy-start | bytes 6148
  (31 other events, 149.6 us)
Sparse Core Ops, SparseCore 0:
  9.6 83.4 all-gather.4
  95.6 52.7 all-gather.6
  149.9 80.7 all-gather.10
  264.1 107.4 all-gather.8
  878.7 24.4 reduce-scatter.15
  907.3 115.2 reduce-scatter.11
  1024.9 144.3 reduce-scatter.9
  1171.7 145.2 reduce-scatter.7
  1321.2 206.0 reduce-scatter.13
where the time goes:
time: 1560 us; the launch traced here: 1550 us
  waiting for transfers between devices  746 us (48%)
  local copies, waits for them, and re-layouts  249 us (16%)
  matrix products  239 us (15%)
  loops' own time  128 us (8%)
  other arithmetic  112 us (7%)
  blocking collectives  38.6 us (2%)
  starting transfers between devices  17.3 us (1%)
    reduce_scatter x1, waiting for transfers between devices, body(): lax.psum_scatter(mlp_local, ('shard', 'context'), scatter_dimension=1, ti...  207 us
    reduce_scatter x1, waiting for transfers between devices, body(): summed = lax.psum_scatter(branch, 'tensor', scatter_dimension=1, tiled=True)  145 us
    reduce_scatter x1, waiting for transfers between devices, body(): lax.psum_scatter(input_part, 'tensor', scatter_dimension=1, tiled=True)  140 us
    dynamic_slice x128, local copies, waits for them, and re-layouts, block_empty(): return doc_row[k_start + block - 1] < doc_row[q_start]  76 us
    all_gather x1, waiting for transfers between devices, body(): lax.all_gather(inputs, 'tensor', axis=2, tiled=True)  65.7 us
    all_gather x1, waiting for transfers between devices, body(): grad_full = lax.all_gather(cotangent, 'tensor', axis=2, tiled=True)  63.6 us
    all_to_all x1, waiting for transfers between devices, body(): lax.all_to_all(outgoing, 'context', split_axis=1, concat_axis=3, tiled=True)  51.6 us
    all_gather x1, waiting for transfers between devices, body(): lax.all_gather(attn_weights.astype(jnp.bfloat16), ('shard', 'context'), a...  46.8 us
  transfers between devices with their start and end apart: 13, of which 10 were waited for; matrix products, arithmetic and copies ran while one was open for 34% of the time, Pallas kernels for 0%

commit v1 on v0

--- a/solution.py
+++ b/solution.py
@@ -1,6 +1,10 @@
+import functools
+
 import jax
 import jax.numpy as jnp
 from jax import lax
+from jax.experimental import pallas as pl
+from jax.experimental.pallas import tpu as pltpu
 from jax.sharding import PartitionSpec as P
 
 D = 2048
@@ -446,9 +450,825 @@
     )
 
 
+def attention_kernel(
+    first_ref,
+    q_ref,
+    k_ref,
+    v_ref,
+    gout_ref,
+    cos_ref,
+    low_ref,
+    high_ref,
+    start_ref,
+    out_ref,
+    gq_ref,
+    gk_ref,
+    gv_ref,
+    key_cat,
+    value_cat,
+    raw,
+    dprob,
+    gk_acc,
+    gv_acc,
+    *,
+    block,
+    steps,
+    scale,
+    half_rot,
+):
+    row, step = pl.program_id(0), pl.program_id(2)
+    pair = q_ref.shape[1]
+    lane_low = lax.broadcasted_iota(jnp.int32, (block, pair), 1) < pair // 2
+    contract_last = (((1,), (1,)), ((), ()))
+    contract_first = (((0,), (0,)), ((), ()))
+    plain = (((1,), (0,)), ((), ()))
+
+    def dot(a, b, dims):
+        return lax.dot_general(a, b, dims, preferred_element_type=jnp.float32)
+
+    def turn(field, start, sign):
+        rows = pl.ds(start, block)
+        return (
+            field * cos_ref[rows, :]
+            + sign * (pltpu.roll(field, pair - half_rot, 1) * low_ref[rows, :])
+            + sign * (pltpu.roll(field, half_rot, 1) * high_ref[rows, :])
+        )
+
+    @pl.when(step == 0)
+    def _():
+        gk_acc[...] = jnp.zeros_like(gk_acc)
+        gv_acc[...] = jnp.zeros_like(gv_acc)
+
+        @pl.loop(0, steps)
+        def _(j):
+            at = pl.multiple_of(j * block, block)
+            keys = turn(k_ref[pl.ds(at, block), :], at, 1.0)
+            values = v_ref[pl.ds(at, block), :]
+            for half in range(2):
+                keep = lane_low if half == 0 else jnp.logical_not(lane_low)
+                rows = pl.ds(pl.multiple_of(2 * at, 2 * block) + half * block, block)
+                key_cat[rows, :] = jnp.where(keep, keys, 0.0).astype(jnp.bfloat16)
+                value_cat[rows, :] = jnp.where(keep, values, 0.0).astype(jnp.bfloat16)
+
+    q_at = pl.multiple_of(step * block, block)
+    queries = turn(q_ref[...], q_at, 1.0).astype(jnp.bfloat16)
+    queries = (queries.astype(jnp.float32) * scale).astype(jnp.bfloat16)
+    gout = gout_ref[...]
+    first = first_ref[row * steps + step]
+    begin = start_ref[...]
+    q_pos = q_at + lax.broadcasted_iota(jnp.int32, (block, block), 0)
+    k_lane = lax.broadcasted_iota(jnp.int32, (block, block), 1)
+
+    def rows_of(j):
+        return pl.ds(pl.multiple_of(j * (2 * block), 2 * block), 2 * block)
+
+    def score_step(j, tops):
+        scores = dot(queries, key_cat[rows_of(j), :], contract_last)
+        k_pos = j * block + k_lane
+        allowed = (k_pos <= q_pos) & (k_pos >= begin)
+        new_tops = []
+        for half in range(2):
+            part = jnp.where(allowed, scores[:, half * block : (half + 1) * block], -3e38)
+            raw[j, :, half * block : (half + 1) * block] = part
+            new_tops.append(jnp.maximum(tops[half], jnp.max(part, axis=1, keepdims=True)))
+        return tuple(new_tops)
+
+    low_start = jnp.full((block, 1), -3e38, jnp.float32)
+    tops = lax.fori_loop(first, step + 1, score_step, (low_start, low_start))
+
+    def weight_step(j, sums):
+        dp = dot(gout, value_cat[rows_of(j), :], contract_last)
+        dprob[j] = dp
+        new_sums = []
+        for half in range(2):
+            cols = slice(half * block, (half + 1) * block)
+            weights = jnp.exp(raw[j, :, cols] - tops[half])
+            raw[j, :, cols] = weights
+            new_sums.append(sums[2 * half] + jnp.sum(weights, axis=1, keepdims=True))
+            new_sums.append(
+                sums[2 * half + 1] + jnp.sum(weights * dp[:, cols], axis=1, keepdims=True)
+            )
+        return tuple(new_sums)
+
+    zero = jnp.zeros((block, 1), jnp.float32)
+    sums = lax.fori_loop(first, step + 1, weight_step, (zero,) * 4)
+    inverse = [1.0 / sums[0], 1.0 / sums[2]]
+    delta = [sums[1] * inverse[0], sums[3] * inverse[1]]
+
+    def grad_step(j, carry):
+        out_acc, gq_acc = carry
+        probs, dscores = [], []
+        for half in range(2):
+            cols = slice(half * block, (half + 1) * block)
+            full = raw[j, :, cols] * inverse[half]
+            probs.append(full.astype(jnp.bfloat16))
+            dscores.append((full * (dprob[j, :, cols] - delta[half])).astype(jnp.bfloat16))
+        probs = jnp.concatenate(probs, axis=1)
+        dscores = jnp.concatenate(dscores, axis=1)
+        rows = rows_of(j)
+        out_acc = out_acc + dot(probs, value_cat[rows, :], plain)
+        gq_acc = gq_acc + dot(dscores, key_cat[rows, :], plain)
+        gk_acc[rows, :] += dot(dscores, queries, contract_first)
+        gv_acc[rows, :] += dot(probs, gout, contract_first)
+        return (out_acc, gq_acc)
+
+    blank = jnp.zeros((block, pair), jnp.float32)
+    out_acc, gq_acc = lax.fori_loop(first, step + 1, grad_step, (blank, blank))
+    out_ref[...] = out_acc.astype(jnp.bfloat16)
+    gq_low = (gq_acc * scale).astype(jnp.bfloat16).astype(jnp.float32)
+    gq_ref[...] = turn(gq_low, q_at, -1.0).astype(jnp.bfloat16)
+
+    @pl.when(step == steps - 1)
+    def _():
+        @pl.loop(0, steps)
+        def _(j):
+            at = pl.multiple_of(j * block, block)
+            top = pl.ds(pl.multiple_of(2 * at, 2 * block), block)
+            bottom = pl.ds(pl.multiple_of(2 * at, 2 * block) + block, block)
+            gk = jnp.where(lane_low, gk_acc[top, :], gk_acc[bottom, :])
+            gk_low = gk.astype(jnp.bfloat16).astype(jnp.float32)
+            gk_ref[pl.ds(at, block), :] = turn(gk_low, at, -1.0).astype(jnp.bfloat16)
+            gv_ref[pl.ds(at, block), :] = jnp.where(
+                lane_low, gv_acc[top, :], gv_acc[bottom, :]
+            ).astype(jnp.bfloat16)
+
+
+def attention(qkv_pre, gout, tables, begin, first, rows, length, block):
+    width = gout.shape[1]
+    pair = 2 * HD
+    pairs = width // pair
+    steps = length // block
+    cosine, low, high = tables
+    whole = pl.BlockSpec((length, pair), lambda r, h, i, f: (r, h))
+    keys = pl.BlockSpec((length, pair), lambda r, h, i, f: (r, pairs + h))
+    values = pl.BlockSpec((length, pair), lambda r, h, i, f: (r, 2 * pairs + h))
+    part = pl.BlockSpec((block, pair), lambda r, h, i, f: (r * steps + i, h))
+    table = pl.BlockSpec((length, pair), lambda r, h, i, f: (r, 0))
+    shape = jax.ShapeDtypeStruct((rows * length, width), jnp.bfloat16)
+    return pl.pallas_call(
+        functools.partial(
+            attention_kernel, block=block, steps=steps, scale=HD ** (-0.5), half_rot=ROT // 2
+        ),
+        out_shape=(shape,) * 4,
+        grid_spec=pltpu.PrefetchScalarGridSpec(
+            num_scalar_prefetch=1,
+            grid=(rows, pairs, steps),
+            in_specs=[
+                part,
+                keys,
+                values,
+                part,
+                table,
+                table,
+                table,
+                pl.BlockSpec((block, 1), lambda r, h, i, f: (r * steps + i, 0)),
+            ],
+            out_specs=[part, part, whole, whole],
+            scratch_shapes=[
+                pltpu.VMEM((2 * length, pair), jnp.bfloat16),
+                pltpu.VMEM((2 * length, pair), jnp.bfloat16),
+                pltpu.VMEM((steps, block, 2 * block), jnp.float32),
+                pltpu.VMEM((steps, block, 2 * block), jnp.float32),
+                pltpu.VMEM((2 * length, pair), jnp.float32),
+                pltpu.VMEM((2 * length, pair), jnp.float32),
+            ],
+        ),
+        compiler_params=pltpu.CompilerParams(
+            dimension_semantics=("arbitrary", "arbitrary", "arbitrary")
+        ),
+        cost_estimate=pl.CostEstimate(
+            flops=rows * width * length * length * 8,
+            bytes_accessed=rows * length * width * 30,
+            transcendentals=rows * pairs * length * length,
+        ),
+    )(first, qkv_pre, qkv_pre, qkv_pre, gout, cosine, low, high, begin)
+
+
+MESH = pl.DeviceIdType.MESH
+
+
+def flipped(index, bits):
+    bit = 1
+    while bit <= bits:
+        if bits & bit:
+            index = index + bit - 2 * bit * ((index // bit) % 2)
+        bit *= 2
+    return index
+
+
+def gather_kernel(
+    x_ref,
+    g_ref,
+    norm_ref,
+    x_out,
+    g_out,
+    normed_out,
+    normed_halves,
+    g_halves,
+    mean_out,
+    inv_out,
+    gain_out,
+    x_buf,
+    g_buf,
+    normed_buf,
+    normed_parts,
+    g_parts,
+    norm_all,
+    own_sem,
+    send_a,
+    recv_a,
+    send_n,
+    recv_n,
+    send_r,
+    recv_r,
+    send_l,
+    recv_l,
+    out_sem,
+    *,
+    n_context,
+    n_tensor,
+    n_block,
+    rows,
+    strip,
+):
+    c, z = lax.axis_index("context"), lax.axis_index("tensor")
+    core = c % 2
+    local_len, width = x_ref.shape[1:]
+    length = local_len * n_context
+    sources, buffers = (x_ref, g_ref), (x_buf, g_buf)
+
+    def peer(k):
+        return flipped(c, k)
+
+    barrier = pltpu.get_barrier_semaphore()
+    for k in range(1, n_context):
+        pl.semaphore_signal(barrier, inc=1, device_id={"context": peer(k)}, device_id_type=MESH)
+    for k in range(1, n_tensor):
+        pl.semaphore_signal(
+            barrier, inc=1, device_id={"tensor": (z + k) % n_tensor}, device_id_type=MESH
+        )
+    pl.semaphore_wait(barrier, n_context + n_tensor - 2)
+
+    def at(r, chunk):
+        return pl.ds(pl.multiple_of(r * length + chunk * local_len, local_len), local_len)
+
+    def piece(f, r, chunk, origin):
+        return buffers[f].at[at(r, chunk), pl.ds(pl.multiple_of(origin * width, width), width)]
+
+    def own_copy(f, r):
+        return pltpu.make_async_copy(
+            sources[f].at[c * rows + r], piece(f, r, c, z), own_sem.at[f, r]
+        )
+
+    own_norm = pltpu.make_async_copy(norm_ref, norm_all.at[z], own_sem.at[2, 0])
+
+    def swap(f, r, k):
+        return pltpu.make_async_remote_copy(
+            src_ref=sources[f].at[peer(k) * rows + r],
+            dst_ref=piece(f, r, c, z),
+            send_sem=send_a.at[f, k - 1, r],
+            recv_sem=recv_a.at[f, k - 1, r],
+            device_id={"context": peer(k)},
+            device_id_type=MESH,
+        )
+
+    def norm_copy(k):
+        return pltpu.make_async_remote_copy(
+            src_ref=norm_ref,
+            dst_ref=norm_all.at[z],
+            send_sem=send_n.at[k - 1],
+            recv_sem=recv_n.at[k - 1],
+            device_id={"tensor": (z + k) % n_tensor},
+            device_id_type=MESH,
+        )
+
+    def hop(f, r, k, d, side, step):
+        origin = z - d if side > 0 else z + d
+        sends, recvs = (send_r, recv_r) if side > 0 else (send_l, recv_l)
+        block = piece(f, r, peer(k), origin)
+        return pltpu.make_async_remote_copy(
+            src_ref=block,
+            dst_ref=block,
+            send_sem=sends.at[f, d - step, k, r],
+            recv_sem=recvs.at[f, d - step, k, r],
+            device_id={"tensor": z + side * (1 - step)},
+            device_id_type=MESH,
+        )
+
+    def has(d, side):
+        return z >= d if side > 0 else z + d <= n_tensor - 1
+
+    def more(side):
+        return z < n_tensor - 1 if side > 0 else z > 0
+
+    for f in range(2):
+        for r in range(rows):
+            own_copy(f, r).start()
+        if f == 0:
+            own_norm.start()
+        for k in range(1, n_context):
+            for r in range(rows):
+                swap(f, r, k).start()
+        if f == 0:
+            for k in range(1, n_tensor):
+                norm_copy(k).start()
+    own_norm.wait()
+    for k in range(1, n_tensor):
+        norm_copy(k).wait_recv()
+
+    gain = jnp.concatenate([norm_all[j, 0:1, :] for j in range(n_tensor)], axis=1)
+    shift = jnp.concatenate([norm_all[j, 1:2, :] for j in range(n_tensor)], axis=1)
+    gain, shift = gain.astype(jnp.float32), shift.astype(jnp.float32)
+    gain_out[...] = gain
+
+    span = x_buf.shape[1] // n_block
+
+    def store_parts(parts, lines, value):
+        for b in range(n_block):
+            cols = slice((b // 2) * span, (b // 2 + 1) * span)
+            parts[(b + core) % 2, lines, cols] = value[:, b * span : (b + 1) * span]
+
+    def finish_x(base):
+        @pl.loop(0, local_len // strip)
+        def _(step):
+            lines = pl.ds(pl.multiple_of(base + step * strip, strip), strip)
+            field = x_buf[lines, :].astype(jnp.float32)
+            mean_val = jnp.mean(field, axis=1, keepdims=True)
+            centered = field - mean_val
+            variance = jnp.mean(centered * centered, axis=1, keepdims=True)
+            inv_std = lax.rsqrt(variance + norm_epsilon)
+            normed = ((centered * inv_std) * gain + shift).astype(jnp.bfloat16)
+            normed_buf[lines, :] = normed
+            store_parts(normed_parts, lines, normed)
+            mean_out[lines, :] = mean_val
+            inv_out[lines, :] = inv_std
+
+    def finish_g(base):
+        @pl.loop(0, local_len // strip)
+        def _(step):
+            lines = pl.ds(pl.multiple_of(base + step * strip, strip), strip)
+            store_parts(g_parts, lines, g_buf[lines, :])
+
+    def results(f, r, k):
+        lines = at(r, peer(k))
+        if f == 0:
+            pairs = [
+                (x_buf.at[lines], x_out.at[lines]),
+                (normed_buf.at[lines], normed_out.at[lines]),
+                (normed_parts.at[0, lines], normed_halves.at[0, lines]),
+                (normed_parts.at[1, lines], normed_halves.at[1, lines]),
+            ]
+        else:
+            pairs = [
+                (g_buf.at[lines], g_out.at[lines]),
+                (g_parts.at[0, lines], g_halves.at[0, lines]),
+                (g_parts.at[1, lines], g_halves.at[1, lines]),
+            ]
+        return [
+            pltpu.make_async_copy(src, dst, out_sem.at[f, k, r, i])
+            for i, (src, dst) in enumerate(pairs)
+        ]
+
+    order = [(f, r, k) for f in range(2) for k in range(n_context) for r in range(rows)]
+    for f, r, k in order:
+        for d in range(n_tensor):
+            if d == 0:
+                if k == 0:
+                    own_copy(f, r).wait()
+                else:
+                    swap(f, r, k).wait_recv()
+            for side in (1, -1):
+                if d > 0:
+
+                    @pl.when(has(d, side))
+                    def _():
+                        hop(f, r, k, d, side, 1).wait_recv()
+
+                if d < n_tensor - 1:
+
+                    @pl.when(has(d, side) & more(side))
+                    def _():
+                        hop(f, r, k, d, side, 0).start()
+
+        base = r * length + peer(k) * local_len
+        if f == 0:
+            finish_x(base)
+        else:
+            finish_g(base)
+        for copy in results(f, r, k):
+            copy.start()
+
+    for f, r, k in order:
+        for d in range(n_tensor - 1):
+            for side in (1, -1):
+
+                @pl.when(has(d, side) & more(side))
+                def _():
+                    hop(f, r, k, d, side, 0).wait_send()
+
+        if k > 0:
+            swap(f, r, k).wait_send()
+        for copy in results(f, r, k):
+            copy.wait()
+    for k in range(1, n_tensor):
+        norm_copy(k).wait_send()
+
+
+def gather_inputs(inputs, cotangent, norm_low, n_context, n_tensor, n_block):
+    sequences, local_len, width = inputs.shape
+    rows = sequences // n_context
+    tokens = sequences * local_len
+    full = width * n_tensor
+    wide, low = jnp.float32, jnp.bfloat16
+    dma = pltpu.SemaphoreType.DMA
+    inside = pl.BlockSpec(memory_space=pltpu.VMEM)
+    outside = pl.BlockSpec(memory_space=pl.ANY)
+    hops = (2, n_tensor - 1, n_context, rows)
+    return pl.pallas_call(
+        functools.partial(
+            gather_kernel,
+            n_context=n_context,
+            n_tensor=n_tensor,
+            n_block=n_block,
+            rows=rows,
+            strip=min(32, local_len),
+        ),
+        out_shape=(
+            jax.ShapeDtypeStruct((tokens, full), low),
+            jax.ShapeDtypeStruct((tokens, full), low),
+            jax.ShapeDtypeStruct((tokens, full), low),
+            jax.ShapeDtypeStruct((2, tokens, full // 2), low),
+            jax.ShapeDtypeStruct((2, tokens, full // 2), low),
+            jax.ShapeDtypeStruct((tokens, 1), wide),
+            jax.ShapeDtypeStruct((tokens, 1), wide),
+            jax.ShapeDtypeStruct((1, full), wide),
+        ),
+        in_specs=[inside] * 3,
+        out_specs=(outside,) * 5 + (inside,) * 3,
+        scratch_shapes=[
+            pltpu.VMEM((tokens, full), low),
+            pltpu.VMEM((tokens, full), low),
+            pltpu.VMEM((tokens, full), low),
+            pltpu.VMEM((2, tokens, full // 2), low),
+            pltpu.VMEM((2, tokens, full // 2), low),
+            pltpu.VMEM((n_tensor, 2, width), low),
+            dma((3, rows)),
+            dma((2, n_context - 1, rows)),
+            dma((2, n_context - 1, rows)),
+            dma((n_tensor - 1,)),
+            dma((n_tensor - 1,)),
+            dma(hops),
+            dma(hops),
+            dma(hops),
+            dma(hops),
+            dma((2, n_context, rows, 4)),
+        ],
+        compiler_params=pltpu.CompilerParams(collective_id=0, has_side_effects=True),
+    )(inputs, cotangent, norm_low)
+
+
+def total_kernel(
+    stats_ref,
+    rest_ref,
+    out_ref,
+    parts,
+    every,
+    send_z,
+    recv_z,
+    send_p,
+    recv_p,
+    *,
+    n_shard,
+    n_context,
+    n_tensor,
+):
+    y, c, z = lax.axis_index("shard"), lax.axis_index("context"), lax.axis_index("tensor")
+    me = y * n_context + c
+    group = n_shard * n_context
+    width = out_ref.shape[1]
+    kept = stats_ref.shape[1]
+
+    barrier = pltpu.get_barrier_semaphore()
+    for k in range(1, n_tensor):
+        pl.semaphore_signal(
+            barrier, inc=1, device_id={"tensor": (z + k) % n_tensor}, device_id_type=MESH
+        )
+
+    def place(k):
+        other = (me + k) % group
+        return {"shard": other // n_context, "context": other % n_context}
+
+    for k in range(1, group):
+        pl.semaphore_signal(barrier, inc=1, device_id=place(k), device_id_type=MESH)
+    pl.semaphore_wait(barrier, n_tensor + group - 2)
+
+    def slice_copy(k):
+        return pltpu.make_async_remote_copy(
+            src_ref=stats_ref.at[(z + k) % n_tensor],
+            dst_ref=parts.at[k],
+            send_sem=send_z.at[k],
+            recv_sem=recv_z.at[k],
+            device_id={"tensor": (z + k) % n_tensor},
+            device_id_type=MESH,
+        )
+
+    for k in range(1, n_tensor):
+        slice_copy(k).start()
+    every[me, kept:, :] = rest_ref[...]
+    total = stats_ref[z]
+    for k in range(1, n_tensor):
+        slice_copy(k).wait_recv()
+        total = total + parts[k]
+    every[me, 0:kept, :] = total
+
+    def spread(k):
+        return pltpu.make_async_remote_copy(
+            src_ref=every.at[me],
+            dst_ref=every.at[me],
+            send_sem=send_p.at[k],
+            recv_sem=recv_p.at[k],
+            device_id=place(k),
+            device_id_type=MESH,
+        )
+
+    def spread_from(k):
+        other = (me + group - k) % group
+        return pltpu.make_async_remote_copy(
+            src_ref=every.at[other],
+            dst_ref=every.at[other],
+            send_sem=send_p.at[k],
+            recv_sem=recv_p.at[k],
+            device_id=place(k),
+            device_id_type=MESH,
+        )
+
+    for k in range(1, group):
+        spread(k).start()
+    for k in range(1, group):
+        spread_from(k).wait_recv()
+    total = every[0]
+    for j in range(1, group):
+        total = total + every[j]
+    out_ref[...] = total
+    for k in range(1, n_tensor):
+        slice_copy(k).wait_send()
+    for k in range(1, group):
+        spread(k).wait_send()
+
+
+def total_vectors(stats, rest, n_shard, n_context, n_tensor):
+    kept, (more, width) = stats.shape[1], rest.shape
+    group = n_shard * n_context
+    dma = pltpu.SemaphoreType.DMA
+    inside = pl.BlockSpec(memory_space=pltpu.VMEM)
+    return pl.pallas_call(
+        functools.partial(
+            total_kernel, n_shard=n_shard, n_context=n_context, n_tensor=n_tensor
+        ),
+        out_shape=jax.ShapeDtypeStruct((kept + more, width), jnp.float32),
+        in_specs=[inside] * 2,
+        out_specs=inside,
+        scratch_shapes=[
+            pltpu.VMEM((n_tensor, kept, width), jnp.float32),
+            pltpu.VMEM((group, kept + more, width), jnp.float32),
+            dma((n_tensor,)),
+            dma((n_tensor,)),
+            dma((group,)),
+            dma((group,)),
+        ],
+        compiler_params=pltpu.CompilerParams(collective_id=1, has_side_effects=True),
+    )(stats, rest)
+
+
+def permute(field, axis, pairs):
+    return lax.ppermute(field, axis, pairs)
+
+
+def ring_shift(field, axis, size, k):
+    return lax.ppermute(field, axis, [(i, (i + k) % size) for i in range(size)])
+
+
+def pick(field, index, axis):
+    return lax.dynamic_index_in_dim(field, index, axis, keepdims=False)
+
+
+def fast_body(
+    inputs,
+    cotangent,
+    doc_lengths,
+    attn_weights,
+    mlp_weights,
+    vectors,
+    hidden_bias,
+    attn_moment,
+    mlp_moment,
+    vector_moment,
+    hidden_moment,
+    attn_second,
+    mlp_second,
+    vector_second,
+    hidden_second,
+):
+    sequences, local_len, width = inputs.shape
+    n_context, n_tensor = lax.axis_size("context"), lax.axis_size("tensor")
+    n_shard = lax.axis_size("shard")
+    rows = sequences // n_context
+    length = local_len * n_context
+    tokens = rows * length
+    block = min(256, length)
+    half_rot = ROT // 2
+    low_type = jnp.bfloat16
+    wide = jnp.float32
+    at_tensor, at_context = lax.axis_index("tensor"), lax.axis_index("context")
+    at_y, at_x, at_core = lax.axis_index("shard"), at_context // 2, at_context % 2
+    flip_core = [(i, i ^ 1) for i in range(n_context)]
+    flip_x = [(i, i ^ 2) for i in range(n_context)]
+    flip_y = [(i, i ^ 1) for i in range(n_shard)]
+
+    def after(field, *others):
+        return lax.optimization_barrier((field,) + others)[0]
+
+    def dot(a, b, left, right):
+        return lax.dot_general(
+            a, b, (((left,), (right,)), ((), ())), preferred_element_type=wide
+        )
+
+    attn_low = jnp.concatenate([attn_weights[i] for i in range(4)], axis=1).astype(low_type)
+    attn_full = lax.all_gather(attn_low, ("shard", "context"), axis=0, tiled=True)
+    mlp_full = lax.all_gather(
+        mlp_weights.astype(low_type), ("shard", "context"), axis=1, tiled=True
+    )
+    w_qkv, w_out = attn_full[:, : 3 * width], attn_full[:, 3 * width :]
+    w_up, w_down = mlp_full[0], mlp_full[1]
+
+    x_full, g_full, normed, normed_halves, g_halves, mean_val, inv_std, gain_full = gather_inputs(
+        inputs,
+        cotangent,
+        vectors[0:2].astype(low_type),
+        n_context,
+        n_tensor,
+        n_shard * n_context,
+    )
+
+    ends = jnp.cumsum(doc_lengths, axis=1)
+    my_ends = lax.dynamic_slice_in_dim(ends, at_context * rows, rows, 0)
+    index = jnp.arange(length, dtype=jnp.int32)
+    doc_start = jnp.max(
+        jnp.where(index[None, :, None] >= my_ends[:, None, :], my_ends[:, None, :], 0), axis=2
+    )
+    first = (doc_start[:, ::block] // block).reshape(-1)
+    begin = doc_start.reshape(tokens, 1)
+    position = (index[None, :] - doc_start).astype(wide).reshape(tokens, 1)
+    lane = jnp.arange(2 * HD, dtype=jnp.int32) % HD
+    freq = rotary_base ** (-(2.0 * (lane % half_rot).astype(wide)) / ROT)
+    angle = position * freq[None, :]
+    cosine, sine = jnp.cos(angle), jnp.sin(angle)
+    tables = (
+        jnp.where(lane < ROT, cosine, 1.0),
+        jnp.where(lane < half_rot, -sine, 0.0),
+        jnp.where((lane >= half_rot) & (lane < ROT), sine, 0.0),
+    )
+
+    qkv_pre = dot(normed, w_qkv, 1, 0) + vectors[2:5].reshape(3 * width)
+    gout = dot(g_full, w_out, 1, 0).astype(low_type)
+    pre_act = dot(normed, w_up, 1, 0) + hidden_bias
+    gelu_value, gelu_back = jax.vjp(lambda field: jax.nn.gelu(field, approximate=True), pre_act)
+    hidden = gelu_value.astype(low_type)
+
+    attended, g_query, g_key, g_value = attention(
+        qkv_pre, gout, tables, begin, first, rows, length, block
+    )
+    g_qkv = jnp.concatenate([g_query, g_key, g_value], axis=1)
+
+    def scatter_features(field):
+        return lax.psum_scatter(field, "tensor", scatter_dimension=1, tiled=True).astype(wide)
+
+    def own_features(field):
+        return lax.dynamic_slice_in_dim(field, at_tensor * width, width, 1).astype(wide)
+
+    def back_rows(field):
+        pieces = field.reshape(rows, n_context, local_len, width)
+        result = jnp.zeros((n_context, rows, local_len, width), field.dtype)
+        for k in range(n_context):
+            piece = pick(pieces, at_context ^ k, 1)
+            if k > 0:
+                piece = permute(piece, "context", [(i, i ^ k) for i in range(n_context)])
+            result = lax.dynamic_update_index_in_dim(result, piece, at_context ^ k, 0)
+        return result.reshape(sequences, local_len, width)
+
+    branch = (dot(attended, w_out, 1, 1) + dot(hidden, w_down, 1, 1)).astype(low_type)
+    summed = scatter_features(branch)
+    output = back_rows(
+        (own_features(x_full) + summed + vectors[5] + vectors[6]).astype(low_type)
+    )
+
+    g_late = after(g_full, branch)
+    pre_grad = gelu_back(dot(g_late, w_down, 1, 0))[0].astype(low_type)
+
+    def reduce_rows(parts, right):
+        mine, other = parts
+        n = right.shape[1]
+        half = n // 2
+        sent = dot(other, right, 0, 0).astype(low_type)
+        chip = (dot(mine, right, 0, 0) + permute(sent, "context", flip_core)).astype(low_type)
+        chip = chip.reshape(n_shard, n_context // 2, -1, n)
+        left, right_part = chip[..., :half], chip[..., half:]
+        from_x = permute(pick(left, 1 - at_x, 1), "context", flip_x)
+        from_y = permute(pick(right_part, 1 - at_y, 0), "shard", flip_y)
+        left, right_part = pick(left, at_x, 1), pick(right_part, at_y, 0)
+
+        def both(a, b, where):
+            return pick(a, where, 0).astype(wide) + pick(b, where, 0).astype(wide)
+
+        next_y = permute(both(left, from_x, 1 - at_y).astype(low_type), "shard", flip_y)
+        next_x = permute(both(right_part, from_y, 1 - at_x).astype(low_type), "context", flip_x)
+        return jnp.concatenate(
+            [both(left, from_x, at_y) + next_y, both(right_part, from_y, at_x) + next_x], axis=1
+        )
+
+    down_grad = reduce_rows(after(g_halves, pre_grad), hidden)
+    up_grad = reduce_rows(normed_halves, pre_grad)
+
+    normed_grad = dot(pre_grad, w_up, 1, 1) + dot(g_qkv, w_qkv, 1, 1)
+    normal = (x_full.astype(wide) - mean_val) * inv_std
+    norm_stats = jnp.stack([jnp.sum(normed_grad * normal, axis=0), jnp.sum(normed_grad, axis=0)])
+    scaled = normed_grad * gain_full
+    input_part = (
+        inv_std
+        * (
+            scaled
+            - jnp.mean(scaled, axis=1, keepdims=True)
+            - normal * jnp.mean(scaled * normal, axis=1, keepdims=True)
+        )
+    ).astype(low_type)
+    g_qkv_late = after(g_qkv, input_part)
+    qkv_grad = reduce_rows(normed_halves, g_qkv_late)
+    out_grad = reduce_rows(g_halves, after(attended, g_qkv_late))
+
+    input_slice = scatter_features(input_part)
+    g_own = own_features(g_full)
+    input_grad = back_rows((g_own + input_slice).astype(low_type))
+
+    stats_grid = norm_stats.reshape(2, n_tensor, width).transpose(1, 0, 2)
+    rest = jnp.concatenate(
+        [
+            jnp.sum(g_qkv.astype(wide), axis=0).reshape(3, width),
+            jnp.sum(g_own, axis=0)[None],
+            jnp.sum(pre_grad.astype(wide), axis=0).reshape(-1, width),
+        ]
+    )
+    totals = total_vectors(stats_grid, rest, n_shard, n_context, n_tensor)
+    vector_grad = jnp.concatenate([totals[0:6], totals[5:6]])
+    hidden_grad = totals[6:].reshape(-1)
+
+    attn_grad = jnp.stack(
+        [qkv_grad[:, i * width : (i + 1) * width] for i in range(3)] + [out_grad]
+    )
+    mlp_grad = jnp.stack([up_grad, down_grad])
+    attn_new, attn_moment_new, attn_second_new = adam_update(
+        attn_weights, attn_moment, attn_second, attn_grad
+    )
+    mlp_new, mlp_moment_new, mlp_second_new = adam_update(
+        mlp_weights, mlp_moment, mlp_second, mlp_grad
+    )
+    vector_new, vector_moment_new, vector_second_new = adam_update(
+        vectors, vector_moment, vector_second, vector_grad
+    )
+    hidden_new, hidden_moment_new, hidden_second_new = adam_update(
+        hidden_bias, hidden_moment, hidden_second, hidden_grad
+    )
+    return (
+        output,
+        input_grad,
+        attn_grad,
+        mlp_grad,
+        vector_grad,
+        hidden_grad,
+        attn_new,
+        mlp_new,
+        vector_new,
+        hidden_new,
+        attn_moment_new,
+        mlp_moment_new,
+        vector_moment_new,
+        hidden_moment_new,
+        attn_second_new,
+        mlp_second_new,
+        vector_second_new,
+        hidden_second_new,
+    )
+
+
+def layer(*arrays):
+    sequences, n_context = arrays[0].shape[0], lax.axis_size("context")
+    if sequences % n_context == 0 and n_context == 4 and lax.axis_size("shard") == 2:
+        return fast_body(*arrays)
+    return body(*arrays)
+
+
 def solution(mesh):
     return jax.shard_map(
-        body,
+        layer,
         mesh=mesh,
         in_specs=(
             P("shard", "context", "tensor"),

time: 1560 us -> 566 us (0.36)
  waiting for transfers between devices: 746 us -> 81 us
  local copies, waits for them, and re-layouts: 249 us -> 18 us
  Pallas kernels: 0 us -> 218 us
  loops' own time: 128 us -> 0 us
  matrix products: 239 us -> 147 us
  other arithmetic: 112 us -> 42.5 us
  blocking collectives: 38.6 us -> 0 us
  starting transfers between devices: 17.3 us -> 35.9 us
    reduce_scatter x4 -> x2, waiting for transfers between devices: 497 us -> 0.02 us  [scatter_features(): lax.psum_scatter(field, 'tensor', scatter_dimension=1, tiled=True)]
    pallas_call x0 -> x3, Pallas kernels: none -> 218 us  [the longest x1 164 us: gather_inputs(): pl.pallas_call(functools.partial(gather_kernel, n_context=n_context, n_te...]
    all_gather x4 -> x2, waiting for transfers between devices: 176 us -> 0.01 us  [the longest x1 0.01 us: fast_body(): lax.all_gather(attn_low, ('shard', 'context'), axis=0, tiled=True)]
    another operation x178 -> x0, loops' own time: 128 us -> none  [the longest x16 32.1 us: query_step(): lax.fori_loop(0, q_block + 1, value_step, jnp.zeros((head_dim, block), jn...]
    dot_general x228 -> x16, matrix products: 239 us -> 147 us  [dot(): lax.dot_general(a, b, (((left,), (right,)), ((), ())), preferred_element_...]
    dynamic_slice x296 -> x0, local copies, waits for them, and re-layouts: 85.2 us -> none  [the longest x128 76 us: block_empty(): return doc_row[k_start + block - 1] < doc_row[q_start]]
    ppermute x0 -> x26, waiting for transfers between devices: none -> 80.9 us  [permute(): return lax.ppermute(field, axis, pairs)]
    all_to_all x4 -> x0, waiting for transfers between devices: 71.3 us -> none  [the longest x1 51.6 us: body(): lax.all_to_all(outgoing, 'context', split_axis=1, concat_axis=3, tiled=True)]
  transfers between devices with their start and end apart: 13 -> 30, of which waited for: 10 -> 9; matrix products, arithmetic and copies ran while one was open for 34% -> 21% of each run, Pallas kernels for 0% -> 39%
where the time goes in v1:
time: 566 us; the launch traced here: 557 us
  Pallas kernels  218 us (39%)
  matrix products  147 us (26%)
  waiting for transfers between devices  81 us (14%)
  other arithmetic  42.5 us (8%)
  starting transfers between devices  35.9 us (6%)
  local copies, waits for them, and re-layouts  18 us (3%)
  between operations  15 us (3%)
    pallas_call x1, Pallas kernels, gather_inputs(): pl.pallas_call(functools.partial(gather_kernel, n_context=n_context, n_te...  164 us
    dot_general x16, matrix products, dot(): lax.dot_general(a, b, (((left,), (right,)), ((), ())), preferred_element_...  147 us
    ppermute x26, waiting for transfers between devices, permute(): return lax.ppermute(field, axis, pairs)  80.9 us
    pallas_call x1, Pallas kernels, attention(): pl.pallas_call(functools.partial(attention_kernel, block=block, steps=ste...  43.4 us
    ppermute x26, starting transfers between devices, permute(): return lax.ppermute(field, axis, pairs)  35.5 us
    sub x4, other arithmetic, adam_update(): weight - learn_rate * (moment_hat / (jnp.sqrt(second_hat) + adam_epsilon)...  13.2 us
    unnamed x74, local copies, waits for them, and re-layouts  11.4 us
  transfers between devices with their start and end apart: 30, of which 9 were waited for; matrix products, arithmetic and copies ran while one was open for 21% of the time, Pallas kernels for 39%

profile of v1, /device:TPU:0, one launch (start us, length us, event | category | flops | bytes accessed | tf_op | source)
XLA Modules:
  0.0 556.9 jit_solution(12563500667158725805)
XLA Ops:
  10.2 3.8 convert_element_type.343
  16.2 163.5 %shard_map.286 = (bf16[1024,2048]{1,0:T(8,128)(2,1)}, bf16[1024,2048]{1,0:T(8,128)(2,1)}, bf16[1024,2048]{1,0:T(8,128)(2,1)}, bf16[2,1024,1024]{2,1,0:T(8,128)(2...) custom-call(bf16[4,256,512]{2,1,0:T(8,128)(2,1)} %x_ref.1, ...), custom_call_target="tpu_custom_call" | custom-call | tf_op jit(solution)/shard_map/pallas_call | solution.py:887
  185.9 6.3 %fusion.55.gout_ref = bf16[1024,512]{1,0:T(8,128)(2,1)} fusion(bf16[1024,2048]{1,0:T(8,128)(2,1)} %get-tuple-element.39, bf16[2048,2048]{1,0:T(8,128)(2,1)} %all-gather.3.cloned.1.call-done), kind=kOutput, calls=%fused_computation.78 | convolution fusion | flops 2148007936 | bytes 7340032 | tf_op jit(solution)/shard_map/dot_general | solution.py:1092
  192.7 8.6 %fusion.16.q_ref.k_ref.v_ref = f32[1024,1536]{1,0:T(8,128)} fusion(bf16[1024,2048]{1,0:T(8,128)(2,1)S(1)} %copy-done.29, bf16[2048,2048]{1,0:T(8,128)(2,1)S(1)} %copy-done.23, f32[1536]{0:T(1024)S(1)} %add.395), kind=kOutput, calls=%fused_computation.33 | convolution fusion | flops 6444023808 | bytes 16785408 | tf_op jit(solution)/shard_map/dot_general | solution.py:1092
  201.3 43.4 %shard_map.287 = (bf16[1024,512]{1,0:T(8,128)(2,1)}, bf16[1024,512]{1,0:T(8,128)(2,1)}, bf16[1024,512]{1,0:T(8,128)(2,1)}, bf16[1024,512]{1,0:T(8,128)(2,1)}) custom-call(s32[4]{0:T(128)} %fusion.90.first_ref, f32[1024,1536]{1,0:T(8,128)} %fusion.16.q_ref.k_ref.v_ref, f32[1024,1536]{1,0:T(8,128)} %fusion.16.q_ref.k_ref.v_ref, ...), custom_call_target="tpu_custom_call" | custom-call | flops 4294967296 | bytes 15728640 | tf_op jit(solution)/shard_map/pallas_call | solution.py:608
  249.1 10.7 %fusion.11 = f32[1024,2048]{1,0:T(8,128)} fusion(bf16[1024,1536]{1,0:T(8,128)(2,1)S(1)} %constant_dynamic-update-slice_fusion.6, bf16[2048,2048]{1,0:T(8,128)(2,1)} %all-gather.3.cloned.1.call-done), kind=kOutput, calls=%fused_computation.28 | convolution fusion | flops 6442450944 | bytes 17825792 | tf_op jit(solution)/shard_map/dot_general | solution.py:1092
  259.8 16.3 %multiply_convert_fusion.1 = (bf16[1024,2048]{1,0:T(8,128)(2,1)S(1)}, f32[1024,2048]{1,0:T(8,128)}) fusion(f32[2048]{0:T(1024)S(1)} %copy-done.18, bf16[1024,2048]{1,0:T(8,128)(2,1)} %get-tuple-element.35, bf16[2,2048,2048]{2,1,0:T(8,128)(2,1)} %all-gather.5.cloned.1.call-done), kind=kOutput, calls=%fused_computation.19 | convolution fusion | flops 8610906112 | bytes 25174016 | tf_op jit(solution)/shard_map/dot_general | solution.py:1092
  276.1 11.0 %fusion.10 = f32[1024,2048]{1,0:T(8,128)} fusion(bf16[1024,2048]{1,0:T(8,128)(2,1)S(1)} %get-tuple-element.97, bf16[2,2048,2048]{2,1,0:T(8,128)(2,1)S(1)} %copy-done.22), kind=kOutput, calls=%fused_computation.23 | convolution fusion | flops 8589934592 | bytes 20971520 | tf_op jit(solution)/shard_map/dot_general | solution.py:1092
  287.2 8.5 %add_convert_fusion.2 = bf16[1024,2048]{1,0:T(8,128)(2,1)} fusion(f32[1024,2048]{1,0:T(8,128)} %fusion.10, bf16[1024,512]{1,0:T(8,128)(2,1)S(1)} %copy-done.30, bf16[2048,2048]{1,0:T(8,128)(2,1)} %all-gather.3.cloned.1.call-done), kind=kOutput, calls=%fused_computation.18 | convolution fusion | flops 2151677952 | bytes 15728640 | tf_op jit(solution)/shard_map/dot_general | solution.py:1092
  295.7 20.2 %convert_reduce_fusion = (f32[2048]{0:T(1024)S(1)}, bf16[1024,2048]{1,0:T(8,128)(2,1)}) fusion(f32[1024,2048]{1,0:T(8,128)} %get-tuple-element.98, f32[2048]{0:T(1024)S(1)} %copy-done.18, bf16[1024,2048]{1,0:T(8,128)(2,1)} %get-tuple-element.39, bf16[2,2048,2048]{2,1,0:T(8,128)(2,1)} %all-gather.5.cloned.1.call-done), kind=kOutput, calls=%fused_computation.11 | convolution fusion | flops 8638167040 | bytes 25182208 | tf_op jit(solution)/shard_map/dot_general | solution.py:1092
  315.9 16.9 %multiply_reduce_fusion = (f32[2048]{0:T(1024)S(1)}, f32[1024]{0:T(1024)S(1)}, f32[1024]{0:T(1024)S(1)}, f32[2048]{0:T(1024)S(1)}, f32[1024,2048]{1,0:T(8,128)S(1)}) fusion(bf16[1024,2048]{1,0:T(8,128)(2,1)} %get-tuple-element.34, f32[1024]{0:T(1024)S(1)} %reduce.2, f32[1024]{0:T(1024)S(1)} %reduce.1, f32[2048]{0:T(1024)S(1)} %bitcast.249, ...), kind=kOutput, calls=%fused_computation.12 | convolution fusion | flops 8612997120 | bytes 33595392 | tf_op jit(solution)/shard_map/dot_general | solution.py:1092
  332.8 5.6 %multiply_convert_fusion = bf16[1024,2048]{1,0:T(8,128)(2,1)} fusion(bf16[1024,2048]{1,0:T(8,128)(2,1)} %get-tuple-element.34, f32[1024,2048]{1,0:T(8,128)S(1)} %get-tuple-element.99, f32[1024]{0:T(1024)S(1)} %broadcast_multiply_fusion, f32[1024]{0:T(1024)S(1)} %reduce.2, f32[1024]{0:T(1024)S(1)} %broadcast_multiply_fusion.1, f32[2048]{0:T(1024)S(1)} %bitcast.250, ...), kind=kLoop, calls=%fused_computation.15 | loop fusion | flops 18874368 | bytes 16801792 | tf_op jit(solution)/shard_map/convert_element_type | solution.py:1203
  338.8 4.3 fusion.52
  343.7 4.9 convolution_convert_fusion
  349.1 9.6 %convolution_convert_fusion.1 = bf16[1024,2048]{1,0:T(8,128)(2,1)} fusion(bf16[1024,2048]{1,0:T(8,128)(2,1)} %copy-done.33, bf16[2,1024,1024]{2,1,0:T(8,128)(2,1)} %get-tuple-element.49), kind=kOutput, calls=%fused_computation.39 | convolution fusion | flops 4297064448 | bytes 10485760 | tf_op jit(solution)/shard_map/dot_general | solution.py:1092
  363.6 10.3 %collective-permute-start.14 = (bf16[2,256,256]{2,1,0:T(8,128)(2,1)S(1)}, bf16[2,256,256]{2,1,0:T(8,128)(2,1)}, u32[]{:S(2)}, u32[]{:S(2)}) collective-permute-start(bf16[2,256,256]{2,1,0:T(8,128)(2,1)S(1)} %dynamic-slice_bitcast_fusion.6), channel_id=1, source_target_pairs={{0,16},{16,0},{1,17},{17,1},{2,18},{18,2},{3,19},{19,3},{4,20},{20... | collective-permute-start | bytes 786440 | tf_op jit(solution)/shard_map/ppermute | solution.py:1044
  373.9 6.3 %convolution_convert_fusion.2 = bf16[1024,2048]{1,0:T(8,128)(2,1)} fusion(bf16[1024,2048]{1,0:T(8,128)(2,1)S(1)} %copy-done.32, bf16[2,1024,1024]{2,1,0:T(8,128)(2,1)S(1)} %copy-done.25), kind=kOutput, calls=%fused_computation.40 | convolution fusion | flops 4297064448 | bytes 10485760 | tf_op jit(solution)/shard_map/dot_general | solution.py:1092
  385.7 6.1 %add_convert_fusion.3 = bf16[1024,1536]{1,0:T(8,128)(2,1)S(1)} fusion(bf16[1024,1536]{1,0:T(8,128)(2,1)} %collective-permute-done.6, bf16[1024,1536]{1,0:T(8,128)(2,1)S(1)} %copy-done.3, bf16[2,1024,1024]{2,1,0:T(8,128)(2,1)} %get-tuple-element.45), kind=kOutput, calls=%fused_computation.27 | convolution fusion | flops 3225944064 | bytes 11534336 | tf_op jit(solution)/shard_map/dot_general | solution.py:1092
  397.4 18.5 %collective-permute-done.13 = bf16[256,256]{1,0:T(8,128)(2,1)S(1)} collective-permute-done((bf16[256,256]{1,0:T(8,128)(2,1)S(1)}, bf16[256,256]{1,0:T(8,128)(2,1)S(1)}, u32[]{:S(2)}, u32[]{:S(2)}) %collective-permute-start.13) | collective-permute-done | bytes 131104 | tf_op jit(solution)/shard_map/ppermute | solution.py:1044
  417.2 6.6 %add_convert_fusion = bf16[1024,2048]{1,0:T(8,128)(2,1)S(1)} fusion(bf16[1024,2048]{1,0:T(8,128)(2,1)} %collective-permute-done.21, bf16[1024,2048]{1,0:T(8,128)(2,1)S(1)} %copy-done.34, bf16[2,1024,1024]{2,1,0:T(8,128)(2,1)S(1)} %copy-done.28), kind=kOutput, calls=%fused_computation.13 | convolution fusion | flops 4301258752 | bytes 14680064 | tf_op jit(solution)/shard_map/dot_general | solution.py:1092
  428.0 7.7 %add_convert_fusion.1 = bf16[1024,2048]{1,0:T(8,128)(2,1)S(1)} fusion(bf16[1024,2048]{1,0:T(8,128)(2,1)} %collective-permute-done.16, bf16[1024,2048]{1,0:T(8,128)(2,1)} %get-tuple-element.101, bf16[2,1024,1024]{2,1,0:T(8,128)(2,1)S(1)} %copy-done.26), kind=kOutput, calls=%fused_computation.14 | convolution fusion | flops 4301258752 | bytes 14680064 | tf_op jit(solution)/shard_map/dot_general | solution.py:1092
  438.8 11.8 %collective-permute-done.24 = bf16[2,256,1024]{2,1,0:T(8,128)(2,1)S(1)} collective-permute-done((bf16[2,256,1024]{2,1,0:T(8,128)(2,1)S(1)}, bf16[2,256,1024]{2,1,0:T(8,128)(2,1)S(1)}, u32[]{:S(2)}, u32[]{:S(2)}) %collective-permute-start.24) | collective-permute-done | bytes 1048608 | tf_op jit(solution)/shard_map/ppermute | solution.py:1044
  454.4 4.4 multiply_subtract_fusion.1
  458.8 14.3 %collective-permute-done.19 = bf16[2,256,1024]{2,1,0:T(8,128)(2,1)S(1)} collective-permute-done((bf16[2,256,1024]{2,1,0:T(8,128)(2,1)S(1)}, bf16[2,256,1024]{2,1,0:T(8,128)(2,1)S(1)}, u32[]{:S(2)}, u32[]{:S(2)}) %collective-permute-start.19) | collective-permute-done | bytes 1048608 | tf_op jit(solution)/shard_map/ppermute | solution.py:1044
  476.9 9.1 %collective-permute-done.25 = bf16[256,1024]{1,0:T(8,128)(2,1)S(1)} collective-permute-done((bf16[256,1024]{1,0:T(8,128)(2,1)S(1)}, bf16[256,1024]{1,0:T(8,128)(2,1)S(1)}, u32[]{:S(2)}, u32[]{:S(2)}) %collective-permute-start.25) | collective-permute-done | bytes 524320 | tf_op jit(solution)/shard_map/ppermute | solution.py:1044
  486.6 7.8 %collective-permute-done.20 = bf16[256,1024]{1,0:T(8,128)(2,1)S(1)} collective-permute-done((bf16[256,1024]{1,0:T(8,128)(2,1)S(1)}, bf16[256,1024]{1,0:T(8,128)(2,1)S(1)}, u32[]{:S(2)}, u32[]{:S(2)}) %collective-permute-start.20) | collective-permute-done | bytes 524320 | tf_op jit(solution)/shard_map/ppermute | solution.py:1044
  499.2 7.5 %multiply_subtract_fusion = (f32[2,256,2048]{2,1,0:T(8,128)}, f32[2,256,2048]{2,1,0:T(8,128)}, f32[2,256,2048]{2,1,0:T(8,128)}, f32[2,256,2048]{2,1,0:T(8,128)}) fusion(f32[2,256,2048]{2,1,0:T(8,128)S(1)} %copy-done, f32[2,256,2048]{2,1,0:T(8,128)S(1)} %copy-done.4, f32[2,256,2048]{2,1,0:T(8,128)S(1)} %copy-done.5, ...), kind=kLoop, calls=%fused_computation.36 | loop fusion | flops 16777216 | bytes 33554432 | tf_op jit(solution)/shard_map/sub | solution.py:221
  509.4 11.0 %shard_map.288 = f32[10,512]{1,0:T(8,128)} custom-call(f32[4,2,512]{2,1,0:T(2,128)} %maximum_bitcast_fusion.3.stats_ref, f32[8,512]{1,0:T(8,128)} %pad_maximum_fusion.4.rest_ref), custom_call_target="tpu_custom_call" | custom-call | tf_op jit(solution)/shard_map/pallas_call | solution.py:1024
  529.6 3.8 collective-permute-done.1
  533.4 4.3 collective-permute-done.2
  537.8 6.8 %collective-permute-done.4 = bf16[1,256,512]{2,1,0:T(8,128)(2,1)S(1)} collective-permute-done((bf16[1,256,512]{2,1,0:T(8,128)(2,1)S(1)}, bf16[1,256,512]{2,1,0:T(8,128)(2,1)S(1)}, u32[]{:S(2)}, u32[]{:S(2)}) %collective-permute-start.4) | collective-permute-done | bytes 262176 | tf_op jit(solution)/shard_map/ppermute | solution.py:1044
  544.6 4.3 collective-permute-done.5
  (208 shorter events, 67.7 us)
Async XLA Ops:
  7.2 178.7 %all-gather.3.cloned.1.call-start = ((), (), s32[]{:S(2)}) async-start(), calls=%async_computation.2 | async-start | bytes 9437184 | tf_op jit(solution)/shard_map/all_gather | solution.py:1097
  10.2 249.6 %all-gather.5.cloned.1.call-start = ((), (), s32[]{:S(2)}) async-start(), calls=%async_computation.3 | async-start | bytes 18874368 | tf_op jit(solution)/shard_map/all_gather | solution.py:1098
  14.1 492.6 %reduce-scatter.5.cloned.1.call-start = ((), (), s32[]{:S(2)}) async-start(), calls=%async_computation.5 | async-start | bytes 5242880 | tf_op jit(solution)/shard_map/reduce_scatter | solution.py:1144
  338.5 183.5 %reduce-scatter.3.cloned.1.call-start = ((), (), s32[]{:S(2)}) async-start(), calls=%async_computation.4 | async-start | bytes 5242880 | tf_op jit(solution)/shard_map/reduce_scatter | solution.py:1144
  343.0 16.1 %collective-permute-start.11 = (bf16[1024,512]{1,0:T(8,128)(2,1)}, bf16[1024,512]{1,0:T(8,128)(2,1)}, u32[]{:S(2)}, u32[]{:S(2)}) collective-permute-start(bf16[1024,512]{1,0:T(8,128)(2,1)} %fusion.52), channel_id=1, source_target_pairs={{0,4},{4,0},{8,12},{12,8},{1,5},{5,1},{9,13},{13,9},{2,6},{6,2},{1... | collective-permute-start | bytes 3145736 | tf_op jit(solution)/shard_map/ppermute | solution.py:1044
  348.5 37.2 %collective-permute-start.6 = (bf16[1024,1536]{1,0:T(8,128)(2,1)}, bf16[1024,1536]{1,0:T(8,128)(2,1)}, u32[]{:S(2)}, u32[]{:S(2)}) collective-permute-start(bf16[1024,1536]{1,0:T(8,128)(2,1)} %convolution_convert_fusion), channel_id=1, source_target_pairs={{0,4},{4,0},{8,12},{12,8},{1,5},{5,1},{9,13},{13,9},{2,6},{6,2},{1... | collective-permute-start | bytes 9437192 | tf_op jit(solution)/shard_map/ppermute | solution.py:1044
  358.6 58.6 %collective-permute-start.21 = (bf16[1024,2048]{1,0:T(8,128)(2,1)}, bf16[1024,2048]{1,0:T(8,128)(2,1)}, u32[]{:S(2)}, u32[]{:S(2)}) collective-permute-start(bf16[1024,2048]{1,0:T(8,128)(2,1)} %convolution_convert_fusion.1), channel_id=1, source_target_pairs={{0,4},{4,0},{8,12},{12,8},{1,5},{5,1},{9,13},{13,9},{2,6},{6,2},{1... | collective-permute-start | bytes 12582920 | tf_op jit(solution)/shard_map/ppermute | solution.py:1044
  363.6 21.0 %collective-permute-start.14 = (bf16[2,256,256]{2,1,0:T(8,128)(2,1)S(1)}, bf16[2,256,256]{2,1,0:T(8,128)(2,1)}, u32[]{:S(2)}, u32[]{:S(2)}) collective-permute-start(bf16[2,256,256]{2,1,0:T(8,128)(2,1)S(1)} %dynamic-slice_bitcast_fusion.6), channel_id=1, source_target_pairs={{0,16},{16,0},{1,17},{17,1},{2,18},{18,2},{3,19},{19,3},{4,20},{20... | collective-permute-start | bytes 786440 | tf_op jit(solution)/shard_map/ppermute | solution.py:1044
  380.2 47.8 %collective-permute-start.16 = (bf16[1024,2048]{1,0:T(8,128)(2,1)}, bf16[1024,2048]{1,0:T(8,128)(2,1)}, u32[]{:S(2)}, u32[]{:S(2)}) collective-permute-start(bf16[1024,2048]{1,0:T(8,128)(2,1)} %convolution_convert_fusion.2), channel_id=1, source_target_pairs={{0,4},{4,0},{8,12},{12,8},{1,5},{5,1},{9,13},{13,9},{2,6},{6,2},{1... | collective-permute-start | bytes 12582920 | tf_op jit(solution)/shard_map/ppermute | solution.py:1044
  382.1 12.0 %collective-permute-start.12 = (bf16[2,256,256]{2,1,0:T(8,128)(2,1)S(1)}, bf16[2,256,256]{2,1,0:T(8,128)(2,1)S(1)}, u32[]{:S(2)}, u32[]{:S(2)}) collective-permute-start(bf16[2,256,256]{2,1,0:T(8,128)(2,1)S(1)} %dynamic-slice_bitcast_fusion.7), channel_id=1, source_target_pairs={{0,8},{4,12},{8,0},{12,4},{1,9},{5,13},{9,1},{13,5},{2,10},{6,14},... | collective-permute-start | bytes 786440 | tf_op jit(solution)/shard_map/ppermute | solution.py:1044
  385.6 9.2 %collective-permute-start.15 = (bf16[256,256]{1,0:T(8,128)(2,1)S(1)}, bf16[256,256]{1,0:T(8,128)(2,1)S(1)}, u32[]{:S(2)}, u32[]{:S(2)}) collective-permute-start(bf16[256,256]{1,0:T(8,128)(2,1)S(1)} %fusion.77), channel_id=1, source_target_pairs={{0,8},{4,12},{8,0},{12,4},{1,9},{5,13},{9,1},{13,5},{2,10},{6,14},... | collective-permute-start | bytes 393224 | tf_op jit(solution)/shard_map/ppermute | solution.py:1044
  391.8 25.5 %copy-start.34 = (bf16[1024,2048]{1,0:T(8,128)(2,1)S(1)}, bf16[1024,2048]{1,0:T(8,128)(2,1)}, u32[]{:S(2)}) copy-start(bf16[1024,2048]{1,0:T(8,128)(2,1)} %copy-done.33) | copy-start | bytes 12582916
  392.0 25.2 %copy-start.28 = (bf16[2,1024,1024]{2,1,0:T(8,128)(2,1)S(1)}, bf16[2,1024,1024]{2,1,0:T(8,128)(2,1)}, u32[]{:S(2)}) copy-start(bf16[2,1024,1024]{2,1,0:T(8,128)(2,1)} %get-tuple-element.49) | copy-start | bytes 12582916
  392.1 23.9 %collective-permute-start.7 = (bf16[2,256,768]{2,1,0:T(8,128)(2,1)S(1)}, bf16[2,256,768]{2,1,0:T(8,128)(2,1)S(1)}, u32[]{:S(2)}, u32[]{:S(2)}) collective-permute-start(bf16[2,256,768]{2,1,0:T(8,128)(2,1)S(1)} %dynamic-slice_bitcast_fusion.5), channel_id=1, source_target_pairs={{0,8},{4,12},{8,0},{12,4},{1,9},{5,13},{9,1},{13,5},{2,10},{6,14},... | collective-permute-start | bytes 2359304 | tf_op jit(solution)/shard_map/ppermute | solution.py:1044
  394.2 22.5 %collective-permute-start.9 = (bf16[2,256,768]{2,1,0:T(8,128)(2,1)S(1)}, bf16[2,256,768]{2,1,0:T(8,128)(2,1)S(1)}, u32[]{:S(2)}, u32[]{:S(2)}) collective-permute-start(bf16[2,256,768]{2,1,0:T(8,128)(2,1)S(1)} %dynamic-slice_bitcast_fusion.4), channel_id=1, source_target_pairs={{0,16},{16,0},{1,17},{17,1},{2,18},{18,2},{3,19},{19,3},{4,20},{20... | collective-permute-start | bytes 2359304 | tf_op jit(solution)/shard_map/ppermute | solution.py:1044
  394.8 21.1 %collective-permute-start.13 = (bf16[256,256]{1,0:T(8,128)(2,1)S(1)}, bf16[256,256]{1,0:T(8,128)(2,1)S(1)}, u32[]{:S(2)}, u32[]{:S(2)}) collective-permute-start(bf16[256,256]{1,0:T(8,128)(2,1)S(1)} %fusion.79), channel_id=1, source_target_pairs={{0,16},{16,0},{1,17},{17,1},{2,18},{18,2},{3,19},{19,3},{4,20},{20... | collective-permute-start | bytes 393224 | tf_op jit(solution)/shard_map/ppermute | solution.py:1044
  416.1 20.7 %collective-permute-start.8 = (bf16[256,768]{1,0:T(8,128)(2,1)S(1)}, bf16[256,768]{1,0:T(8,128)(2,1)S(1)}, u32[]{:S(2)}, u32[]{:S(2)}) collective-permute-start(bf16[256,768]{1,0:T(8,128)(2,1)S(1)} %fusion.70), channel_id=1, source_target_pairs={{0,16},{16,0},{1,17},{17,1},{2,18},{18,2},{3,19},{19,3},{4,20},{20... | collective-permute-start | bytes 1179656 | tf_op jit(solution)/shard_map/ppermute | solution.py:1044
  416.8 21.7 %collective-permute-start.10 = (bf16[256,768]{1,0:T(8,128)(2,1)S(1)}, bf16[256,768]{1,0:T(8,128)(2,1)S(1)}, u32[]{:S(2)}, u32[]{:S(2)}) collective-permute-start(bf16[256,768]{1,0:T(8,128)(2,1)S(1)} %fusion.68), channel_id=1, source_target_pairs={{0,8},{4,12},{8,0},{12,4},{1,9},{5,13},{9,1},{13,5},{2,10},{6,14},... | collective-permute-start | bytes 1179656 | tf_op jit(solution)/shard_map/ppermute | solution.py:1044
  424.6 26.1 %collective-permute-start.24 = (bf16[2,256,1024]{2,1,0:T(8,128)(2,1)S(1)}, bf16[2,256,1024]{2,1,0:T(8,128)(2,1)S(1)}, u32[]{:S(2)}, u32[]{:S(2)}) collective-permute-start(bf16[2,256,1024]{2,1,0:T(8,128)(2,1)S(1)} %dynamic-slice_bitcast_fusion), channel_id=1, source_target_pairs={{0,16},{16,0},{1,17},{17,1},{2,18},{18,2},{3,19},{19,3},{4,20},{20... | collective-permute-start | bytes 3145736 | tf_op jit(solution)/shard_map/ppermute | solution.py:1044
  426.2 26.4 %collective-permute-start.22 = (bf16[2,256,1024]{2,1,0:T(8,128)(2,1)S(1)}, bf16[2,256,1024]{2,1,0:T(8,128)(2,1)S(1)}, u32[]{:S(2)}, u32[]{:S(2)}) collective-permute-start(bf16[2,256,1024]{2,1,0:T(8,128)(2,1)S(1)} %dynamic-slice_bitcast_fusion.1), channel_id=1, source_target_pairs={{0,8},{4,12},{8,0},{12,4},{1,9},{5,13},{9,1},{13,5},{2,10},{6,14},... | collective-permute-start | bytes 3145736 | tf_op jit(solution)/shard_map/ppermute | solution.py:1044
  436.2 36.9 %collective-permute-start.19 = (bf16[2,256,1024]{2,1,0:T(8,128)(2,1)S(1)}, bf16[2,256,1024]{2,1,0:T(8,128)(2,1)S(1)}, u32[]{:S(2)}, u32[]{:S(2)}) collective-permute-start(bf16[2,256,1024]{2,1,0:T(8,128)(2,1)S(1)} %dynamic-slice_bitcast_fusion.2), channel_id=1, source_target_pairs={{0,16},{16,0},{1,17},{17,1},{2,18},{18,2},{3,19},{19,3},{4,20},{20... | collective-permute-start | bytes 3145736 | tf_op jit(solution)/shard_map/ppermute | solution.py:1044
  436.9 38.2 %collective-permute-start.17 = (bf16[2,256,1024]{2,1,0:T(8,128)(2,1)S(1)}, bf16[2,256,1024]{2,1,0:T(8,128)(2,1)S(1)}, u32[]{:S(2)}, u32[]{:S(2)}) collective-permute-start(bf16[2,256,1024]{2,1,0:T(8,128)(2,1)S(1)} %dynamic-slice_bitcast_fusion.3), channel_id=1, source_target_pairs={{0,8},{4,12},{8,0},{12,4},{1,9},{5,13},{9,1},{13,5},{2,10},{6,14},... | collective-permute-start | bytes 3145736 | tf_op jit(solution)/shard_map/ppermute | solution.py:1044
  450.9 35.2 %collective-permute-start.25 = (bf16[256,1024]{1,0:T(8,128)(2,1)S(1)}, bf16[256,1024]{1,0:T(8,128)(2,1)S(1)}, u32[]{:S(2)}, u32[]{:S(2)}) collective-permute-start(bf16[256,1024]{1,0:T(8,128)(2,1)S(1)} %fusion.60), channel_id=1, source_target_pairs={{0,8},{4,12},{8,0},{12,4},{1,9},{5,13},{9,1},{13,5},{2,10},{6,14},... | collective-permute-start | bytes 1572872 | tf_op jit(solution)/shard_map/ppermute | solution.py:1044
  452.8 33.5 %collective-permute-start.23 = (bf16[256,1024]{1,0:T(8,128)(2,1)S(1)}, bf16[256,1024]{1,0:T(8,128)(2,1)S(1)}, u32[]{:S(2)}, u32[]{:S(2)}) collective-permute-start(bf16[256,1024]{1,0:T(8,128)(2,1)S(1)} %fusion.62), channel_id=1, source_target_pairs={{0,16},{16,0},{1,17},{17,1},{2,18},{18,2},{3,19},{19,3},{4,20},{20... | collective-permute-start | bytes 1572872 | tf_op jit(solution)/shard_map/ppermute | solution.py:1044
  473.3 21.0 %collective-permute-start.20 = (bf16[256,1024]{1,0:T(8,128)(2,1)S(1)}, bf16[256,1024]{1,0:T(8,128)(2,1)S(1)}, u32[]{:S(2)}, u32[]{:S(2)}) collective-permute-start(bf16[256,1024]{1,0:T(8,128)(2,1)S(1)} %fusion.64), channel_id=1, source_target_pairs={{0,8},{4,12},{8,0},{12,4},{1,9},{5,13},{9,1},{13,5},{2,10},{6,14},... | collective-permute-start | bytes 1572872 | tf_op jit(solution)/shard_map/ppermute | solution.py:1044
  475.3 19.3 %collective-permute-start.18 = (bf16[256,1024]{1,0:T(8,128)(2,1)S(1)}, bf16[256,1024]{1,0:T(8,128)(2,1)S(1)}, u32[]{:S(2)}, u32[]{:S(2)}) collective-permute-start(bf16[256,1024]{1,0:T(8,128)(2,1)S(1)} %fusion.66), channel_id=1, source_target_pairs={{0,16},{16,0},{1,17},{17,1},{2,18},{18,2},{3,19},{19,3},{4,20},{20... | collective-permute-start | bytes 1572872 | tf_op jit(solution)/shard_map/ppermute | solution.py:1044
  524.0 5.1 collective-permute-start
  524.2 9.2 %collective-permute-start.1 = (bf16[1,256,512]{2,1,0:T(8,128)(2,1)S(1)}, bf16[1,256,512]{2,1,0:T(8,128)(2,1)S(1)}, u32[]{:S(2)}, u32[]{:S(2)}) collective-permute-start(bf16[1,256,512]{2,1,0:T(8,128)(2,1)S(1)} %get-tuple-element.83), channel_id=1, source_target_pairs={{0,8},{4,12},{8,0},{12,4},{1,9},{5,13},{9,1},{13,5},{2,10},{6,14},... | collective-permute-start | bytes 786440 | tf_op jit(solution)/shard_map/ppermute | solution.py:1044
  525.1 12.6 %collective-permute-start.3 = (bf16[1,256,512]{2,1,0:T(8,128)(2,1)S(1)}, bf16[1,256,512]{2,1,0:T(8,128)(2,1)S(1)}, u32[]{:S(2)}, u32[]{:S(2)}) collective-permute-start(bf16[1,256,512]{2,1,0:T(8,128)(2,1)S(1)} %get-tuple-element.81), channel_id=1, source_target_pairs={{0,4},{4,0},{8,12},{12,8},{1,5},{5,1},{9,13},{13,9},{2,6},{6,2},{1... | collective-permute-start | bytes 786440 | tf_op jit(solution)/shard_map/ppermute | solution.py:1044
  526.7 11.1 %collective-permute-start.2 = (bf16[1,256,512]{2,1,0:T(8,128)(2,1)S(1)}, bf16[1,256,512]{2,1,0:T(8,128)(2,1)S(1)}, u32[]{:S(2)}, u32[]{:S(2)}) collective-permute-start(bf16[1,256,512]{2,1,0:T(8,128)(2,1)S(1)} %get-tuple-element.82), channel_id=1, source_target_pairs={{0,12},{4,8},{8,4},{12,0},{1,13},{5,9},{9,5},{13,1},{2,14},{6,10},... | collective-permute-start | bytes 786440 | tf_op jit(solution)/shard_map/ppermute | solution.py:1044
  528.1 16.5 %collective-permute-start.4 = (bf16[1,256,512]{2,1,0:T(8,128)(2,1)S(1)}, bf16[1,256,512]{2,1,0:T(8,128)(2,1)S(1)}, u32[]{:S(2)}, u32[]{:S(2)}) collective-permute-start(bf16[1,256,512]{2,1,0:T(8,128)(2,1)S(1)} %get-tuple-element.80), channel_id=1, source_target_pairs={{0,8},{4,12},{8,0},{12,4},{1,9},{5,13},{9,1},{13,5},{2,10},{6,14},... | collective-permute-start | bytes 786440 | tf_op jit(solution)/shard_map/ppermute | solution.py:1044
  529.0 20.0 %collective-permute-start.5 = (bf16[1,256,512]{2,1,0:T(8,128)(2,1)S(1)}, bf16[1,256,512]{2,1,0:T(8,128)(2,1)S(1)}, u32[]{:S(2)}, u32[]{:S(2)}) collective-permute-start(bf16[1,256,512]{2,1,0:T(8,128)(2,1)S(1)} %get-tuple-element.79), channel_id=1, source_target_pairs={{0,12},{4,8},{8,4},{12,0},{1,13},{5,9},{9,5},{13,1},{2,14},{6,10},... | collective-permute-start | bytes 786440 | tf_op jit(solution)/shard_map/ppermute | solution.py:1044
  (34 other events, 336.8 us)
Sparse Core Ops, SparseCore 0:
  10.5 70.9 all-gather.2
  83.9 89.5 all-gather.4
  338.6 86.0 reduce-scatter.4
  426.9 77.2 reduce-scatter.2

commit v2 on v1

--- a/solution.py
+++ b/solution.py
@@ -6,6 +6,9 @@
 from jax.experimental import pallas as pl
 from jax.experimental.pallas import tpu as pltpu
 from jax.sharding import PartitionSpec as P
+
+
+SHARD, CONTEXT, TENSOR = "shard", "context", "tensor"
 
 D = 2048
 HEADS = 32
@@ -143,7 +146,7 @@
             k_start = k_block * block
 
             def delta_live(delta_in):
-                key_blk, probs, dprobs = pieces(k_start)
+                _, probs, dprobs = pieces(k_start)
                 return delta_in + jnp.sum(probs * dprobs, axis=1)
 
             return lax.cond(
@@ -242,8 +245,8 @@
     hidden_second,
 ):
     sequences, local_len, width_part = inputs.shape
-    n_context = lax.axis_size("context")
-    n_tensor = lax.axis_size("tensor")
+    n_context = lax.axis_size(CONTEXT)
+    n_tensor = lax.axis_size(TENSOR)
     heads_here = HEADS // n_tensor
     tokens_here = sequences * local_len
     length = local_len * n_context
@@ -255,7 +258,7 @@
     starts = ends - doc_lengths
     all_index = jnp.arange(length, dtype=jnp.int32)
     doc_ids = jnp.sum((all_index[None, :, None] >= ends[:, None, :]).astype(jnp.int32), axis=2)
-    local_index = lax.axis_index("context") * local_len + jnp.arange(local_len, dtype=jnp.int32)
+    local_index = lax.axis_index(CONTEXT) * local_len + jnp.arange(local_len, dtype=jnp.int32)
     inside = (local_index[None, :, None] >= starts[:, None, :]) & (
         local_index[None, :, None] < ends[:, None, :]
     )
@@ -267,8 +270,8 @@
     sine = jnp.sin(angle)[:, None]
     norm_low = vectors[0:2].astype(jnp.bfloat16)
     tokens_full, norm_full = (
-        lax.all_gather(inputs, "tensor", axis=2, tiled=True),
-        lax.all_gather(norm_low, "tensor", axis=1, tiled=True),
+        lax.all_gather(inputs, TENSOR, axis=2, tiled=True),
+        lax.all_gather(norm_low, TENSOR, axis=1, tiled=True),
     )
     rows_in = tokens_full.astype(jnp.float32).reshape(tokens_here, D)
     mean_val = jnp.mean(rows_in, axis=1, keepdims=True)
@@ -279,8 +282,8 @@
     gain_full = norm_full[0].astype(jnp.float32)
     normed = (normal * gain_full + norm_full[1].astype(jnp.float32)).astype(jnp.bfloat16)
     attn_full, mlp_full = (
-        lax.all_gather(attn_weights.astype(jnp.bfloat16), ("shard", "context"), axis=1, tiled=True),
-        lax.all_gather(mlp_weights.astype(jnp.bfloat16), ("shard", "context"), axis=1, tiled=True),
+        lax.all_gather(attn_weights.astype(jnp.bfloat16), (SHARD, CONTEXT), axis=1, tiled=True),
+        lax.all_gather(mlp_weights.astype(jnp.bfloat16), (SHARD, CONTEXT), axis=1, tiled=True),
     )
     token_grid = normed.reshape(sequences, local_len, D)
     qkv_weights = attn_full[0:3].reshape(3, D, heads_here, HD)
@@ -298,8 +301,8 @@
         ]
     ).astype(jnp.bfloat16)
     outgoing = outgoing.reshape(3, sequences * heads_here, HD, local_len)
-    attn_in = lax.all_to_all(outgoing, "context", split_axis=1, concat_axis=3, tiled=True)
-    item_index = lax.axis_index("context") * per_device + jnp.arange(per_device, dtype=jnp.int32)
+    attn_in = lax.all_to_all(outgoing, CONTEXT, split_axis=1, concat_axis=3, tiled=True)
+    item_index = lax.axis_index(CONTEXT) * per_device + jnp.arange(per_device, dtype=jnp.int32)
     item_docs = jnp.take(doc_ids, item_index // heads_here, axis=0)
 
     def attend_one(parts):
@@ -307,7 +310,7 @@
         return attend_item(query, key_part, value_part, doc_row, block, scale)
 
     attn_out, lse = lax.map(attend_one, (attn_in[0], attn_in[1], attn_in[2], item_docs))
-    heads_out = lax.all_to_all(attn_out, "context", split_axis=2, concat_axis=0, tiled=True)
+    heads_out = lax.all_to_all(attn_out, CONTEXT, split_axis=2, concat_axis=0, tiled=True)
     heads_grid = heads_out.reshape(sequences, heads_here, HD, local_len)
     out_weights = attn_full[3].reshape(D, heads_here, HD)
     branch = jnp.einsum(
@@ -319,25 +322,25 @@
     branch = branch + jnp.einsum(
         "tf,of->to", hidden, mlp_full[1], preferred_element_type=jnp.float32
     )
-    summed = lax.psum_scatter(branch, "tensor", scatter_dimension=1, tiled=True)
+    summed = lax.psum_scatter(branch, TENSOR, scatter_dimension=1, tiled=True)
     input_rows = inputs.astype(jnp.float32).reshape(tokens_here, width_part)
     output = (
         (input_rows + summed + vectors[5] + vectors[6])
         .astype(jnp.bfloat16)
         .reshape(sequences, local_len, width_part)
     )
-    grad_full = lax.all_gather(cotangent, "tensor", axis=2, tiled=True)
+    grad_full = lax.all_gather(cotangent, TENSOR, axis=2, tiled=True)
     grad_rows = grad_full.reshape(tokens_here, D)
     attn_back, mlp_back = (
-        lax.all_gather(attn_weights.astype(jnp.bfloat16), ("shard", "context"), axis=1, tiled=True),
-        lax.all_gather(mlp_weights.astype(jnp.bfloat16), ("shard", "context"), axis=1, tiled=True),
+        lax.all_gather(attn_weights.astype(jnp.bfloat16), (SHARD, CONTEXT), axis=1, tiled=True),
+        lax.all_gather(mlp_weights.astype(jnp.bfloat16), (SHARD, CONTEXT), axis=1, tiled=True),
     )
     out_back = attn_back[3].reshape(D, heads_here, HD)
     grad_heads = jnp.einsum(
         "sto,ohe->shet", grad_full, out_back, preferred_element_type=jnp.float32
     ).astype(jnp.bfloat16)
     grad_heads = grad_heads.reshape(sequences * heads_here, HD, local_len)
-    grad_items = lax.all_to_all(grad_heads, "context", split_axis=0, concat_axis=2, tiled=True)
+    grad_items = lax.all_to_all(grad_heads, CONTEXT, split_axis=0, concat_axis=2, tiled=True)
 
     def attend_grad(parts):
         query, key_part, value_part, gout, lse_row, doc_row = parts
@@ -348,7 +351,7 @@
     )
     grads_back = lax.all_to_all(
         jnp.stack([grad_query_item, grad_key_item, grad_value_item]),
-        "context",
+        CONTEXT,
         split_axis=3,
         concat_axis=1,
         tiled=True,
@@ -386,8 +389,8 @@
         - normal * jnp.mean(scaled * normal, axis=1, keepdims=True)
     )
     input_slice, norm_slice = (
-        lax.psum_scatter(input_part, "tensor", scatter_dimension=1, tiled=True),
-        lax.psum_scatter(norm_stats, "tensor", scatter_dimension=1, tiled=True),
+        lax.psum_scatter(input_part, TENSOR, scatter_dimension=1, tiled=True),
+        lax.psum_scatter(norm_stats, TENSOR, scatter_dimension=1, tiled=True),
     )
     cot_rows = cotangent.astype(jnp.float32).reshape(tokens_here, width_part)
     input_grad = (
@@ -409,12 +412,12 @@
         ]
     )
     local_hidden = jnp.sum(pre_grad.astype(jnp.float32), axis=0)
-    vector_grad, hidden_grad = lax.psum((local_vectors, local_hidden), ("shard", "context"))
+    vector_grad, hidden_grad = lax.psum((local_vectors, local_hidden), (SHARD, CONTEXT))
     attn_local = jnp.concatenate([qkv_grad, out_grad[None]], axis=0)
     mlp_local = jnp.stack([first_grad, second_grad])
     attn_grad, mlp_grad = (
-        lax.psum_scatter(attn_local, ("shard", "context"), scatter_dimension=1, tiled=True),
-        lax.psum_scatter(mlp_local, ("shard", "context"), scatter_dimension=1, tiled=True),
+        lax.psum_scatter(attn_local, (SHARD, CONTEXT), scatter_dimension=1, tiled=True),
+        lax.psum_scatter(mlp_local, (SHARD, CONTEXT), scatter_dimension=1, tiled=True),
     )
     attn_new, attn_moment_new, attn_second_new = adam_update(
         attn_weights, attn_moment, attn_second, attn_grad
@@ -691,7 +694,7 @@
     rows,
     strip,
 ):
-    c, z = lax.axis_index("context"), lax.axis_index("tensor")
+    c, z = lax.axis_index(CONTEXT), lax.axis_index(TENSOR)
     core = c % 2
     local_len, width = x_ref.shape[1:]
     length = local_len * n_context
@@ -702,10 +705,10 @@
 
     barrier = pltpu.get_barrier_semaphore()
     for k in range(1, n_context):
-        pl.semaphore_signal(barrier, inc=1, device_id={"context": peer(k)}, device_id_type=MESH)
+        pl.semaphore_signal(barrier, inc=1, device_id={CONTEXT: peer(k)}, device_id_type=MESH)
     for k in range(1, n_tensor):
         pl.semaphore_signal(
-            barrier, inc=1, device_id={"tensor": (z + k) % n_tensor}, device_id_type=MESH
+            barrier, inc=1, device_id={TENSOR: (z + k) % n_tensor}, device_id_type=MESH
         )
     pl.semaphore_wait(barrier, n_context + n_tensor - 2)
 
@@ -728,7 +731,7 @@
             dst_ref=piece(f, r, c, z),
             send_sem=send_a.at[f, k - 1, r],
             recv_sem=recv_a.at[f, k - 1, r],
-            device_id={"context": peer(k)},
+            device_id={CONTEXT: peer(k)},
             device_id_type=MESH,
         )
 
@@ -738,7 +741,7 @@
             dst_ref=norm_all.at[z],
             send_sem=send_n.at[k - 1],
             recv_sem=recv_n.at[k - 1],
-            device_id={"tensor": (z + k) % n_tensor},
+            device_id={TENSOR: (z + k) % n_tensor},
             device_id_type=MESH,
         )
 
@@ -751,7 +754,7 @@
             dst_ref=block,
             send_sem=sends.at[f, d - step, k, r],
             recv_sem=recvs.at[f, d - step, k, r],
-            device_id={"tensor": z + side * (1 - step)},
+            device_id={TENSOR: z + side * (1 - step)},
             device_id_type=MESH,
         )
 
@@ -942,21 +945,20 @@
     n_context,
     n_tensor,
 ):
-    y, c, z = lax.axis_index("shard"), lax.axis_index("context"), lax.axis_index("tensor")
+    y, c, z = lax.axis_index(SHARD), lax.axis_index(CONTEXT), lax.axis_index(TENSOR)
     me = y * n_context + c
     group = n_shard * n_context
-    width = out_ref.shape[1]
     kept = stats_ref.shape[1]
 
     barrier = pltpu.get_barrier_semaphore()
     for k in range(1, n_tensor):
         pl.semaphore_signal(
-            barrier, inc=1, device_id={"tensor": (z + k) % n_tensor}, device_id_type=MESH
+            barrier, inc=1, device_id={TENSOR: (z + k) % n_tensor}, device_id_type=MESH
         )
 
     def place(k):
         other = (me + k) % group
-        return {"shard": other // n_context, "context": other % n_context}
+        return {SHARD: other // n_context, CONTEXT: other % n_context}
 
     for k in range(1, group):
         pl.semaphore_signal(barrier, inc=1, device_id=place(k), device_id_type=MESH)
@@ -968,7 +970,7 @@
             dst_ref=parts.at[k],
             send_sem=send_z.at[k],
             recv_sem=recv_z.at[k],
-            device_id={"tensor": (z + k) % n_tensor},
+            device_id={TENSOR: (z + k) % n_tensor},
             device_id_type=MESH,
         )
 
@@ -1040,12 +1042,80 @@
     )(stats, rest)
 
 
+def return_kernel(sum_ref, base_ref, out_ref, mixed, send, recv, own, *, n_context, rows):
+    c = lax.axis_index(CONTEXT)
+    local_len = out_ref.shape[1]
+    length = local_len * n_context
+
+    def peer(k):
+        return flipped(c, k)
+
+    barrier = pltpu.get_barrier_semaphore()
+    for k in range(1, n_context):
+        pl.semaphore_signal(barrier, inc=1, device_id={CONTEXT: peer(k)}, device_id_type=MESH)
+
+    def lines(r, k):
+        return pl.ds(pl.multiple_of(r * length + peer(k) * local_len, local_len), local_len)
+
+    def swap(r, k, place):
+        return pltpu.make_async_remote_copy(
+            src_ref=mixed.at[lines(r, k)],
+            dst_ref=out_ref.at[place * rows + r],
+            send_sem=send.at[k, r],
+            recv_sem=recv.at[k, r],
+            device_id={CONTEXT: peer(k)},
+            device_id_type=MESH,
+        )
+
+    def blend(r, k):
+        at = lines(r, k)
+        mixed[at, :] = (
+            sum_ref[at, :].astype(jnp.float32) + base_ref[at, :].astype(jnp.float32)
+        ).astype(jnp.bfloat16)
+
+    order = [(r, k) for k in range(n_context - 1, -1, -1) for r in range(rows)]
+    for r, k in order:
+        blend(r, k)
+        if (r, k) == order[0]:
+            pl.semaphore_wait(barrier, n_context - 1)
+        if k > 0:
+            swap(r, k, c).start()
+        else:
+            pltpu.make_async_copy(
+                mixed.at[lines(r, 0)], out_ref.at[c * rows + r], own.at[r]
+            ).start()
+    for r, k in order:
+        if k > 0:
+            swap(r, k, peer(k)).wait_recv()
+            swap(r, k, c).wait_send()
+        else:
+            pltpu.make_async_copy(
+                mixed.at[lines(r, 0)], out_ref.at[c * rows + r], own.at[r]
+            ).wait()
+
+
+def return_rows(summed, base, n_context, rows):
+    tokens, width = summed.shape
+    local_len = tokens // (rows * n_context)
+    dma = pltpu.SemaphoreType.DMA
+    inside = pl.BlockSpec(memory_space=pltpu.VMEM)
+    return pl.pallas_call(
+        functools.partial(return_kernel, n_context=n_context, rows=rows),
+        out_shape=jax.ShapeDtypeStruct((n_context * rows, local_len, width), jnp.bfloat16),
+        in_specs=[inside] * 2,
+        out_specs=inside,
+        scratch_shapes=[
+            pltpu.VMEM((tokens, width), jnp.bfloat16),
+            dma((n_context, rows)),
+            dma((n_context, rows)),
+            dma((rows,)),
+        ],
+        compiler_params=pltpu.CompilerParams(collective_id=2, has_side_effects=True),
+    )(summed, base)
+
+
 def permute(field, axis, pairs):
     return lax.ppermute(field, axis, pairs)
-
-
-def ring_shift(field, axis, size, k):
-    return lax.ppermute(field, axis, [(i, (i + k) % size) for i in range(size)])
 
 
 def pick(field, index, axis):
@@ -1070,8 +1140,8 @@
     hidden_second,
 ):
     sequences, local_len, width = inputs.shape
-    n_context, n_tensor = lax.axis_size("context"), lax.axis_size("tensor")
-    n_shard = lax.axis_size("shard")
+    n_context, n_tensor = lax.axis_size(CONTEXT), lax.axis_size(TENSOR)
+    n_shard = lax.axis_size(SHARD)
     rows = sequences // n_context
     length = local_len * n_context
     tokens = rows * length
@@ -1079,24 +1149,19 @@
     half_rot = ROT // 2
     low_type = jnp.bfloat16
     wide = jnp.float32
-    at_tensor, at_context = lax.axis_index("tensor"), lax.axis_index("context")
-    at_y, at_x, at_core = lax.axis_index("shard"), at_context // 2, at_context % 2
+    at_tensor, at_context = lax.axis_index(TENSOR), lax.axis_index(CONTEXT)
+    at_y, at_x = lax.axis_index(SHARD), at_context // 2
     flip_core = [(i, i ^ 1) for i in range(n_context)]
     flip_x = [(i, i ^ 2) for i in range(n_context)]
     flip_y = [(i, i ^ 1) for i in range(n_shard)]
 
-    def after(field, *others):
-        return lax.optimization_barrier((field,) + others)[0]
-
     def dot(a, b, left, right):
-        return lax.dot_general(
-            a, b, (((left,), (right,)), ((), ())), preferred_element_type=wide
-        )
+        return lax.dot_general(a, b, (((left,), (right,)), ((), ())), preferred_element_type=wide)
 
     attn_low = jnp.concatenate([attn_weights[i] for i in range(4)], axis=1).astype(low_type)
-    attn_full = lax.all_gather(attn_low, ("shard", "context"), axis=0, tiled=True)
+    attn_full = lax.all_gather(attn_low, (SHARD, CONTEXT), axis=0, tiled=True)
     mlp_full = lax.all_gather(
-        mlp_weights.astype(low_type), ("shard", "context"), axis=1, tiled=True
+        mlp_weights.astype(low_type), (SHARD, CONTEXT), axis=1, tiled=True
     )
     w_qkv, w_out = attn_full[:, : 3 * width], attn_full[:, 3 * width :]
     w_up, w_down = mlp_full[0], mlp_full[1]
@@ -1141,10 +1206,10 @@
     g_qkv = jnp.concatenate([g_query, g_key, g_value], axis=1)
 
     def scatter_features(field):
-        return lax.psum_scatter(field, "tensor", scatter_dimension=1, tiled=True).astype(wide)
-
-    def own_features(field):
-        return lax.dynamic_slice_in_dim(field, at_tensor * width, width, 1).astype(wide)
+        return lax.psum_scatter(field, TENSOR, scatter_dimension=1, tiled=True)
+
+    def own_features(field, kind):
+        return lax.dynamic_slice_in_dim(field, at_tensor * width, width, 1).astype(kind)
 
     def back_rows(field):
         pieces = field.reshape(rows, n_context, local_len, width)
@@ -1152,44 +1217,58 @@
         for k in range(n_context):
             piece = pick(pieces, at_context ^ k, 1)
             if k > 0:
-                piece = permute(piece, "context", [(i, i ^ k) for i in range(n_context)])
+                piece = permute(piece, CONTEXT, [(i, i ^ k) for i in range(n_context)])
             result = lax.dynamic_update_index_in_dim(result, piece, at_context ^ k, 0)
         return result.reshape(sequences, local_len, width)
 
     branch = (dot(attended, w_out, 1, 1) + dot(hidden, w_down, 1, 1)).astype(low_type)
     summed = scatter_features(branch)
-    output = back_rows(
-        (own_features(x_full) + summed + vectors[5] + vectors[6]).astype(low_type)
-    )
-
-    g_late = after(g_full, branch)
-    pre_grad = gelu_back(dot(g_late, w_down, 1, 0))[0].astype(low_type)
-
-    def reduce_rows(parts, right):
-        mine, other = parts
-        n = right.shape[1]
-        half = n // 2
-        sent = dot(other, right, 0, 0).astype(low_type)
-        chip = (dot(mine, right, 0, 0) + permute(sent, "context", flip_core)).astype(low_type)
-        chip = chip.reshape(n_shard, n_context // 2, -1, n)
-        left, right_part = chip[..., :half], chip[..., half:]
-        from_x = permute(pick(left, 1 - at_x, 1), "context", flip_x)
-        from_y = permute(pick(right_part, 1 - at_y, 0), "shard", flip_y)
-        left, right_part = pick(left, at_x, 1), pick(right_part, at_y, 0)
-
-        def both(a, b, where):
-            return pick(a, where, 0).astype(wide) + pick(b, where, 0).astype(wide)
-
-        next_y = permute(both(left, from_x, 1 - at_y).astype(low_type), "shard", flip_y)
-        next_x = permute(both(right_part, from_y, 1 - at_x).astype(low_type), "context", flip_x)
+
+    pre_grad = gelu_back(dot(g_full, w_down, 1, 0))[0].astype(low_type)
+    local_hidden = jnp.sum(pre_grad.astype(wide), axis=0)
+
+    def both(a, b, where):
+        return pick(a, where, 0).astype(wide) + pick(b, where, 0).astype(wide)
+
+    def core_send(parts, right):
+        return dot(parts[1], right, 0, 0).astype(low_type)
+
+    def chip_send(parts, right, sent):
+        half = right.shape[1] // 2
+        arrived = permute(sent, CONTEXT, flip_core)
+        chip = dot(parts[0], right, 0, 0) + arrived
+        chip = chip.astype(low_type).reshape(n_shard, n_context // 2, -1, right.shape[1])
+        first_half, second_half = chip[..., :half], chip[..., half:]
+        return (
+            pick(first_half, at_x, 1),
+            pick(second_half, at_y, 0),
+            pick(first_half, 1 - at_x, 1),
+            pick(second_half, 1 - at_y, 0),
+        )
+
+    def line_send(chip):
+        kept_x, kept_y, for_x, for_y = chip
+        from_x = permute(for_x, CONTEXT, flip_x)
+        from_y = permute(for_y, SHARD, flip_y)
+        for_y = both(kept_x, from_x, 1 - at_y).astype(low_type)
+        for_x = both(kept_y, from_y, 1 - at_x).astype(low_type)
+        return (kept_x, from_x, kept_y, from_y), for_y, for_x
+
+    def own_rows(line):
+        (kept_x, from_x, kept_y, from_y), for_y, for_x = line
+        next_y = permute(for_y, SHARD, flip_y)
+        next_x = permute(for_x, CONTEXT, flip_x)
         return jnp.concatenate(
-            [both(left, from_x, at_y) + next_y, both(right_part, from_y, at_x) + next_x], axis=1
+            [both(kept_x, from_x, at_y) + next_y, both(kept_y, from_y, at_x) + next_x], axis=1
         )
 
-    down_grad = reduce_rows(after(g_halves, pre_grad), hidden)
-    up_grad = reduce_rows(normed_halves, pre_grad)
-
-    normed_grad = dot(pre_grad, w_up, 1, 1) + dot(g_qkv, w_qkv, 1, 1)
+    down_sent = core_send(g_halves, hidden)
+    up_sent = core_send(normed_halves, pre_grad)
+    qkv_part = dot(g_qkv, w_qkv, 1, 1)
+    down_chip = chip_send(g_halves, hidden, down_sent)
+    up_chip = chip_send(normed_halves, pre_grad, up_sent)
+
+    normed_grad = dot(pre_grad, w_up, 1, 1) + qkv_part
     normal = (x_full.astype(wide) - mean_val) * inv_std
     norm_stats = jnp.stack([jnp.sum(normed_grad * normal, axis=0), jnp.sum(normed_grad, axis=0)])
     scaled = normed_grad * gain_full
@@ -1201,22 +1280,34 @@
             - normal * jnp.mean(scaled * normal, axis=1, keepdims=True)
         )
     ).astype(low_type)
-    g_qkv_late = after(g_qkv, input_part)
-    qkv_grad = reduce_rows(normed_halves, g_qkv_late)
-    out_grad = reduce_rows(g_halves, after(attended, g_qkv_late))
-
     input_slice = scatter_features(input_part)
-    g_own = own_features(g_full)
-    input_grad = back_rows((g_own + input_slice).astype(low_type))
+
+    qkv_sent = core_send(normed_halves, g_qkv)
+    out_sent = core_send(g_halves, attended)
+    qkv_chip = chip_send(normed_halves, g_qkv, qkv_sent)
+    out_chip = chip_send(g_halves, attended, out_sent)
+    output = own_features(x_full, wide) + summed.astype(wide) + vectors[5] + vectors[6]
+    output = output.astype(low_type)
+    output = back_rows(output)
+    down_line = line_send(down_chip)
+    up_line = line_send(up_chip)
+    qkv_line = line_send(qkv_chip)
+    out_line = line_send(out_chip)
+    down_grad, up_grad = own_rows(down_line), own_rows(up_line)
+    qkv_grad, out_grad = own_rows(qkv_line), own_rows(out_line)
+
+    g_own = own_features(g_full, low_type)
+    input_grad = return_rows(input_slice, g_own, n_context, rows)
 
     stats_grid = norm_stats.reshape(2, n_tensor, width).transpose(1, 0, 2)
     rest = jnp.concatenate(
         [
             jnp.sum(g_qkv.astype(wide), axis=0).reshape(3, width),
-            jnp.sum(g_own, axis=0)[None],
-            jnp.sum(pre_grad.astype(wide), axis=0).reshape(-1, width),
+            jnp.sum(own_features(g_full, wide), axis=0)[None],
+            local_hidden.reshape(-1, width),
         ]
     )
+    stats_grid, rest = lax.optimization_barrier((stats_grid, rest))
     totals = total_vectors(stats_grid, rest, n_shard, n_context, n_tensor)
     vector_grad = jnp.concatenate([totals[0:6], totals[5:6]])
     hidden_grad = totals[6:].reshape(-1)
@@ -1259,9 +1350,13 @@
     )
 
 
+def row_local(n_shard, n_context):
+    return n_shard == 2 and n_context == 4
+
+
 def layer(*arrays):
-    sequences, n_context = arrays[0].shape[0], lax.axis_size("context")
-    if sequences % n_context == 0 and n_context == 4 and lax.axis_size("shard") == 2:
+    n_shard, n_context = lax.axis_size(SHARD), lax.axis_size(CONTEXT)
+    if row_local(n_shard, n_context) and arrays[0].shape[0] % n_context == 0:
         return fast_body(*arrays)
     return body(*arrays)
 
@@ -1271,41 +1366,41 @@
         layer,
         mesh=mesh,
         in_specs=(
-            P("shard", "context", "tensor"),
-            P("shard", "context", "tensor"),
-            P("shard", None),
-            P(None, ("shard", "context"), "tensor"),
-            P(None, ("shard", "context"), "tensor"),
-            P(None, "tensor"),
-            P("tensor"),
-            P(None, ("shard", "context"), "tensor"),
-            P(None, ("shard", "context"), "tensor"),
-            P(None, "tensor"),
-            P("tensor"),
-            P(None, ("shard", "context"), "tensor"),
-            P(None, ("shard", "context"), "tensor"),
-            P(None, "tensor"),
-            P("tensor"),
+            P(SHARD, CONTEXT, TENSOR),
+            P(SHARD, CONTEXT, TENSOR),
+            P(SHARD, None),
+            P(None, (SHARD, CONTEXT), TENSOR),
+            P(None, (SHARD, CONTEXT), TENSOR),
+            P(None, TENSOR),
+            P(TENSOR),
+            P(None, (SHARD, CONTEXT), TENSOR),
+            P(None, (SHARD, CONTEXT), TENSOR),
+            P(None, TENSOR),
+            P(TENSOR),
+            P(None, (SHARD, CONTEXT), TENSOR),
+            P(None, (SHARD, CONTEXT), TENSOR),
+            P(None, TENSOR),
+            P(TENSOR),
         ),
         out_specs=(
-            P("shard", "context", "tensor"),
-            P("shard", "context", "tensor"),
-            P(None, ("shard", "context"), "tensor"),
-            P(None, ("shard", "context"), "tensor"),
-            P(None, "tensor"),
-            P("tensor"),
-            P(None, ("shard", "context"), "tensor"),
-            P(None, ("shard", "context"), "tensor"),
-            P(None, "tensor"),
-            P("tensor"),
-            P(None, ("shard", "context"), "tensor"),
-            P(None, ("shard", "context"), "tensor"),
-            P(None, "tensor"),
-            P("tensor"),
-            P(None, ("shard", "context"), "tensor"),
-            P(None, ("shard", "context"), "tensor"),
-            P(None, "tensor"),
-            P("tensor"),
+            P(SHARD, CONTEXT, TENSOR),
+            P(SHARD, CONTEXT, TENSOR),
+            P(None, (SHARD, CONTEXT), TENSOR),
+            P(None, (SHARD, CONTEXT), TENSOR),
+            P(None, TENSOR),
+            P(TENSOR),
+            P(None, (SHARD, CONTEXT), TENSOR),
+            P(None, (SHARD, CONTEXT), TENSOR),
+            P(None, TENSOR),
+            P(TENSOR),
+            P(None, (SHARD, CONTEXT), TENSOR),
+            P(None, (SHARD, CONTEXT), TENSOR),
+            P(None, TENSOR),
+            P(TENSOR),
+            P(None, (SHARD, CONTEXT), TENSOR),
+            P(None, (SHARD, CONTEXT), TENSOR),
+            P(None, TENSOR),
+            P(TENSOR),
         ),
         check_vma=False,
     )

time: 566 us -> 572 us (1.011)
  Pallas kernels: 218 us -> 247 us
  starting transfers between devices: 35.9 us -> 21.2 us
  other arithmetic: 42.5 us -> 53.6 us
  matrix products: 147 us -> 137 us
  waiting for transfers between devices: 81 us -> 73.1 us
    pallas_call x0 -> x1, Pallas kernels: none -> 20.3 us  [return_rows(): pl.pallas_call(functools.partial(return_kernel, n_context=n_context, rows...]
    ppermute x26 -> x23, starting transfers between devices: 35.5 us -> 20.9 us  [permute(): return lax.ppermute(field, axis, pairs)]
    dot_general x16, matrix products: 147 us -> 137 us  [dot(): lax.dot_general(a, b, (((left,), (right,)), ((), ())), preferred_element_...]
    pallas_call x1, Pallas kernels: 43.4 us -> 52.2 us  [attention(): pl.pallas_call(functools.partial(attention_kernel, block=block, steps=ste...]
    ppermute x26 -> x23, waiting for transfers between devices: 80.9 us -> 73 us  [permute(): return lax.ppermute(field, axis, pairs)]
  transfers between devices with their start and end apart: 30 -> 27, of which waited for: 9 -> 9; matrix products, arithmetic and copies ran while one was open for 21% -> 29% of each run, Pallas kernels for 39% -> 44%
where the time goes in v2:
time: 572 us; the launch traced here: 562 us
  Pallas kernels  247 us (43%)
  matrix products  137 us (24%)
  waiting for transfers between devices  73.1 us (13%)
  other arithmetic  53.6 us (9%)
  starting transfers between devices  21.2 us (4%)
  between operations  15.1 us (3%)
  local copies, waits for them, and re-layouts  14.7 us (3%)
    pallas_call x1, Pallas kernels, gather_inputs(): pl.pallas_call(functools.partial(gather_kernel, n_context=n_context, n_te...  164 us
    dot_general x16, matrix products, dot(): lax.dot_general(a, b, (((left,), (right,)), ((), ())), preferred_element_...  137 us
    ppermute x23, waiting for transfers between devices, permute(): return lax.ppermute(field, axis, pairs)  73 us
    pallas_call x1, Pallas kernels, attention(): pl.pallas_call(functools.partial(attention_kernel, block=block, steps=ste...  52.2 us
    ppermute x23, starting transfers between devices, permute(): return lax.ppermute(field, axis, pairs)  20.9 us
    pallas_call x1, Pallas kernels, return_rows(): pl.pallas_call(functools.partial(return_kernel, n_context=n_context, rows...  20.3 us
    sub x4, other arithmetic, adam_update(): weight - learn_rate * (moment_hat / (jnp.sqrt(second_hat) + adam_epsilon)...  15.5 us
  transfers between devices with their start and end apart: 27, of which 9 were waited for; matrix products, arithmetic and copies ran while one was open for 29% of the time, Pallas kernels for 44%

profile of v2, /device:TPU:0, one launch (start us, length us, event | category | flops | bytes accessed | tf_op | source)
XLA Modules:
  0.0 562.1 jit_solution(10295936241001284129)
XLA Ops:
  10.2 3.8 convert_element_type.337
  16.2 163.5 %shard_map.286 = (bf16[1024,2048]{1,0:T(8,128)(2,1)}, bf16[1024,2048]{1,0:T(8,128)(2,1)}, bf16[1024,2048]{1,0:T(8,128)(2,1)}, bf16[2,1024,1024]{2,1,0:T(8,128)(2...) custom-call(bf16[4,256,512]{2,1,0:T(8,128)(2,1)} %x_ref.1, ...), custom_call_target="tpu_custom_call" | custom-call | tf_op jit(solution)/shard_map/pallas_call | solution.py:890
  183.4 3.0 convert_reduce_fusion.2
  187.6 3.2 fusion.71
  190.8 6.3 %fusion.54.gout_ref = bf16[1024,512]{1,0:T(8,128)(2,1)} fusion(bf16[1024,2048]{1,0:T(8,128)(2,1)} %get-tuple-element.34, bf16[2048,2048]{1,0:T(8,128)(2,1)} %all-gather.3.cloned.1.call-done), kind=kOutput, calls=%fused_computation.76 | convolution fusion | flops 2148007936 | bytes 7340032 | tf_op jit(solution)/shard_map/dot_general | solution.py:1159
  197.5 8.6 %fusion.16.q_ref.k_ref.v_ref = f32[1024,1536]{1,0:T(8,128)} fusion(bf16[1024,2048]{1,0:T(8,128)(2,1)S(1)} %copy-done.32, bf16[2048,2048]{1,0:T(8,128)(2,1)S(1)} %copy-done.27, f32[1536]{0:T(1024)S(1)} %add.385), kind=kOutput, calls=%fused_computation.33 | convolution fusion | flops 6444023808 | bytes 16785408 | tf_op jit(solution)/shard_map/dot_general | solution.py:1159
  206.1 52.2 %shard_map.287 = (bf16[1024,512]{1,0:T(8,128)(2,1)}, bf16[1024,512]{1,0:T(8,128)(2,1)}, bf16[1024,512]{1,0:T(8,128)(2,1)}, bf16[1024,512]{1,0:T(8,128)(2,1)}) custom-call(s32[4]{0:T(128)} %fusion.89.first_ref, f32[1024,1536]{1,0:T(8,128)} %fusion.16.q_ref.k_ref.v_ref, f32[1024,1536]{1,0:T(8,128)} %fusion.16.q_ref.k_ref.v_ref, ...), custom_call_target="tpu_custom_call" | custom-call | flops 4294967296 | bytes 15728640 | tf_op jit(solution)/shard_map/pallas_call | solution.py:611
  261.6 3.7 convolution_convert_fusion
  267.3 9.2 %fusion.11 = f32[1024,2048]{1,0:T(8,128)} fusion(bf16[1024,1536]{1,0:T(8,128)(2,1)S(1)} %constant_dynamic-update-slice_fusion.3, bf16[2048,2048]{1,0:T(8,128)(2,1)S(1)} %bitcast.244), kind=kOutput, calls=%fused_computation.28 | convolution fusion | flops 6442450944 | bytes 17825792 | tf_op jit(solution)/shard_map/dot_general | solution.py:1159
  278.0 3.1 collective-permute-start.9
  281.1 3.8 add_convert_fusion.3
  293.3 15.1 %collective-permute-done.12 = bf16[256,256]{1,0:T(8,128)(2,1)} collective-permute-done((bf16[256,256]{1,0:T(8,128)(2,1)S(1)}, bf16[256,256]{1,0:T(8,128)(2,1)}, u32[]{:S(2)}, u32[]{:S(2)}) %collective-permute-start.12) | collective-permute-done | bytes 131104 | tf_op jit(solution)/shard_map/ppermute | solution.py:1118
  315.4 5.2 collective-permute-done.5
  324.2 4.2 multiply_subtract_fusion.1
  328.5 16.7 %multiply_convert_fusion.1 = (bf16[1024,2048]{1,0:T(8,128)(2,1)S(1)}, f32[1024,2048]{1,0:T(8,128)}) fusion(f32[2048]{0:T(1024)S(1)} %copy-done.19, bf16[1024,2048]{1,0:T(8,128)(2,1)} %get-tuple-element.33, bf16[2,2048,2048]{2,1,0:T(8,128)(2,1)} %all-gather.5.cloned.1.call-done), kind=kOutput, calls=%fused_computation.19 | convolution fusion | flops 8610906112 | bytes 25174016 | tf_op jit(solution)/shard_map/dot_general | solution.py:1159
  345.1 11.2 %fusion.10 = f32[1024,2048]{1,0:T(8,128)} fusion(bf16[1024,2048]{1,0:T(8,128)(2,1)S(1)} %get-tuple-element.90, bf16[2,2048,2048]{2,1,0:T(8,128)(2,1)S(1)} %copy-done.26), kind=kOutput, calls=%fused_computation.23 | convolution fusion | flops 8589934592 | bytes 20971520 | tf_op jit(solution)/shard_map/dot_general | solution.py:1159
  356.3 8.4 %add_convert_fusion.2 = bf16[1024,2048]{1,0:T(8,128)(2,1)} fusion(f32[1024,2048]{1,0:T(8,128)} %fusion.10, bf16[1024,512]{1,0:T(8,128)(2,1)S(1)} %copy-done.34, bf16[2048,2048]{1,0:T(8,128)(2,1)} %all-gather.3.cloned.1.call-done), kind=kOutput, calls=%fused_computation.18 | convolution fusion | flops 2151677952 | bytes 15728640 | tf_op jit(solution)/shard_map/dot_general | solution.py:1159
  365.0 9.6 %convolution_convert_fusion.1 = bf16[1024,2048]{1,0:T(8,128)(2,1)} fusion(bf16[1024,2048]{1,0:T(8,128)(2,1)} %copy-done.35, bf16[2,1024,1024]{2,1,0:T(8,128)(2,1)} %get-tuple-element.43), kind=kOutput, calls=%fused_computation.39 | convolution fusion | flops 4297064448 | bytes 10485760 | tf_op jit(solution)/shard_map/dot_general | solution.py:1159
  374.6 17.5 %convert_reduce_fusion = (f32[2048]{0:T(1024)S(1)}, bf16[1024,2048]{1,0:T(8,128)(2,1)S(1)}) fusion(f32[1024,2048]{1,0:T(8,128)} %get-tuple-element.91, f32[2048]{0:T(1024)S(1)} %copy-done.19, bf16[1024,2048]{1,0:T(8,128)(2,1)S(1)} %copy-done.8, bf16[2,2048,2048]{2,1,0:T(8,128)(2,1)} %all-gather.5.cloned.1.call-done), kind=kOutput, calls=%fused_computation.11 | convolution fusion | flops 8638167040 | bytes 25182208 | tf_op jit(solution)/shard_map/dot_general | solution.py:1159
  392.2 6.3 %convolution_convert_fusion.2 = bf16[1024,2048]{1,0:T(8,128)(2,1)} fusion(bf16[1024,2048]{1,0:T(8,128)(2,1)S(1)} %get-tuple-element.94, bf16[2,1024,1024]{2,1,0:T(8,128)(2,1)S(1)} %copy-done.29), kind=kOutput, calls=%fused_computation.40 | convolution fusion | flops 4297064448 | bytes 10485760 | tf_op jit(solution)/shard_map/dot_general | solution.py:1159
  399.1 17.2 %multiply_reduce_fusion = (f32[2048]{0:T(1024)S(1)}, f32[1024]{0:T(1024)S(1)}, f32[1024]{0:T(1024)S(1)}, f32[2048]{0:T(1024)S(1)}, f32[1024,2048]{1,0:T(8,128)S(1)}) fusion(bf16[1024,2048]{1,0:T(8,128)(2,1)} %get-tuple-element.32, f32[1024]{0:T(1024)S(1)} %copy-done.14, f32[1024]{0:T(1024)S(1)} %copy-done.15, f32[2048]{0:T(1024)S(1)} %bitcast.236, ...), kind=kOutput, calls=%fused_computation.12 | convolution fusion | flops 8612997120 | bytes 33595392 | tf_op jit(solution)/shard_map/dot_general | solution.py:1159
  416.4 5.6 %multiply_convert_fusion = bf16[1024,2048]{1,0:T(8,128)(2,1)} fusion(bf16[1024,2048]{1,0:T(8,128)(2,1)} %get-tuple-element.32, f32[1024,2048]{1,0:T(8,128)S(1)} %get-tuple-element.92, f32[1024]{0:T(1024)S(1)} %broadcast_multiply_fusion, f32[1024]{0:T(1024)S(1)} %copy-done.14, f32[1024]{0:T(1024)S(1)} %broadcast_multiply_fusion.1, f32[2048]{0:T(1024)S(1)} %bitcast.237, ...), kind=kLoop, calls=%fused_computation.15 | loop fusion | flops 18874368 | bytes 16801792 | tf_op jit(solution)/shard_map/convert_element_type | solution.py:1282
  423.3 11.3 %shard_map.289 = f32[10,512]{1,0:T(8,128)} custom-call(f32[4,2,512]{2,1,0:T(2,128)} %maximum_bitcast_fusion.3.stats_ref, f32[8,512]{1,0:T(8,128)} %pad_maximum_fusion.4.rest_ref), custom_call_target="tpu_custom_call" | custom-call | tf_op jit(solution)/shard_map/pallas_call | solution.py:1026
  435.3 8.6 %add_convert_fusion = bf16[1024,2048]{1,0:T(8,128)(2,1)S(1)} fusion(bf16[1024,2048]{1,0:T(8,128)(2,1)} %collective-permute-done.18, bf16[1024,2048]{1,0:T(8,128)(2,1)} %copy-done.35, bf16[2,1024,1024]{2,1,0:T(8,128)(2,1)} %get-tuple-element.43), kind=kOutput, calls=%fused_computation.13 | convolution fusion | flops 4301258752 | bytes 14680064 | tf_op jit(solution)/shard_map/dot_general | solution.py:1159
  447.6 7.3 %add_convert_fusion.1 = bf16[1024,2048]{1,0:T(8,128)(2,1)S(1)} fusion(bf16[1024,2048]{1,0:T(8,128)(2,1)} %collective-permute-done.13, bf16[1024,2048]{1,0:T(8,128)(2,1)S(1)} %copy-done.37, bf16[2,1024,1024]{2,1,0:T(8,128)(2,1)S(1)} %copy-done.30), kind=kOutput, calls=%fused_computation.14 | convolution fusion | flops 4301258752 | bytes 14680064 | tf_op jit(solution)/shard_map/dot_general | solution.py:1159
  458.0 12.8 %collective-permute-done.21 = bf16[2,256,1024]{2,1,0:T(8,128)(2,1)S(1)} collective-permute-done((bf16[2,256,1024]{2,1,0:T(8,128)(2,1)S(1)}, bf16[2,256,1024]{2,1,0:T(8,128)(2,1)S(1)}, u32[]{:S(2)}, u32[]{:S(2)}) %collective-permute-start.21) | collective-permute-done | bytes 1048608 | tf_op jit(solution)/shard_map/ppermute | solution.py:1118
  474.0 19.2 %collective-permute-done.16 = bf16[2,256,1024]{2,1,0:T(8,128)(2,1)S(1)} collective-permute-done((bf16[2,256,1024]{2,1,0:T(8,128)(2,1)S(1)}, bf16[2,256,1024]{2,1,0:T(8,128)(2,1)S(1)}, u32[]{:S(2)}, u32[]{:S(2)}) %collective-permute-start.16) | collective-permute-done | bytes 1048608 | tf_op jit(solution)/shard_map/ppermute | solution.py:1118
  495.9 9.5 %collective-permute-done.22 = bf16[256,1024]{1,0:T(8,128)(2,1)S(1)} collective-permute-done((bf16[256,1024]{1,0:T(8,128)(2,1)S(1)}, bf16[256,1024]{1,0:T(8,128)(2,1)S(1)}, u32[]{:S(2)}, u32[]{:S(2)}) %collective-permute-start.22) | collective-permute-done | bytes 524320 | tf_op jit(solution)/shard_map/ppermute | solution.py:1118
  506.0 9.6 %collective-permute-done.17 = bf16[256,1024]{1,0:T(8,128)(2,1)S(1)} collective-permute-done((bf16[256,1024]{1,0:T(8,128)(2,1)S(1)}, bf16[256,1024]{1,0:T(8,128)(2,1)S(1)}, u32[]{:S(2)}, u32[]{:S(2)}) %collective-permute-start.17) | collective-permute-done | bytes 524320 | tf_op jit(solution)/shard_map/ppermute | solution.py:1118
  521.4 10.0 %multiply_subtract_fusion = (f32[2,256,2048]{2,1,0:T(8,128)}, f32[2,256,2048]{2,1,0:T(8,128)}, f32[2,256,2048]{2,1,0:T(8,128)}, f32[2,256,2048]{2,1,0:T(8,128)}) fusion(f32[2,256,2048]{2,1,0:T(8,128)S(1)} %copy-done, f32[2,256,2048]{2,1,0:T(8,128)} %param.23, f32[2,256,2048]{2,1,0:T(8,128)} %param.27, f32[1,256,2048]{2,1,0:T(8,128)S(1)} %maximum_bitcast_fusion.1, ...), kind=kLoop, calls=%fused_computation.36 | loop fusion | flops 16777216 | bytes 33554432 | tf_op jit(solution)/shard_map/sub | solution.py:224
  532.1 20.3 %shard_map.288 = bf16[4,256,512]{2,1,0:T(8,128)(2,1)} custom-call(bf16[1024,512]{1,0:T(8,128)(2,1)} %reduce-scatter.5.cloned.1.call-done.sum_ref, bf16[1024,512]{1,0:T(8,128)(2,1)} %get-tuple-element.66.base_ref), custom_call_target="tpu_custom_call" | custom-call | tf_op jit(solution)/shard_map/pallas_call | solution.py:1102
  552.5 2.6 copy.43
  (209 shorter events, 58.2 us)
Async XLA Ops:
  7.2 183.6 %all-gather.3.cloned.1.call-start = ((), (), s32[]{:S(2)}) async-start(), calls=%async_computation.2 | async-start | bytes 9437184 | tf_op jit(solution)/shard_map/all_gather | solution.py:1162
  10.2 318.3 %all-gather.5.cloned.1.call-start = ((), (), s32[]{:S(2)}) async-start(), calls=%async_computation.3 | async-start | bytes 18874368 | tf_op jit(solution)/shard_map/all_gather | solution.py:1163
  14.1 503.7 %reduce-scatter.3.cloned.1.call-start = ((), (), s32[]{:S(2)}) async-start(), calls=%async_computation.4 | async-start | bytes 5242880 | tf_op jit(solution)/shard_map/reduce_scatter | solution.py:1209
  265.3 15.7 %collective-permute-start.3 = (bf16[1024,1536]{1,0:T(8,128)(2,1)S(1)}, bf16[1024,1536]{1,0:T(8,128)(2,1)S(1)}, u32[]{:S(2)}, u32[]{:S(2)}) collective-permute-start(bf16[1024,1536]{1,0:T(8,128)(2,1)S(1)} %convolution_convert_fusion), channel_id=1, source_target_pairs={{0,4},{4,0},{8,12},{12,8},{1,5},{5,1},{9,13},{13,9},{2,6},{6,2},{1... | collective-permute-start | bytes 9437192 | tf_op jit(solution)/shard_map/ppermute | solution.py:1118
  266.7 9.8 %collective-permute-start.8 = (bf16[1024,512]{1,0:T(8,128)(2,1)S(1)}, bf16[1024,512]{1,0:T(8,128)(2,1)S(1)}, u32[]{:S(2)}, u32[]{:S(2)}) collective-permute-start(bf16[1024,512]{1,0:T(8,128)(2,1)S(1)} %fusion.51), channel_id=1, source_target_pairs={{0,4},{4,0},{8,12},{12,8},{1,5},{5,1},{9,13},{13,9},{2,6},{6,2},{1... | collective-permute-start | bytes 3145736 | tf_op jit(solution)/shard_map/ppermute | solution.py:1118
  277.9 11.1 %collective-permute-start.11 = (bf16[2,256,256]{2,1,0:T(8,128)(2,1)S(1)}, bf16[2,256,256]{2,1,0:T(8,128)(2,1)S(1)}, u32[]{:S(2)}, u32[]{:S(2)}) collective-permute-start(bf16[2,256,256]{2,1,0:T(8,128)(2,1)S(1)} %dynamic-slice_bitcast_fusion.6), channel_id=1, source_target_pairs={{0,16},{16,0},{1,17},{17,1},{2,18},{18,2},{3,19},{19,3},{4,20},{20... | collective-permute-start | bytes 786440 | tf_op jit(solution)/shard_map/ppermute | solution.py:1118
  278.0 14.2 %collective-permute-start.9 = (bf16[2,256,256]{2,1,0:T(8,128)(2,1)S(1)}, bf16[2,256,256]{2,1,0:T(8,128)(2,1)}, u32[]{:S(2)}, u32[]{:S(2)}) collective-permute-start(bf16[2,256,256]{2,1,0:T(8,128)(2,1)S(1)} %dynamic-slice_bitcast_fusion.7), channel_id=1, source_target_pairs={{0,8},{4,12},{8,0},{12,4},{1,9},{5,13},{9,1},{13,5},{2,10},{6,14},... | collective-permute-start | bytes 786440 | tf_op jit(solution)/shard_map/ppermute | solution.py:1118
  286.0 23.4 %collective-permute-start.4 = (bf16[2,256,768]{2,1,0:T(8,128)(2,1)}, bf16[2,256,768]{2,1,0:T(8,128)(2,1)}, u32[]{:S(2)}, u32[]{:S(2)}) collective-permute-start(bf16[2,256,768]{2,1,0:T(8,128)(2,1)} %dynamic-slice_bitcast_fusion.5), channel_id=1, source_target_pairs={{0,8},{4,12},{8,0},{12,4},{1,9},{5,13},{9,1},{13,5},{2,10},{6,14},... | collective-permute-start | bytes 2359304 | tf_op jit(solution)/shard_map/ppermute | solution.py:1118
  287.5 24.8 %collective-permute-start.6 = (bf16[2,256,768]{2,1,0:T(8,128)(2,1)}, bf16[2,256,768]{2,1,0:T(8,128)(2,1)}, u32[]{:S(2)}, u32[]{:S(2)}) collective-permute-start(bf16[2,256,768]{2,1,0:T(8,128)(2,1)} %dynamic-slice_bitcast_fusion.4), channel_id=1, source_target_pairs={{0,16},{16,0},{1,17},{17,1},{2,18},{18,2},{3,19},{19,3},{4,20},{20... | collective-permute-start | bytes 2359304 | tf_op jit(solution)/shard_map/ppermute | solution.py:1118
  289.7 18.7 %collective-permute-start.12 = (bf16[256,256]{1,0:T(8,128)(2,1)S(1)}, bf16[256,256]{1,0:T(8,128)(2,1)}, u32[]{:S(2)}, u32[]{:S(2)}) collective-permute-start(bf16[256,256]{1,0:T(8,128)(2,1)S(1)} %fusion.76), channel_id=1, source_target_pairs={{0,8},{4,12},{8,0},{12,4},{1,9},{5,13},{9,1},{13,5},{2,10},{6,14},... | collective-permute-start | bytes 393224 | tf_op jit(solution)/shard_map/ppermute | solution.py:1118
  293.2 21.0 %collective-permute-start.10 = (bf16[256,256]{1,0:T(8,128)(2,1)S(1)}, bf16[256,256]{1,0:T(8,128)(2,1)S(1)}, u32[]{:S(2)}, u32[]{:S(2)}) collective-permute-start(bf16[256,256]{1,0:T(8,128)(2,1)S(1)} %fusion.78), channel_id=1, source_target_pairs={{0,16},{16,0},{1,17},{17,1},{2,18},{18,2},{3,19},{19,3},{4,20},{20... | collective-permute-start | bytes 393224 | tf_op jit(solution)/shard_map/ppermute | solution.py:1118
  310.6 10.0 %collective-permute-start.5 = (bf16[256,768]{1,0:T(8,128)(2,1)S(1)}, bf16[256,768]{1,0:T(8,128)(2,1)S(1)}, u32[]{:S(2)}, u32[]{:S(2)}) collective-permute-start(bf16[256,768]{1,0:T(8,128)(2,1)S(1)} %fusion.69), channel_id=1, source_target_pairs={{0,16},{16,0},{1,17},{17,1},{2,18},{18,2},{3,19},{19,3},{4,20},{20... | collective-permute-start | bytes 1179656 | tf_op jit(solution)/shard_map/ppermute | solution.py:1118
  313.4 9.4 %collective-permute-start.7 = (bf16[256,768]{1,0:T(8,128)(2,1)S(1)}, bf16[256,768]{1,0:T(8,128)(2,1)S(1)}, u32[]{:S(2)}, u32[]{:S(2)}) collective-permute-start(bf16[256,768]{1,0:T(8,128)(2,1)S(1)} %fusion.67), channel_id=1, source_target_pairs={{0,8},{4,12},{8,0},{12,4},{1,9},{5,13},{9,1},{13,5},{2,10},{6,14},... | collective-permute-start | bytes 1179656 | tf_op jit(solution)/shard_map/ppermute | solution.py:1118
  328.5 16.7 %copy-start.26 = (bf16[2,2048,2048]{2,1,0:T(8,128)(2,1)S(1)}, bf16[2,2048,2048]{2,1,0:T(8,128)(2,1)}, u32[]{:S(2)}) copy-start(bf16[2,2048,2048]{2,1,0:T(8,128)(2,1)} %all-gather.5.cloned.1.call-done) | copy-start | bytes 50331652
  364.8 167.3 %reduce-scatter.5.cloned.1.call-start = ((), (), s32[]{:S(2)}) async-start(), calls=%async_computation.5 | async-start | bytes 5242880 | tf_op jit(solution)/shard_map/reduce_scatter | solution.py:1209
  374.6 60.7 %collective-permute-start.18 = (bf16[1024,2048]{1,0:T(8,128)(2,1)}, bf16[1024,2048]{1,0:T(8,128)(2,1)}, u32[]{:S(2)}, u32[]{:S(2)}) collective-permute-start(bf16[1024,2048]{1,0:T(8,128)(2,1)} %convolution_convert_fusion.1), channel_id=1, source_target_pairs={{0,4},{4,0},{8,12},{12,8},{1,5},{5,1},{9,13},{13,9},{2,6},{6,2},{1... | collective-permute-start | bytes 12582920 | tf_op jit(solution)/shard_map/ppermute | solution.py:1118
  374.6 17.5 %copy-start.29 = (bf16[2,1024,1024]{2,1,0:T(8,128)(2,1)S(1)}, bf16[2,1024,1024]{2,1,0:T(8,128)(2,1)}, u32[]{:S(2)}) copy-start(bf16[2,1024,1024]{2,1,0:T(8,128)(2,1)} %get-tuple-element.42) | copy-start | bytes 12582916
  398.5 48.5 %collective-permute-start.13 = (bf16[1024,2048]{1,0:T(8,128)(2,1)}, bf16[1024,2048]{1,0:T(8,128)(2,1)}, u32[]{:S(2)}, u32[]{:S(2)}) collective-permute-start(bf16[1024,2048]{1,0:T(8,128)(2,1)} %convolution_convert_fusion.2), channel_id=1, source_target_pairs={{0,4},{4,0},{8,12},{12,8},{1,5},{5,1},{9,13},{13,9},{2,6},{6,2},{1... | collective-permute-start | bytes 12582920 | tf_op jit(solution)/shard_map/ppermute | solution.py:1118
  444.7 26.1 %collective-permute-start.21 = (bf16[2,256,1024]{2,1,0:T(8,128)(2,1)S(1)}, bf16[2,256,1024]{2,1,0:T(8,128)(2,1)S(1)}, u32[]{:S(2)}, u32[]{:S(2)}) collective-permute-start(bf16[2,256,1024]{2,1,0:T(8,128)(2,1)S(1)} %dynamic-slice_bitcast_fusion), channel_id=1, source_target_pairs={{0,16},{16,0},{1,17},{17,1},{2,18},{18,2},{3,19},{19,3},{4,20},{20... | collective-permute-start | bytes 3145736 | tf_op jit(solution)/shard_map/ppermute | solution.py:1118
  445.6 26.1 %collective-permute-start.19 = (bf16[2,256,1024]{2,1,0:T(8,128)(2,1)S(1)}, bf16[2,256,1024]{2,1,0:T(8,128)(2,1)S(1)}, u32[]{:S(2)}, u32[]{:S(2)}) collective-permute-start(bf16[2,256,1024]{2,1,0:T(8,128)(2,1)S(1)} %dynamic-slice_bitcast_fusion.1), channel_id=1, source_target_pairs={{0,8},{4,12},{8,0},{12,4},{1,9},{5,13},{9,1},{13,5},{2,10},{6,14},... | collective-permute-start | bytes 3145736 | tf_op jit(solution)/shard_map/ppermute | solution.py:1118
  455.5 17.9 %copy-start.20 = (f32[2048]{0:T(1024)S(1)}, f32[2048]{0:T(1024)}, u32[]{:S(2)}) copy-start(f32[2048]{0:T(1024)} %param.25) | copy-start | bytes 24580
  455.5 17.9 %copy-start.21 = (f32[2048]{0:T(1024)S(1)}, f32[2048]{0:T(1024)}, u32[]{:S(2)}) copy-start(f32[2048]{0:T(1024)} %param.29) | copy-start | bytes 24580
  455.6 37.7 %collective-permute-start.16 = (bf16[2,256,1024]{2,1,0:T(8,128)(2,1)S(1)}, bf16[2,256,1024]{2,1,0:T(8,128)(2,1)S(1)}, u32[]{:S(2)}, u32[]{:S(2)}) collective-permute-start(bf16[2,256,1024]{2,1,0:T(8,128)(2,1)S(1)} %dynamic-slice_bitcast_fusion.2), channel_id=1, source_target_pairs={{0,16},{16,0},{1,17},{17,1},{2,18},{18,2},{3,19},{19,3},{4,20},{20... | collective-permute-start | bytes 3145736 | tf_op jit(solution)/shard_map/ppermute | solution.py:1118
  455.9 38.3 %collective-permute-start.14 = (bf16[2,256,1024]{2,1,0:T(8,128)(2,1)S(1)}, bf16[2,256,1024]{2,1,0:T(8,128)(2,1)S(1)}, u32[]{:S(2)}, u32[]{:S(2)}) collective-permute-start(bf16[2,256,1024]{2,1,0:T(8,128)(2,1)S(1)} %dynamic-slice_bitcast_fusion.3), channel_id=1, source_target_pairs={{0,8},{4,12},{8,0},{12,4},{1,9},{5,13},{9,1},{13,5},{2,10},{6,14},... | collective-permute-start | bytes 3145736 | tf_op jit(solution)/shard_map/ppermute | solution.py:1118
  457.4 48.3 %copy-start.13 = (f32[1,4,4,128]{3,1,2,0:T(4,128)}, f32[1,4,4,128]{3,1,2,0:T(4,128)S(1)}, u32[]{:S(2)}) copy-start(f32[1,4,4,128]{3,1,2,0:T(4,128)S(1)} %copy.35) | copy-start | bytes 24580
  471.0 34.4 %collective-permute-start.22 = (bf16[256,1024]{1,0:T(8,128)(2,1)S(1)}, bf16[256,1024]{1,0:T(8,128)(2,1)S(1)}, u32[]{:S(2)}, u32[]{:S(2)}) collective-permute-start(bf16[256,1024]{1,0:T(8,128)(2,1)S(1)} %fusion.59), channel_id=1, source_target_pairs={{0,8},{4,12},{8,0},{12,4},{1,9},{5,13},{9,1},{13,5},{2,10},{6,14},... | collective-permute-start | bytes 1572872 | tf_op jit(solution)/shard_map/ppermute | solution.py:1118
  471.9 33.8 %collective-permute-start.20 = (bf16[256,1024]{1,0:T(8,128)(2,1)S(1)}, bf16[256,1024]{1,0:T(8,128)(2,1)S(1)}, u32[]{:S(2)}, u32[]{:S(2)}) collective-permute-start(bf16[256,1024]{1,0:T(8,128)(2,1)S(1)} %fusion.61), channel_id=1, source_target_pairs={{0,16},{16,0},{1,17},{17,1},{2,18},{18,2},{3,19},{19,3},{4,20},{20... | collective-permute-start | bytes 1572872 | tf_op jit(solution)/shard_map/ppermute | solution.py:1118
  493.5 22.1 %collective-permute-start.17 = (bf16[256,1024]{1,0:T(8,128)(2,1)S(1)}, bf16[256,1024]{1,0:T(8,128)(2,1)S(1)}, u32[]{:S(2)}, u32[]{:S(2)}) collective-permute-start(bf16[256,1024]{1,0:T(8,128)(2,1)S(1)} %fusion.63), channel_id=1, source_target_pairs={{0,8},{4,12},{8,0},{12,4},{1,9},{5,13},{9,1},{13,5},{2,10},{6,14},... | collective-permute-start | bytes 1572872 | tf_op jit(solution)/shard_map/ppermute | solution.py:1118
  494.4 21.5 %collective-permute-start.15 = (bf16[256,1024]{1,0:T(8,128)(2,1)S(1)}, bf16[256,1024]{1,0:T(8,128)(2,1)S(1)}, u32[]{:S(2)}, u32[]{:S(2)}) collective-permute-start(bf16[256,1024]{1,0:T(8,128)(2,1)S(1)} %fusion.65), channel_id=1, source_target_pairs={{0,16},{16,0},{1,17},{17,1},{2,18},{18,2},{3,19},{19,3},{4,20},{20... | collective-permute-start | bytes 1572872 | tf_op jit(solution)/shard_map/ppermute | solution.py:1118
  520.0 32.4 %collective-permute-start = (bf16[1,256,512]{2,1,0:T(8,128)(2,1)S(1)}, bf16[1,256,512]{2,1,0:T(8,128)(2,1)S(1)}, u32[]{:S(2)}, u32[]{:S(2)}) collective-permute-start(bf16[1,256,512]{2,1,0:T(8,128)(2,1)S(1)} %get-tuple-element.77), channel_id=1, source_target_pairs={{0,4},{4,0},{8,12},{12,8},{1,5},{5,1},{9,13},{13,9},{2,6},{6,2},{1... | collective-permute-start | bytes 786440 | tf_op jit(solution)/shard_map/ppermute | solution.py:1118
  520.1 32.3 %collective-permute-start.1 = (bf16[1,256,512]{2,1,0:T(8,128)(2,1)S(1)}, bf16[1,256,512]{2,1,0:T(8,128)(2,1)S(1)}, u32[]{:S(2)}, u32[]{:S(2)}) collective-permute-start(bf16[1,256,512]{2,1,0:T(8,128)(2,1)S(1)} %get-tuple-element.76), channel_id=1, source_target_pairs={{0,8},{4,12},{8,0},{12,4},{1,9},{5,13},{9,1},{13,5},{2,10},{6,14},... | collective-permute-start | bytes 786440 | tf_op jit(solution)/shard_map/ppermute | solution.py:1118
  531.4 21.0 %collective-permute-start.2 = (bf16[1,256,512]{2,1,0:T(8,128)(2,1)S(1)}, bf16[1,256,512]{2,1,0:T(8,128)(2,1)S(1)}, u32[]{:S(2)}, u32[]{:S(2)}) collective-permute-start(bf16[1,256,512]{2,1,0:T(8,128)(2,1)S(1)} %get-tuple-element.75), channel_id=1, source_target_pairs={{0,12},{4,8},{8,4},{12,0},{1,13},{5,9},{9,5},{13,1},{2,14},{6,10},... | collective-permute-start | bytes 786440 | tf_op jit(solution)/shard_map/ppermute | solution.py:1118
  (36 other events, 178.2 us)
Sparse Core Ops, SparseCore 0:
  10.5 70.9 all-gather.2
  83.9 89.5 all-gather.4
  364.9 74.8 reduce-scatter.2
  442.0 77.2 reduce-scatter.4

commit v3 on v2

--- a/solution.py
+++ b/solution.py
@@ -833,26 +833,32 @@
         ]
 
     order = [(f, r, k) for f in range(2) for k in range(n_context) for r in range(rows)]
-    for f, r, k in order:
-        for d in range(n_tensor):
-            if d == 0:
-                if k == 0:
-                    own_copy(f, r).wait()
-                else:
-                    swap(f, r, k).wait_recv()
-            for side in (1, -1):
-                if d > 0:
-
-                    @pl.when(has(d, side))
-                    def _():
-                        hop(f, r, k, d, side, 1).wait_recv()
-
-                if d < n_tensor - 1:
-
-                    @pl.when(has(d, side) & more(side))
-                    def _():
-                        hop(f, r, k, d, side, 0).start()
-
+
+    def advance(f, r, k, d):
+        if d == 0:
+            if k == 0:
+                own_copy(f, r).wait()
+            else:
+                swap(f, r, k).wait_recv()
+        for side in (1, -1):
+            if d > 0:
+
+                @pl.when(has(d, side))
+                def _():
+                    hop(f, r, k, d, side, 1).wait_recv()
+
+            if d < n_tensor - 1:
+
+                @pl.when(has(d, side) & more(side))
+                def _():
+                    hop(f, r, k, d, side, 0).start()
+
+    advance(*order[0], 0)
+    for i, (f, r, k) in enumerate(order):
+        if i + 1 < len(order):
+            advance(*order[i + 1], 0)
+        for d in range(1, n_tensor):
+            advance(f, r, k, d)
         base = r * length + peer(k) * local_len
         if f == 0:
             finish_x(base)

time: 572 us -> 556 us (0.972)
  Pallas kernels: 247 us -> 232 us
    pallas_call x1, Pallas kernels: 164 us -> 149 us  [gather_inputs(): pl.pallas_call(functools.partial(gather_kernel, n_context=n_context, n_te...]
  transfers between devices with their start and end apart: 27 -> 27, of which waited for: 9 -> 7; matrix products, arithmetic and copies ran while one was open for 29% -> 29% of each run, Pallas kernels for 44% -> 43%
where the time goes in v3:
time: 556 us; the launch traced here: 546 us
  Pallas kernels  232 us (42%)
  matrix products  137 us (25%)
  waiting for transfers between devices  72 us (13%)
  other arithmetic  53.5 us (10%)
  starting transfers between devices  22.6 us (4%)
  between operations  15.1 us (3%)
  local copies, waits for them, and re-layouts  14.2 us (3%)
    pallas_call x1, Pallas kernels, gather_inputs(): pl.pallas_call(functools.partial(gather_kernel, n_context=n_context, n_te...  149 us
    dot_general x16, matrix products, dot(): lax.dot_general(a, b, (((left,), (right,)), ((), ())), preferred_element_...  137 us
    ppermute x23, waiting for transfers between devices, permute(): return lax.ppermute(field, axis, pairs)  71.9 us
    pallas_call x1, Pallas kernels, attention(): pl.pallas_call(functools.partial(attention_kernel, block=block, steps=ste...  52.2 us
    ppermute x23, starting transfers between devices, permute(): return lax.ppermute(field, axis, pairs)  22.3 us
    pallas_call x1, Pallas kernels, return_rows(): pl.pallas_call(functools.partial(return_kernel, n_context=n_context, rows...  20.3 us
    sub x4, other arithmetic, adam_update(): weight - learn_rate * (moment_hat / (jnp.sqrt(second_hat) + adam_epsilon)...  15.5 us
  transfers between devices with their start and end apart: 27, of which 7 were waited for; matrix products, arithmetic and copies ran while one was open for 29% of the time, Pallas kernels for 43%

profile of v3, /device:TPU:0, one launch (start us, length us, event | category | flops | bytes accessed | tf_op | source)
XLA Modules:
  0.0 546.4 jit_solution(10803959248797201544)
XLA Ops:
  10.2 3.8 convert_element_type.337
  16.2 149.0 %shard_map.286 = (bf16[1024,2048]{1,0:T(8,128)(2,1)}, bf16[1024,2048]{1,0:T(8,128)(2,1)}, bf16[1024,2048]{1,0:T(8,128)(2,1)}, bf16[2,1024,1024]{2,1,0:T(8,128)(2...) custom-call(bf16[4,256,512]{2,1,0:T(8,128)(2,1)} %x_ref.1, ...), custom_call_target="tpu_custom_call" | custom-call | tf_op jit(solution)/shard_map/pallas_call | solution.py:896
  168.9 3.0 convert_reduce_fusion.2
  173.1 3.2 fusion.71
  176.2 6.3 %fusion.54.gout_ref = bf16[1024,512]{1,0:T(8,128)(2,1)} fusion(bf16[1024,2048]{1,0:T(8,128)(2,1)} %get-tuple-element.34, bf16[2048,2048]{1,0:T(8,128)(2,1)} %all-gather.3.cloned.1.call-done), kind=kOutput, calls=%fused_computation.76 | convolution fusion | flops 2148007936 | bytes 7340032 | tf_op jit(solution)/shard_map/dot_general | solution.py:1165
  183.0 8.6 %fusion.16.q_ref.k_ref.v_ref = f32[1024,1536]{1,0:T(8,128)} fusion(bf16[1024,2048]{1,0:T(8,128)(2,1)S(1)} %copy-done.32, bf16[2048,2048]{1,0:T(8,128)(2,1)S(1)} %copy-done.27, f32[1536]{0:T(1024)S(1)} %add.385), kind=kOutput, calls=%fused_computation.33 | convolution fusion | flops 6444023808 | bytes 16785408 | tf_op jit(solution)/shard_map/dot_general | solution.py:1165
  191.6 52.2 %shard_map.287 = (bf16[1024,512]{1,0:T(8,128)(2,1)}, bf16[1024,512]{1,0:T(8,128)(2,1)}, bf16[1024,512]{1,0:T(8,128)(2,1)}, bf16[1024,512]{1,0:T(8,128)(2,1)}) custom-call(s32[4]{0:T(128)} %fusion.89.first_ref, f32[1024,1536]{1,0:T(8,128)} %fusion.16.q_ref.k_ref.v_ref, f32[1024,1536]{1,0:T(8,128)} %fusion.16.q_ref.k_ref.v_ref, ...), custom_call_target="tpu_custom_call" | custom-call | flops 4294967296 | bytes 15728640 | tf_op jit(solution)/shard_map/pallas_call | solution.py:611
  247.1 3.7 convolution_convert_fusion
  252.8 9.2 %fusion.11 = f32[1024,2048]{1,0:T(8,128)} fusion(bf16[1024,1536]{1,0:T(8,128)(2,1)S(1)} %constant_dynamic-update-slice_fusion.3, bf16[2048,2048]{1,0:T(8,128)(2,1)S(1)} %bitcast.244), kind=kOutput, calls=%fused_computation.28 | convolution fusion | flops 6442450944 | bytes 17825792 | tf_op jit(solution)/shard_map/dot_general | solution.py:1165
  265.2 3.8 add_convert_fusion.3
  277.4 15.1 %collective-permute-done.12 = bf16[256,256]{1,0:T(8,128)(2,1)} collective-permute-done((bf16[256,256]{1,0:T(8,128)(2,1)S(1)}, bf16[256,256]{1,0:T(8,128)(2,1)}, u32[]{:S(2)}, u32[]{:S(2)}) %collective-permute-start.12) | collective-permute-done | bytes 131104 | tf_op jit(solution)/shard_map/ppermute | solution.py:1124
  299.4 5.2 collective-permute-done.5
  308.3 4.2 multiply_subtract_fusion.1
  312.6 16.7 %multiply_convert_fusion.1 = (bf16[1024,2048]{1,0:T(8,128)(2,1)S(1)}, f32[1024,2048]{1,0:T(8,128)}) fusion(f32[2048]{0:T(1024)S(1)} %copy-done.19, bf16[1024,2048]{1,0:T(8,128)(2,1)} %get-tuple-element.33, bf16[2,2048,2048]{2,1,0:T(8,128)(2,1)} %all-gather.5.cloned.1.call-done), kind=kOutput, calls=%fused_computation.19 | convolution fusion | flops 8610906112 | bytes 25174016 | tf_op jit(solution)/shard_map/dot_general | solution.py:1165
  329.2 11.2 %fusion.10 = f32[1024,2048]{1,0:T(8,128)} fusion(bf16[1024,2048]{1,0:T(8,128)(2,1)S(1)} %get-tuple-element.90, bf16[2,2048,2048]{2,1,0:T(8,128)(2,1)S(1)} %copy-done.26), kind=kOutput, calls=%fused_computation.23 | convolution fusion | flops 8589934592 | bytes 20971520 | tf_op jit(solution)/shard_map/dot_general | solution.py:1165
  340.4 8.4 %add_convert_fusion.2 = bf16[1024,2048]{1,0:T(8,128)(2,1)} fusion(f32[1024,2048]{1,0:T(8,128)} %fusion.10, bf16[1024,512]{1,0:T(8,128)(2,1)S(1)} %copy-done.34, bf16[2048,2048]{1,0:T(8,128)(2,1)} %all-gather.3.cloned.1.call-done), kind=kOutput, calls=%fused_computation.18 | convolution fusion | flops 2151677952 | bytes 15728640 | tf_op jit(solution)/shard_map/dot_general | solution.py:1165
  349.1 9.6 %convolution_convert_fusion.1 = bf16[1024,2048]{1,0:T(8,128)(2,1)} fusion(bf16[1024,2048]{1,0:T(8,128)(2,1)} %copy-done.35, bf16[2,1024,1024]{2,1,0:T(8,128)(2,1)} %get-tuple-element.43), kind=kOutput, calls=%fused_computation.39 | convolution fusion | flops 4297064448 | bytes 10485760 | tf_op jit(solution)/shard_map/dot_general | solution.py:1165
  358.7 17.5 %convert_reduce_fusion = (f32[2048]{0:T(1024)S(1)}, bf16[1024,2048]{1,0:T(8,128)(2,1)S(1)}) fusion(f32[1024,2048]{1,0:T(8,128)} %get-tuple-element.91, f32[2048]{0:T(1024)S(1)} %copy-done.19, bf16[1024,2048]{1,0:T(8,128)(2,1)S(1)} %copy-done.8, bf16[2,2048,2048]{2,1,0:T(8,128)(2,1)} %all-gather.5.cloned.1.call-done), kind=kOutput, calls=%fused_computation.11 | convolution fusion | flops 8638167040 | bytes 25182208 | tf_op jit(solution)/shard_map/dot_general | solution.py:1165
  376.2 6.3 %convolution_convert_fusion.2 = bf16[1024,2048]{1,0:T(8,128)(2,1)} fusion(bf16[1024,2048]{1,0:T(8,128)(2,1)S(1)} %get-tuple-element.94, bf16[2,1024,1024]{2,1,0:T(8,128)(2,1)S(1)} %copy-done.29), kind=kOutput, calls=%fused_computation.40 | convolution fusion | flops 4297064448 | bytes 10485760 | tf_op jit(solution)/shard_map/dot_general | solution.py:1165
  383.1 17.2 %multiply_reduce_fusion = (f32[2048]{0:T(1024)S(1)}, f32[1024]{0:T(1024)S(1)}, f32[1024]{0:T(1024)S(1)}, f32[2048]{0:T(1024)S(1)}, f32[1024,2048]{1,0:T(8,128)S(1)}) fusion(bf16[1024,2048]{1,0:T(8,128)(2,1)} %get-tuple-element.32, f32[1024]{0:T(1024)S(1)} %copy-done.14, f32[1024]{0:T(1024)S(1)} %copy-done.15, f32[2048]{0:T(1024)S(1)} %bitcast.236, ...), kind=kOutput, calls=%fused_computation.12 | convolution fusion | flops 8612997120 | bytes 33595392 | tf_op jit(solution)/shard_map/dot_general | solution.py:1165
  400.4 5.6 %multiply_convert_fusion = bf16[1024,2048]{1,0:T(8,128)(2,1)} fusion(bf16[1024,2048]{1,0:T(8,128)(2,1)} %get-tuple-element.32, f32[1024,2048]{1,0:T(8,128)S(1)} %get-tuple-element.92, f32[1024]{0:T(1024)S(1)} %broadcast_multiply_fusion, f32[1024]{0:T(1024)S(1)} %copy-done.14, f32[1024]{0:T(1024)S(1)} %broadcast_multiply_fusion.1, f32[2048]{0:T(1024)S(1)} %bitcast.237, ...), kind=kLoop, calls=%fused_computation.15 | loop fusion | flops 18874368 | bytes 16801792 | tf_op jit(solution)/shard_map/convert_element_type | solution.py:1288
  407.3 10.8 %shard_map.289 = f32[10,512]{1,0:T(8,128)} custom-call(f32[4,2,512]{2,1,0:T(2,128)} %maximum_bitcast_fusion.3.stats_ref, f32[8,512]{1,0:T(8,128)} %pad_maximum_fusion.4.rest_ref), custom_call_target="tpu_custom_call" | custom-call | tf_op jit(solution)/shard_map/pallas_call | solution.py:1032
  418.9 8.6 %add_convert_fusion = bf16[1024,2048]{1,0:T(8,128)(2,1)S(1)} fusion(bf16[1024,2048]{1,0:T(8,128)(2,1)} %collective-permute-done.18, bf16[1024,2048]{1,0:T(8,128)(2,1)} %copy-done.35, bf16[2,1024,1024]{2,1,0:T(8,128)(2,1)} %get-tuple-element.43), kind=kOutput, calls=%fused_computation.13 | convolution fusion | flops 4301258752 | bytes 14680064 | tf_op jit(solution)/shard_map/dot_general | solution.py:1165
  431.2 6.9 %add_convert_fusion.1 = bf16[1024,2048]{1,0:T(8,128)(2,1)S(1)} fusion(bf16[1024,2048]{1,0:T(8,128)(2,1)} %collective-permute-done.13, bf16[1024,2048]{1,0:T(8,128)(2,1)S(1)} %copy-done.37, bf16[2,1024,1024]{2,1,0:T(8,128)(2,1)S(1)} %copy-done.30), kind=kOutput, calls=%fused_computation.14 | convolution fusion | flops 4301258752 | bytes 14680064 | tf_op jit(solution)/shard_map/dot_general | solution.py:1165
  442.1 12.3 %collective-permute-done.21 = bf16[2,256,1024]{2,1,0:T(8,128)(2,1)S(1)} collective-permute-done((bf16[2,256,1024]{2,1,0:T(8,128)(2,1)S(1)}, bf16[2,256,1024]{2,1,0:T(8,128)(2,1)S(1)}, u32[]{:S(2)}, u32[]{:S(2)}) %collective-permute-start.21) | collective-permute-done | bytes 1048608 | tf_op jit(solution)/shard_map/ppermute | solution.py:1124
  458.1 18.7 %collective-permute-done.16 = bf16[2,256,1024]{2,1,0:T(8,128)(2,1)S(1)} collective-permute-done((bf16[2,256,1024]{2,1,0:T(8,128)(2,1)S(1)}, bf16[2,256,1024]{2,1,0:T(8,128)(2,1)S(1)}, u32[]{:S(2)}, u32[]{:S(2)}) %collective-permute-start.16) | collective-permute-done | bytes 1048608 | tf_op jit(solution)/shard_map/ppermute | solution.py:1124
  479.9 9.2 %collective-permute-done.22 = bf16[256,1024]{1,0:T(8,128)(2,1)S(1)} collective-permute-done((bf16[256,1024]{1,0:T(8,128)(2,1)S(1)}, bf16[256,1024]{1,0:T(8,128)(2,1)S(1)}, u32[]{:S(2)}, u32[]{:S(2)}) %collective-permute-start.22) | collective-permute-done | bytes 524320 | tf_op jit(solution)/shard_map/ppermute | solution.py:1124
  489.7 10.2 %collective-permute-done.17 = bf16[256,1024]{1,0:T(8,128)(2,1)S(1)} collective-permute-done((bf16[256,1024]{1,0:T(8,128)(2,1)S(1)}, bf16[256,1024]{1,0:T(8,128)(2,1)S(1)}, u32[]{:S(2)}, u32[]{:S(2)}) %collective-permute-start.17) | collective-permute-done | bytes 524320 | tf_op jit(solution)/shard_map/ppermute | solution.py:1124
  502.1 2.1 add_convert_fusion.5
  505.7 10.0 %multiply_subtract_fusion = (f32[2,256,2048]{2,1,0:T(8,128)}, f32[2,256,2048]{2,1,0:T(8,128)}, f32[2,256,2048]{2,1,0:T(8,128)}, f32[2,256,2048]{2,1,0:T(8,128)}) fusion(f32[2,256,2048]{2,1,0:T(8,128)S(1)} %copy-done, f32[2,256,2048]{2,1,0:T(8,128)} %param.23, f32[2,256,2048]{2,1,0:T(8,128)} %param.27, f32[1,256,2048]{2,1,0:T(8,128)S(1)} %maximum_bitcast_fusion.1, ...), kind=kLoop, calls=%fused_computation.36 | loop fusion | flops 16777216 | bytes 33554432 | tf_op jit(solution)/shard_map/sub | solution.py:224
  516.3 20.3 %shard_map.288 = bf16[4,256,512]{2,1,0:T(8,128)(2,1)} custom-call(bf16[1024,512]{1,0:T(8,128)(2,1)} %reduce-scatter.5.cloned.1.call-done.sum_ref, bf16[1024,512]{1,0:T(8,128)(2,1)} %get-tuple-element.66.base_ref), custom_call_target="tpu_custom_call" | custom-call | tf_op jit(solution)/shard_map/pallas_call | solution.py:1108
  536.8 2.6 copy.43
  (209 shorter events, 59.7 us)
Async XLA Ops:
  7.2 169.1 %all-gather.3.cloned.1.call-start = ((), (), s32[]{:S(2)}) async-start(), calls=%async_computation.2 | async-start | bytes 9437184 | tf_op jit(solution)/shard_map/all_gather | solution.py:1168
  10.2 302.4 %all-gather.5.cloned.1.call-start = ((), (), s32[]{:S(2)}) async-start(), calls=%async_computation.3 | async-start | bytes 18874368 | tf_op jit(solution)/shard_map/all_gather | solution.py:1169
  14.1 488.0 %reduce-scatter.3.cloned.1.call-start = ((), (), s32[]{:S(2)}) async-start(), calls=%async_computation.4 | async-start | bytes 5242880 | tf_op jit(solution)/shard_map/reduce_scatter | solution.py:1215
  250.8 14.3 %collective-permute-start.3 = (bf16[1024,1536]{1,0:T(8,128)(2,1)S(1)}, bf16[1024,1536]{1,0:T(8,128)(2,1)S(1)}, u32[]{:S(2)}, u32[]{:S(2)}) collective-permute-start(bf16[1024,1536]{1,0:T(8,128)(2,1)S(1)} %convolution_convert_fusion), channel_id=1, source_target_pairs={{0,4},{4,0},{8,12},{12,8},{1,5},{5,1},{9,13},{13,9},{2,6},{6,2},{1... | collective-permute-start | bytes 9437192 | tf_op jit(solution)/shard_map/ppermute | solution.py:1124
  252.2 9.8 %collective-permute-start.8 = (bf16[1024,512]{1,0:T(8,128)(2,1)S(1)}, bf16[1024,512]{1,0:T(8,128)(2,1)S(1)}, u32[]{:S(2)}, u32[]{:S(2)}) collective-permute-start(bf16[1024,512]{1,0:T(8,128)(2,1)S(1)} %fusion.51), channel_id=1, source_target_pairs={{0,4},{4,0},{8,12},{12,8},{1,5},{5,1},{9,13},{13,9},{2,6},{6,2},{1... | collective-permute-start | bytes 3145736 | tf_op jit(solution)/shard_map/ppermute | solution.py:1124
  263.4 10.1 %collective-permute-start.11 = (bf16[2,256,256]{2,1,0:T(8,128)(2,1)S(1)}, bf16[2,256,256]{2,1,0:T(8,128)(2,1)S(1)}, u32[]{:S(2)}, u32[]{:S(2)}) collective-permute-start(bf16[2,256,256]{2,1,0:T(8,128)(2,1)S(1)} %dynamic-slice_bitcast_fusion.6), channel_id=1, source_target_pairs={{0,16},{16,0},{1,17},{17,1},{2,18},{18,2},{3,19},{19,3},{4,20},{20... | collective-permute-start | bytes 786440 | tf_op jit(solution)/shard_map/ppermute | solution.py:1124
  263.5 12.8 %collective-permute-start.9 = (bf16[2,256,256]{2,1,0:T(8,128)(2,1)S(1)}, bf16[2,256,256]{2,1,0:T(8,128)(2,1)}, u32[]{:S(2)}, u32[]{:S(2)}) collective-permute-start(bf16[2,256,256]{2,1,0:T(8,128)(2,1)S(1)} %dynamic-slice_bitcast_fusion.7), channel_id=1, source_target_pairs={{0,8},{4,12},{8,0},{12,4},{1,9},{5,13},{9,1},{13,5},{2,10},{6,14},... | collective-permute-start | bytes 786440 | tf_op jit(solution)/shard_map/ppermute | solution.py:1124
  270.1 23.4 %collective-permute-start.4 = (bf16[2,256,768]{2,1,0:T(8,128)(2,1)}, bf16[2,256,768]{2,1,0:T(8,128)(2,1)}, u32[]{:S(2)}, u32[]{:S(2)}) collective-permute-start(bf16[2,256,768]{2,1,0:T(8,128)(2,1)} %dynamic-slice_bitcast_fusion.5), channel_id=1, source_target_pairs={{0,8},{4,12},{8,0},{12,4},{1,9},{5,13},{9,1},{13,5},{2,10},{6,14},... | collective-permute-start | bytes 2359304 | tf_op jit(solution)/shard_map/ppermute | solution.py:1124
  271.6 24.8 %collective-permute-start.6 = (bf16[2,256,768]{2,1,0:T(8,128)(2,1)}, bf16[2,256,768]{2,1,0:T(8,128)(2,1)}, u32[]{:S(2)}, u32[]{:S(2)}) collective-permute-start(bf16[2,256,768]{2,1,0:T(8,128)(2,1)} %dynamic-slice_bitcast_fusion.4), channel_id=1, source_target_pairs={{0,16},{16,0},{1,17},{17,1},{2,18},{18,2},{3,19},{19,3},{4,20},{20... | collective-permute-start | bytes 2359304 | tf_op jit(solution)/shard_map/ppermute | solution.py:1124
  274.2 18.3 %collective-permute-start.12 = (bf16[256,256]{1,0:T(8,128)(2,1)S(1)}, bf16[256,256]{1,0:T(8,128)(2,1)}, u32[]{:S(2)}, u32[]{:S(2)}) collective-permute-start(bf16[256,256]{1,0:T(8,128)(2,1)S(1)} %fusion.76), channel_id=1, source_target_pairs={{0,8},{4,12},{8,0},{12,4},{1,9},{5,13},{9,1},{13,5},{2,10},{6,14},... | collective-permute-start | bytes 393224 | tf_op jit(solution)/shard_map/ppermute | solution.py:1124
  277.3 21.0 %collective-permute-start.10 = (bf16[256,256]{1,0:T(8,128)(2,1)S(1)}, bf16[256,256]{1,0:T(8,128)(2,1)S(1)}, u32[]{:S(2)}, u32[]{:S(2)}) collective-permute-start(bf16[256,256]{1,0:T(8,128)(2,1)S(1)} %fusion.78), channel_id=1, source_target_pairs={{0,16},{16,0},{1,17},{17,1},{2,18},{18,2},{3,19},{19,3},{4,20},{20... | collective-permute-start | bytes 393224 | tf_op jit(solution)/shard_map/ppermute | solution.py:1124
  294.6 10.0 %collective-permute-start.5 = (bf16[256,768]{1,0:T(8,128)(2,1)S(1)}, bf16[256,768]{1,0:T(8,128)(2,1)S(1)}, u32[]{:S(2)}, u32[]{:S(2)}) collective-permute-start(bf16[256,768]{1,0:T(8,128)(2,1)S(1)} %fusion.69), channel_id=1, source_target_pairs={{0,16},{16,0},{1,17},{17,1},{2,18},{18,2},{3,19},{19,3},{4,20},{20... | collective-permute-start | bytes 1179656 | tf_op jit(solution)/shard_map/ppermute | solution.py:1124
  297.5 9.4 %collective-permute-start.7 = (bf16[256,768]{1,0:T(8,128)(2,1)S(1)}, bf16[256,768]{1,0:T(8,128)(2,1)S(1)}, u32[]{:S(2)}, u32[]{:S(2)}) collective-permute-start(bf16[256,768]{1,0:T(8,128)(2,1)S(1)} %fusion.67), channel_id=1, source_target_pairs={{0,8},{4,12},{8,0},{12,4},{1,9},{5,13},{9,1},{13,5},{2,10},{6,14},... | collective-permute-start | bytes 1179656 | tf_op jit(solution)/shard_map/ppermute | solution.py:1124
  312.5 16.7 %copy-start.26 = (bf16[2,2048,2048]{2,1,0:T(8,128)(2,1)S(1)}, bf16[2,2048,2048]{2,1,0:T(8,128)(2,1)}, u32[]{:S(2)}) copy-start(bf16[2,2048,2048]{2,1,0:T(8,128)(2,1)} %all-gather.5.cloned.1.call-done) | copy-start | bytes 50331652
  348.9 167.4 %reduce-scatter.5.cloned.1.call-start = ((), (), s32[]{:S(2)}) async-start(), calls=%async_computation.5 | async-start | bytes 5242880 | tf_op jit(solution)/shard_map/reduce_scatter | solution.py:1215
  358.7 60.2 %collective-permute-start.18 = (bf16[1024,2048]{1,0:T(8,128)(2,1)}, bf16[1024,2048]{1,0:T(8,128)(2,1)}, u32[]{:S(2)}, u32[]{:S(2)}) collective-permute-start(bf16[1024,2048]{1,0:T(8,128)(2,1)} %convolution_convert_fusion.1), channel_id=1, source_target_pairs={{0,4},{4,0},{8,12},{12,8},{1,5},{5,1},{9,13},{13,9},{2,6},{6,2},{1... | collective-permute-start | bytes 12582920 | tf_op jit(solution)/shard_map/ppermute | solution.py:1124
  358.7 17.5 %copy-start.29 = (bf16[2,1024,1024]{2,1,0:T(8,128)(2,1)S(1)}, bf16[2,1024,1024]{2,1,0:T(8,128)(2,1)}, u32[]{:S(2)}) copy-start(bf16[2,1024,1024]{2,1,0:T(8,128)(2,1)} %get-tuple-element.42) | copy-start | bytes 12582916
  382.6 48.5 %collective-permute-start.13 = (bf16[1024,2048]{1,0:T(8,128)(2,1)}, bf16[1024,2048]{1,0:T(8,128)(2,1)}, u32[]{:S(2)}, u32[]{:S(2)}) collective-permute-start(bf16[1024,2048]{1,0:T(8,128)(2,1)} %convolution_convert_fusion.2), channel_id=1, source_target_pairs={{0,4},{4,0},{8,12},{12,8},{1,5},{5,1},{9,13},{13,9},{2,6},{6,2},{1... | collective-permute-start | bytes 12582920 | tf_op jit(solution)/shard_map/ppermute | solution.py:1124
  428.3 26.1 %collective-permute-start.21 = (bf16[2,256,1024]{2,1,0:T(8,128)(2,1)S(1)}, bf16[2,256,1024]{2,1,0:T(8,128)(2,1)S(1)}, u32[]{:S(2)}, u32[]{:S(2)}) collective-permute-start(bf16[2,256,1024]{2,1,0:T(8,128)(2,1)S(1)} %dynamic-slice_bitcast_fusion), channel_id=1, source_target_pairs={{0,16},{16,0},{1,17},{17,1},{2,18},{18,2},{3,19},{19,3},{4,20},{20... | collective-permute-start | bytes 3145736 | tf_op jit(solution)/shard_map/ppermute | solution.py:1124
  429.3 26.4 %collective-permute-start.19 = (bf16[2,256,1024]{2,1,0:T(8,128)(2,1)S(1)}, bf16[2,256,1024]{2,1,0:T(8,128)(2,1)S(1)}, u32[]{:S(2)}, u32[]{:S(2)}) collective-permute-start(bf16[2,256,1024]{2,1,0:T(8,128)(2,1)S(1)} %dynamic-slice_bitcast_fusion.1), channel_id=1, source_target_pairs={{0,8},{4,12},{8,0},{12,4},{1,9},{5,13},{9,1},{13,5},{2,10},{6,14},... | collective-permute-start | bytes 3145736 | tf_op jit(solution)/shard_map/ppermute | solution.py:1124
  438.5 18.9 %copy-start.20 = (f32[2048]{0:T(1024)S(1)}, f32[2048]{0:T(1024)}, u32[]{:S(2)}) copy-start(f32[2048]{0:T(1024)} %param.25) | copy-start | bytes 24580
  438.6 18.9 %copy-start.21 = (f32[2048]{0:T(1024)S(1)}, f32[2048]{0:T(1024)}, u32[]{:S(2)}) copy-start(f32[2048]{0:T(1024)} %param.29) | copy-start | bytes 24580
  438.7 38.2 %collective-permute-start.16 = (bf16[2,256,1024]{2,1,0:T(8,128)(2,1)S(1)}, bf16[2,256,1024]{2,1,0:T(8,128)(2,1)S(1)}, u32[]{:S(2)}, u32[]{:S(2)}) collective-permute-start(bf16[2,256,1024]{2,1,0:T(8,128)(2,1)S(1)} %dynamic-slice_bitcast_fusion.2), channel_id=1, source_target_pairs={{0,16},{16,0},{1,17},{17,1},{2,18},{18,2},{3,19},{19,3},{4,20},{20... | collective-permute-start | bytes 3145736 | tf_op jit(solution)/shard_map/ppermute | solution.py:1124
  439.6 38.6 %collective-permute-start.14 = (bf16[2,256,1024]{2,1,0:T(8,128)(2,1)S(1)}, bf16[2,256,1024]{2,1,0:T(8,128)(2,1)S(1)}, u32[]{:S(2)}, u32[]{:S(2)}) collective-permute-start(bf16[2,256,1024]{2,1,0:T(8,128)(2,1)S(1)} %dynamic-slice_bitcast_fusion.3), channel_id=1, source_target_pairs={{0,8},{4,12},{8,0},{12,4},{1,9},{5,13},{9,1},{13,5},{2,10},{6,14},... | collective-permute-start | bytes 3145736 | tf_op jit(solution)/shard_map/ppermute | solution.py:1124
  441.4 48.0 %copy-start.13 = (f32[1,4,4,128]{3,1,2,0:T(4,128)}, f32[1,4,4,128]{3,1,2,0:T(4,128)S(1)}, u32[]{:S(2)}) copy-start(f32[1,4,4,128]{3,1,2,0:T(4,128)S(1)} %copy.35) | copy-start | bytes 24580
  454.6 34.6 %collective-permute-start.22 = (bf16[256,1024]{1,0:T(8,128)(2,1)S(1)}, bf16[256,1024]{1,0:T(8,128)(2,1)S(1)}, u32[]{:S(2)}, u32[]{:S(2)}) collective-permute-start(bf16[256,1024]{1,0:T(8,128)(2,1)S(1)} %fusion.59), channel_id=1, source_target_pairs={{0,8},{4,12},{8,0},{12,4},{1,9},{5,13},{9,1},{13,5},{2,10},{6,14},... | collective-permute-start | bytes 1572872 | tf_op jit(solution)/shard_map/ppermute | solution.py:1124
  455.9 33.5 %collective-permute-start.20 = (bf16[256,1024]{1,0:T(8,128)(2,1)S(1)}, bf16[256,1024]{1,0:T(8,128)(2,1)S(1)}, u32[]{:S(2)}, u32[]{:S(2)}) collective-permute-start(bf16[256,1024]{1,0:T(8,128)(2,1)S(1)} %fusion.61), channel_id=1, source_target_pairs={{0,16},{16,0},{1,17},{17,1},{2,18},{18,2},{3,19},{19,3},{4,20},{20... | collective-permute-start | bytes 1572872 | tf_op jit(solution)/shard_map/ppermute | solution.py:1124
  477.0 22.8 %collective-permute-start.17 = (bf16[256,1024]{1,0:T(8,128)(2,1)S(1)}, bf16[256,1024]{1,0:T(8,128)(2,1)S(1)}, u32[]{:S(2)}, u32[]{:S(2)}) collective-permute-start(bf16[256,1024]{1,0:T(8,128)(2,1)S(1)} %fusion.63), channel_id=1, source_target_pairs={{0,8},{4,12},{8,0},{12,4},{1,9},{5,13},{9,1},{13,5},{2,10},{6,14},... | collective-permute-start | bytes 1572872 | tf_op jit(solution)/shard_map/ppermute | solution.py:1124
  478.4 21.7 %collective-permute-start.15 = (bf16[256,1024]{1,0:T(8,128)(2,1)S(1)}, bf16[256,1024]{1,0:T(8,128)(2,1)S(1)}, u32[]{:S(2)}, u32[]{:S(2)}) collective-permute-start(bf16[256,1024]{1,0:T(8,128)(2,1)S(1)} %fusion.65), channel_id=1, source_target_pairs={{0,16},{16,0},{1,17},{17,1},{2,18},{18,2},{3,19},{19,3},{4,20},{20... | collective-permute-start | bytes 1572872 | tf_op jit(solution)/shard_map/ppermute | solution.py:1124
  504.3 32.4 %collective-permute-start = (bf16[1,256,512]{2,1,0:T(8,128)(2,1)S(1)}, bf16[1,256,512]{2,1,0:T(8,128)(2,1)S(1)}, u32[]{:S(2)}, u32[]{:S(2)}) collective-permute-start(bf16[1,256,512]{2,1,0:T(8,128)(2,1)S(1)} %get-tuple-element.77), channel_id=1, source_target_pairs={{0,4},{4,0},{8,12},{12,8},{1,5},{5,1},{9,13},{13,9},{2,6},{6,2},{1... | collective-permute-start | bytes 786440 | tf_op jit(solution)/shard_map/ppermute | solution.py:1124
  504.3 32.4 %collective-permute-start.1 = (bf16[1,256,512]{2,1,0:T(8,128)(2,1)S(1)}, bf16[1,256,512]{2,1,0:T(8,128)(2,1)S(1)}, u32[]{:S(2)}, u32[]{:S(2)}) collective-permute-start(bf16[1,256,512]{2,1,0:T(8,128)(2,1)S(1)} %get-tuple-element.76), channel_id=1, source_target_pairs={{0,8},{4,12},{8,0},{12,4},{1,9},{5,13},{9,1},{13,5},{2,10},{6,14},... | collective-permute-start | bytes 786440 | tf_op jit(solution)/shard_map/ppermute | solution.py:1124
  515.7 21.0 %collective-permute-start.2 = (bf16[1,256,512]{2,1,0:T(8,128)(2,1)S(1)}, bf16[1,256,512]{2,1,0:T(8,128)(2,1)S(1)}, u32[]{:S(2)}, u32[]{:S(2)}) collective-permute-start(bf16[1,256,512]{2,1,0:T(8,128)(2,1)S(1)} %get-tuple-element.75), channel_id=1, source_target_pairs={{0,12},{4,8},{8,4},{12,0},{1,13},{5,9},{9,5},{13,1},{2,14},{6,10},... | collective-permute-start | bytes 786440 | tf_op jit(solution)/shard_map/ppermute | solution.py:1124
  (36 other events, 181.0 us)
Sparse Core Ops, SparseCore 0:
  10.5 70.9 all-gather.2
  83.9 89.4 all-gather.4
  349.0 75.2 reduce-scatter.2
  426.5 77.2 reduce-scatter.4
